TPU v7x, 32 devices: a whole 2x2x4 slice. The times are simulated.
32 devices in a mesh: gz: 2 (over y), row: 4 (over z), col: 4 (over x, core).
Axes of the slice: x: 2, y: 2, z: 4, core: 2. Of those that a mesh axis runs over, the one named last changes fastest.
Arguments:
- lpanel: bfloat16 [2, 2, 1024, 2048], P(None, 'gz', 'row', 'col'), may hold values from -6 to 6
- upanel: bfloat16 [2, 2, 2048, 4096], P(None, 'gz', 'row', 'col'), may hold values from -0.125 to 0.125
- rowmap: int32 [2, 2, 4], P(None, 'gz', 'row'), may hold values from 0 to 1
- colmap: int32 [2, 2, 16], P(None, 'gz', 'col'), may hold values from 0 to 1
- blockmask: int32 [2, 2, 4, 16], P(None, 'gz', 'row', 'col'), may hold values 0 or 1
- front_blocks: bfloat16 [2, 2048, 2048], P(None, 'row', ('gz', 'col')), may hold values from -6 to 6
Outputs:
- front_update: bfloat16 [2, 2048, 2048], P(None, 'row', ('gz', 'col'))
All inputs are finite; a program needn't handle non-finite values. No bound on the sum of `blockmask` on one device may be relied on, other than what follows from the above.
Results may differ from a plain program's by a relative error of at most 0.008.
Values may be sent and summed in bfloat16 or wider, within the bound.
No kernel may reach another device: no remote copies, remote signals or barrier semaphores. Data moves between devices by JAX's collectives and lax.ppermute only.
A program may use at most 64 MiB of HBM per device.

v0:
```python
import jax
import jax.numpy as jnp
from jax import lax
from jax.sharding import PartitionSpec as P

CB = 4
FRB = 2
LEVELS = 2


def column_sums(schur, cols_of, live, layers):
    width = schur.shape[0]
    blocks = schur.reshape(width, CB, width)
    targets = cols_of[:, None] == jnp.arange(layers, dtype=jnp.int32)[None, :]
    col_select = targets.astype(jnp.float32) * live.astype(jnp.float32)[:, None]
    return jnp.einsum("bjk,jl->lbk", blocks, col_select, precision=lax.Precision.HIGHEST)


def on_device(lpanel, upanel, rowmap, colmap, blockmask, front_blocks):
    layers = lax.axis_size("gz")
    width = lpanel.shape[2]
    tiles = []
    for depth in range(LEVELS):
        left_rows = lax.all_gather(lpanel[depth, 0], "col", axis=1, tiled=True)
        tiles.append(
            jnp.dot(
                left_rows,
                lax.all_gather(upanel[depth, 0], "row", axis=0, tiled=True),
                preferred_element_type=jnp.float32,
            )
        )
    results = []
    every_row = lax.all_gather(rowmap[:, :, 0], "gz", axis=1, tiled=True)
    for depth in range(LEVELS):
        sums = column_sums(tiles[depth], colmap[depth, 0], blockmask[depth, 0, 0], layers).astype(
            jnp.bfloat16
        )
        arrived = lax.all_to_all(sums, "gz", split_axis=0, concat_axis=0, tiled=True)
        row_select = (
            every_row[depth][:, None] == jnp.arange(FRB, dtype=jnp.int32)[None, :]
        ).astype(jnp.float32)
        placed = jnp.einsum(
            "sf,sbk->fbk", row_select, arrived.astype(jnp.float32), precision=lax.Precision.HIGHEST
        )
        placed = placed.reshape(FRB * width, width)
        results.append((front_blocks[depth].astype(jnp.float32) - placed).astype(jnp.bfloat16))
    return jnp.stack(results)


def solution(mesh):
    return jax.shard_map(
        on_device,
        mesh=mesh,
        in_specs=(
            P(None, "gz", "row", "col"),
            P(None, "gz", "row", "col"),
            P(None, "gz", "row"),
            P(None, "gz", "col"),
            P(None, "gz", "row", "col"),
            P(None, "row", ("gz", "col")),
        ),
        out_specs=P(None, "row", ("gz", "col")),
        check_vma=False,
    )
```

profile of v0, /device:TPU:0, one launch (start us, length us, event | category | flops | bytes accessed | tf_op | source)
XLA Modules:
  0.0 233.3 jit_solution(8685987046296502088)
XLA Ops:
  6.5 1.9 fusion.31
  8.5 0.0 all-gather.14.cloned.1.call-update
  8.5 0.0 all-gather.16.cloned.1.call-start
  8.5 3.0 %fusion.30 = (bf16[1,1,512,1024]{3,2,1,0:T(8,128)(2,1)}, bf16[1,1,512,1024]{3,2,1,0:T(8,128)(2,1)}) fusion(bf16[2,1,512,1024]{3,2,1,0:T(8,128)(2,1)} %param.7), kind=kLoop, calls=%fused_computation.43 | loop fusion | bytes 4194304 | tf_op jit(solution)/shard_map/slice | solution.py:28
  11.6 0.0 all-gather.16.cloned.1.call-update
  11.6 0.0 all-gather.10.cloned.1.call-start
  11.7 0.7 all-gather.10.cloned.1.call-update
  12.3 0.0 all-gather.12.cloned.1.call-start
  12.4 0.5 all-gather.12.cloned.1.call-update
  12.9 5.2 %all-gather = s32[2,2,1]{0,2,1:T(1,128)S(1)} all-gather(s32[2,1,1]{0,2,1:T(1,128)S(1)} %copy-done.4), channel_id=2, replica_groups=mesh['gz'=2,'row'=4,'col'=4] {'gz'}, dimensions={1}, use_global_device_ids=true | all-gather | bytes 24 | tf_op jit(solution)/shard_map/all_gather | solution.py:33
  18.1 0.2 slice_reduce_fusion.1
  18.4 10.0 %all-gather.14.cloned.1.call-done = bf16[1,1,256,2048]{3,2,1,0:T(8,128)(2,1)} async-done(((bf16[1,1,256,512]{3,2,1,0:T(8,128)(2,1)}), bf16[1,1,256,2048]{3,2,1,0:T(8,128)(2,1)}) %all-gather.14.cloned.1.call-update) | async-done | bytes 1048592 | tf_op jit(solution)/shard_map/all_gather | solution.py:24
  28.4 82.3 %all-gather.16.cloned.1.call-done = bf16[1,1,2048,1024]{3,2,1,0:T(8,128)(2,1)} async-done(((bf16[1,1,512,1024]{3,2,1,0:T(8,128)(2,1)}), bf16[1,1,2048,1024]{3,2,1,0:T(8,128)(2,1)}) %all-gather.16.cloned.1.call-update) | async-done | bytes 4194320 | tf_op jit(solution)/shard_map/all_gather | solution.py:28
  110.7 3.8 %fusion = f32[256,1024]{1,0:T(8,128)S(1)} fusion(bf16[1,1,2048,1024]{3,2,1,0:T(8,128)(2,1)} %all-gather.16.cloned.1.call-done, bf16[1,1,256,2048]{3,2,1,0:T(8,128)(2,1)} %all-gather.14.cloned.1.call-done), kind=kOutput, calls=%fused_computation | convolution fusion | flops 1073741824 | bytes 6291456 | tf_op jit(solution)/shard_map/dot_general | solution.py:26
  114.5 0.5 reshape.32
  115.0 1.9 convolution_convert_fusion
  116.8 0.8 copy.12
  117.6 3.4 %all-to-all-start.1 = ((bf16[2,256,256]{2,1,0:T(8,128)(2,1)}), bf16[2,256,256]{2,1,0:T(8,128)(2,1)S(1)}, u32[]{:S(2)}, u32[]{:S(2)}) async-start(bf16[2,256,256]{2,1,0:T(8,128)(2,1)} %copy.12), calls=%async_computation.1 | async-start | bytes 524288 | tf_op jit(solution)/shard_map/all_to_all | solution.py:38
  121.0 6.4 %all-gather.10.cloned.1.call-done = bf16[1,1,256,2048]{3,2,1,0:T(8,128)(2,1)} async-done(((bf16[1,1,256,512]{3,2,1,0:T(8,128)(2,1)}), bf16[1,1,256,2048]{3,2,1,0:T(8,128)(2,1)}) %all-gather.10.cloned.1.call-update) | async-done | bytes 1048592 | tf_op jit(solution)/shard_map/all_gather | solution.py:24
  127.5 82.2 %all-gather.12.cloned.1.call-done = bf16[1,1,2048,1024]{3,2,1,0:T(8,128)(2,1)} async-done(((bf16[1,1,512,1024]{3,2,1,0:T(8,128)(2,1)}), bf16[1,1,2048,1024]{3,2,1,0:T(8,128)(2,1)}) %all-gather.12.cloned.1.call-update) | async-done | bytes 4194320 | tf_op jit(solution)/shard_map/all_gather | solution.py:28
  209.7 3.8 %fusion.2 = f32[256,1024]{1,0:T(8,128)S(1)} fusion(bf16[1,1,2048,1024]{3,2,1,0:T(8,128)(2,1)} %all-gather.12.cloned.1.call-done, bf16[1,1,256,2048]{3,2,1,0:T(8,128)(2,1)} %all-gather.10.cloned.1.call-done), kind=kOutput, calls=%fused_computation.2 | convolution fusion | flops 1073741824 | bytes 6291456 | tf_op jit(solution)/shard_map/dot_general | solution.py:26
  213.4 0.0 copy-start
  213.5 0.5 reshape.30
  214.0 1.9 convolution_convert_fusion.1
  215.8 0.7 copy.9
  216.6 3.4 %all-to-all-start = ((bf16[2,256,256]{2,1,0:T(8,128)(2,1)}), bf16[2,256,256]{2,1,0:T(8,128)(2,1)S(1)}, u32[]{:S(2)}, u32[]{:S(2)}) async-start(bf16[2,256,256]{2,1,0:T(8,128)(2,1)} %copy.9), calls=%async_computation | async-start | bytes 524288 | tf_op jit(solution)/shard_map/all_to_all | solution.py:38
  220.0 0.4 fusion.8
  220.5 4.8 %all-to-all-done = bf16[2,256,256]{2,1,0:T(8,128)(2,1)S(1)} async-done(((bf16[2,256,256]{2,1,0:T(8,128)(2,1)}), bf16[2,256,256]{2,1,0:T(8,128)(2,1)S(1)}, u32[]{:S(2)}, u32[]{:S(2)}) %all-to-all-start) | async-done | bytes 262176 | tf_op jit(solution)/shard_map/all_to_all | solution.py:38
  225.3 0.4 fusion.10
  225.8 0.2 fusion.7
  225.9 0.0 copy-start.3
  226.0 0.8 copy-done.3
  (14 shorter events, 0.1 us)
Async XLA Ops:
  6.5 6.4 %copy-start.4 = (s32[2,1,1]{0,2,1:T(1,128)S(1)}, s32[2,1,1]{0,2,1:T(1,128)}, u32[]{:S(2)}) copy-start(s32[2,1,1]{0,2,1:T(1,128)} %param.8) | copy-start | bytes 28
  6.5 11.8 %copy-start.1 = (s32[2,1,4]{2,1,0:T(1,128)S(1)}, s32[2,1,4]{2,1,0:T(1,128)}, u32[]{:S(2)}) copy-start(s32[2,1,4]{2,1,0:T(1,128)} %param.9) | copy-start | bytes 100
  6.5 11.8 %copy-start.2 = (s32[2,1,1,4]{3,2,1,0:T(1,128)S(1)}, s32[2,1,1,4]{3,2,1,0:T(1,128)}, u32[]{:S(2)}) copy-start(s32[2,1,1,4]{3,2,1,0:T(1,128)} %param.10) | copy-start | bytes 100
  6.5 21.8 %all-gather.14.cloned.1.call-start = ((), (), s32[]{:S(2)}) async-start(), calls=%async_computation.4 | async-start | bytes 1310720 | tf_op jit(solution)/shard_map/all_gather | solution.py:24
  8.5 102.2 %all-gather.16.cloned.1.call-start = ((), (), s32[]{:S(2)}) async-start(), calls=%async_computation.5 | async-start | bytes 5242880 | tf_op jit(solution)/shard_map/all_gather | solution.py:28
  11.6 115.9 %all-gather.10.cloned.1.call-start = ((), (), s32[]{:S(2)}) async-start(), calls=%async_computation.2 | async-start | bytes 1310720 | tf_op jit(solution)/shard_map/all_gather | solution.py:24
  12.3 197.3 %all-gather.12.cloned.1.call-start = ((), (), s32[]{:S(2)}) async-start(), calls=%async_computation.3 | async-start | bytes 5242880 | tf_op jit(solution)/shard_map/all_gather | solution.py:28
  117.6 99.0 %all-to-all-start.1 = ((bf16[2,256,256]{2,1,0:T(8,128)(2,1)}), bf16[2,256,256]{2,1,0:T(8,128)(2,1)S(1)}, u32[]{:S(2)}, u32[]{:S(2)}) async-start(bf16[2,256,256]{2,1,0:T(8,128)(2,1)} %copy.12), calls=%async_computation.1 | async-start | bytes 524288 | tf_op jit(solution)/shard_map/all_to_all | solution.py:38
  213.4 12.3 %copy-start = (bf16[2,512,256]{2,1,0:T(8,128)(2,1)S(1)}, bf16[2,512,256]{2,1,0:T(8,128)(2,1)}, u32[]{:S(2)}) copy-start(bf16[2,512,256]{2,1,0:T(8,128)(2,1)} %param.11) | copy-start | bytes 1572868
  216.6 8.7 %all-to-all-start = ((bf16[2,256,256]{2,1,0:T(8,128)(2,1)}), bf16[2,256,256]{2,1,0:T(8,128)(2,1)S(1)}, u32[]{:S(2)}, u32[]{:S(2)}) async-start(bf16[2,256,256]{2,1,0:T(8,128)(2,1)} %copy.9), calls=%async_computation | async-start | bytes 524288 | tf_op jit(solution)/shard_map/all_to_all | solution.py:38
  225.9 0.8 copy-start.3
Sparse Core Ops, SparseCore 0:
  8.9 19.4 all-gather.13
  29.9 80.7 all-gather.15
  112.3 15.1 all-gather.9
  128.9 80.7 all-gather.11
where the time goes:
time: 234 us; the launch traced here: 233 us
  waiting for transfers between devices  187 us (80%)
  between operations  13.3 us (6%)
  matrix products  12.1 us (5%)
  local copies, waits for them, and re-layouts  8.54 us (4%)
  starting transfers between devices  7.01 us (3%)
  blocking collectives  5.19 us (2%)
    all_gather x2, waiting for transfers between devices, on_device(): lax.all_gather(upanel[depth, 0], 'row', axis=0, tiled=True)  165 us
    all_gather x2, waiting for transfers between devices, on_device(): left_rows = lax.all_gather(lpanel[depth, 0], 'col', axis=1, tiled=True)  16.4 us
    dot_general x2, matrix products, on_device(): jnp.dot(left_rows, lax.all_gather(upanel[depth, 0], 'row', axis=0, tiled=...  7.52 us
    all_to_all x2, starting transfers between devices, on_device(): lax.all_to_all(sums, 'gz', split_axis=0, concat_axis=0, tiled=True)  6.89 us
    all_gather x1, blocking collectives, on_device(): every_row = lax.all_gather(rowmap[:, :, 0], 'gz', axis=1, tiled=True)  5.19 us
    all_to_all x2, waiting for transfers between devices, on_device(): lax.all_to_all(sums, 'gz', split_axis=0, concat_axis=0, tiled=True)  4.82 us
  transfers between devices with their start and end apart: 6, of which 5 were waited for; matrix products, arithmetic and copies ran while one was open for 7% of the time, Pallas kernels for 0%

commit v1 on v0

v1 whole, which is shorter than its diff:
```python
import jax
import jax.numpy as jnp
from jax import lax
from jax.experimental import pallas as pl
from jax.experimental.pallas import tpu as pltpu
from jax.sharding import PartitionSpec as P


def product_kernel(picks, left, right, out):
    slot = pl.program_id(0)
    layers, width = out.shape[1], out.shape[3]
    count = right.shape[1] // width
    tile = jnp.dot(left[0], right[...], preferred_element_type=jnp.float32)
    for layer in range(layers):
        total = None
        for j in range(count):
            term = picks[(slot * count + j) * layers + layer] * tile[:, j * width : (j + 1) * width]
            total = term if total is None else total + term
        out[0, layer] = total.astype(out.dtype)


def products(picks, left, right, layers):
    slots, rows, depth = left.shape
    columns = right.shape[1]
    width = rows
    return pl.pallas_call(
        product_kernel,
        grid=(slots,),
        in_specs=[
            pl.BlockSpec(memory_space=pltpu.SMEM),
            pl.BlockSpec((1, rows, depth), lambda i: (i, 0, 0)),
            pl.BlockSpec((depth, columns), lambda i: (0, 0)),
        ],
        out_specs=pl.BlockSpec((1, layers, rows, width), lambda i: (i, 0, 0, 0)),
        out_shape=jax.ShapeDtypeStruct((slots, layers, rows, width), jnp.bfloat16),
        cost_estimate=pl.CostEstimate(
            flops=2 * slots * rows * depth * columns,
            bytes_accessed=2 * (left.size + right.size + slots * layers * rows * width),
            transcendentals=0,
        ),
    )(picks, left, right)


def on_device(lpanel, upanel, rowmap, colmap, blockmask, front_blocks):
    layers, n_row, n_col = (lax.axis_size(name) for name in ("gz", "row", "col"))
    levels, _, rows, _ = lpanel.shape
    depth = upanel.shape[2]
    count = colmap.shape[2]
    places = front_blocks.shape[1] // rows
    folds = n_row // n_col
    layer, row, col = (lax.axis_index(name) for name in ("gz", "row", "col"))
    fold = row % folds

    lefts = []
    for level in range(levels):
        pieces = []
        for turn in range(folds):
            pairs = []
            for a in range(n_row):
                for k in range(n_col):
                    target = k * folds + (a // n_col + turn) % folds
                    pairs.append((a * n_col + k, target * n_col + a % n_col))
            part = lpanel[level, 0]
            if folds > 1:
                part = lax.dynamic_slice_in_dim(part, ((row // n_col + turn) % folds) * depth, depth, 1)
            pieces.append(lax.ppermute(part, ("row", "col"), pairs))
        held = jnp.stack(pieces)
        step = n_col // 2
        while step >= 1:
            other = lax.ppermute(held, "col", [(i, i ^ step) for i in range(n_col)])
            held = jnp.concatenate([held, other])
            step //= 2
        lefts.append(held)
    flips = [0]
    step = n_col // 2
    while step >= 1:
        flips = flips + [flip ^ step for flip in flips]
        step //= 2
    slot_flip = jnp.asarray([flip for flip in flips for _ in range(folds)], jnp.int32)
    slot_turn = jnp.asarray([turn for _ in flips for turn in range(folds)], jnp.int32)
    slot_block = (col ^ slot_flip) + n_col * ((fold - slot_turn) % folds)
    position = jnp.asarray([flips.index(flip) for flip in range(n_col)], jnp.int32)

    def slot_of(block):
        return position[col ^ (block % n_col)] * folds + (fold - block // n_col) % folds

    small = jnp.concatenate([rowmap.reshape(-1), blockmask.reshape(-1)])
    small = lax.all_gather(small, ("gz", "row")).reshape(layers, n_row, -1)
    every_row = lax.dynamic_index_in_dim(small, row, 1, False)[:, :levels]
    masks = lax.dynamic_index_in_dim(small, layer, 0, False)[:, levels:].reshape(n_row, levels, count)
    masks = masks[slot_block]

    results = []
    for level in range(levels):
        goes = colmap[level, 0][:, None] == jnp.arange(layers, dtype=jnp.int32)[None, :]
        picks = masks[:, level, :, None].astype(jnp.float32) * goes.astype(jnp.float32)[None]
        sums = products(picks.reshape(-1), lefts[level], upanel[level, 0], layers)

        def term(block):
            block = jnp.clip(block, 0, n_row - 1)
            return lax.dynamic_index_in_dim(sums, slot_of(block), 0, False)

        up = down = None
        for stage in range(1, n_row):
            send_up = term(n_row - stage + row)
            send_down = term(stage - n_row + row)
            if stage > 1:
                send_up = (send_up.astype(jnp.float32) + up.astype(jnp.float32)).astype(jnp.bfloat16)
                send_down = (send_down.astype(jnp.float32) + down.astype(jnp.float32)).astype(jnp.bfloat16)
            up = lax.ppermute(send_up, "row", [(z, z + 1) for z in range(stage)])
            down = lax.ppermute(send_down, "row", [(n_row - 1 - z, n_row - 2 - z) for z in range(stage)])
        mine = term(row).astype(jnp.float32) + up.astype(jnp.float32) + down.astype(jnp.float32)
        mine = mine.astype(jnp.bfloat16)
        placed = jnp.zeros((places, rows, rows), jnp.float32)
        spots = jnp.arange(places, dtype=jnp.int32)
        for turn in range(layers):
            block = lax.dynamic_index_in_dim(mine, (layer + turn) % layers, 0, False)
            if turn:
                block = lax.ppermute(block, "gz", [(g, (g + turn) % layers) for g in range(layers)])
            spot = every_row[(layer - turn) % layers, level]
            placed = placed + jnp.where((spots == spot)[:, None, None], block.astype(jnp.float32)[None], 0.0)
        placed = placed.reshape(places * rows, rows)
        results.append((front_blocks[level].astype(jnp.float32) - placed).astype(jnp.bfloat16))
    return jnp.stack(results)


def solution(mesh):
    return jax.shard_map(
        on_device,
        mesh=mesh,
        in_specs=(
            P(None, "gz", "row", "col"),
            P(None, "gz", "row", "col"),
            P(None, "gz", "row"),
            P(None, "gz", "col"),
            P(None, "gz", "row", "col"),
            P(None, "row", ("gz", "col")),
        ),
        out_specs=P(None, "row", ("gz", "col")),
        check_vma=False,
    )
```

time: 234 us -> 130 us (0.56)
  waiting for transfers between devices: 187 us -> 17.2 us
  blocking collectives: 5.19 us -> 28 us
  starting transfers between devices: 7.01 us -> 27.3 us
  other arithmetic: 0.16 us -> 20.4 us
  matrix products: 12.1 us -> 0 us
  Pallas kernels: 0 us -> 9.32 us
  local copies, waits for them, and re-layouts: 8.54 us -> 12.2 us
    all_gather x4 -> x0, waiting for transfers between devices: 181 us -> none  [the longest x2 165 us: on_device(): lax.all_gather(upanel[depth, 0], 'row', axis=0, tiled=True)]
    unnamed x0 -> x1, blocking collectives: none -> 28 us
    ppermute x0 -> x20, starting transfers between devices: none -> 27.3 us  [the longest x6 14.9 us: on_device(): up = lax.ppermute(send_up, 'row', [(z, z + 1) for z in range(stage)])]
    ppermute x0 -> x20, waiting for transfers between devices: none -> 17.2 us  [the longest x4 7 us: on_device(): other = lax.ppermute(held, 'col', [(i, i ^ step) for i in range(n_col)])]
    dot_general x6 -> x0, matrix products: 12.1 us -> none  [the longest x2 7.52 us: on_device(): jnp.dot(left_rows, lax.all_gather(upanel[depth, 0], 'row', axis=0, tiled=...]
    pallas_call x0 -> x2, Pallas kernels: none -> 9.32 us  [products(): pl.pallas_call(product_kernel, grid=(slots,), in_specs=[pl.BlockSpec(memo...]
    convert_element_type x3 -> x12, other arithmetic: 0.16 us -> 9.05 us  [the longest x4 6.13 us: on_device(): (send_up.astype(jnp.float32) + up.astype(jnp.float32)).astype(jnp.bfloat16)]
    all_to_all x2 -> x0, starting transfers between devices: 6.89 us -> none  [on_device(): lax.all_to_all(sums, 'gz', split_axis=0, concat_axis=0, tiled=True)]
  transfers between devices with their start and end apart: 6 -> 20, of which waited for: 5 -> 4; matrix products, arithmetic and copies ran while one was open for 7% -> 23% of each run, Pallas kernels for 0% -> 7%
where the time goes in v1:
time: 130 us; the launch traced here: 129 us
  blocking collectives  28 us (22%)
  starting transfers between devices  27.3 us (21%)
  other arithmetic  20.4 us (16%)
  waiting for transfers between devices  17.2 us (13%)
  between operations  14.8 us (11%)
  local copies, waits for them, and re-layouts  12.2 us (9%)
  Pallas kernels  9.32 us (7%)
    unnamed x1, blocking collectives  28 us
    ppermute x6, starting transfers between devices, on_device(): up = lax.ppermute(send_up, 'row', [(z, z + 1) for z in range(stage)])  14.9 us
    pallas_call x2, Pallas kernels, products(): pl.pallas_call(product_kernel, grid=(slots,), in_specs=[pl.BlockSpec(memo...  9.32 us
    ppermute x6, starting transfers between devices, on_device(): lax.ppermute(send_down, 'row', [(n_row - 1 - z, n_row - 2 - z) for z in r...  7.31 us
    ppermute x4, waiting for transfers between devices, on_device(): other = lax.ppermute(held, 'col', [(i, i ^ step) for i in range(n_col)])  7 us
    convert_element_type x4, other arithmetic, on_device(): (send_up.astype(jnp.float32) + up.astype(jnp.float32)).astype(jnp.bfloat16)  6.13 us
    concatenate x4, other arithmetic, on_device(): held = jnp.concatenate([held, other])  5.97 us
    ppermute x6, waiting for transfers between devices, on_device(): lax.ppermute(send_down, 'row', [(n_row - 1 - z, n_row - 2 - z) for z in r...  5.79 us
  transfers between devices with their start and end apart: 20, of which 4 were waited for; matrix products, arithmetic and copies ran while one was open for 23% of the time, Pallas kernels for 7%

profile of v1, /device:TPU:0, one launch (start us, length us, event | category | flops | bytes accessed | tf_op | source)
XLA Modules:
  0.0 129.3 jit_solution(14190253177096372422)
XLA Ops:
  0.0 1.2 slice_bitcast_fusion.3
  3.1 1.3 %reduce.3 = s32[2,4]{1,0:T(2,128)S(1)} reduce(s32[2,1,1,4]{3,2,1,0:T(1,128)} %param.12, s32[]{:T(128)} %broadcast.199), dimensions={1,2}, to_apply=%param.12.reduce_sub_computation.3 | reduce | bytes 68 | tf_op args[4]
  4.5 1.2 dynamic-slice
  7.3 28.0 %all-reduce = s32[80]{0:T(128)S(1)} all-reduce(s32[80]{0:T(128)S(1)} %add_dynamic-update-slice_fusion), channel_id=2, replica_groups=mesh['gz'=2,'row'=4,'col'=4] {'gz','row'}, use_global_device_ids=true, to_apply=%add | all-reduce | flops 80 | bytes 640
  37.7 2.0 %collective-permute-start.11 = (bf16[1,256,512]{2,1,0:T(8,128)(2,1)S(1)}, bf16[1,256,512]{2,1,0:T(8,128)(2,1)S(1)}, u32[]{:S(2)}, u32[]{:S(2)}) collective-permute-start(bf16[1,256,512]{2,1,0:T(8,128)(2,1)S(1)} %bitcast.111), channel_id=1, source_target_pairs={{0,2},{1,3},{2,0},{3,1},{4,6},{5,7},{6,4},{7,5},{8,10},{9,11},{10,... | collective-permute-start | bytes 786440 | tf_op jit(solution)/shard_map/ppermute | solution.py:70
  39.7 7.0 %collective-permute-done.1 = bf16[1,256,512]{2,1,0:T(8,128)(2,1)S(1)} collective-permute-done((bf16[1,256,512]{2,1,0:T(8,128)(2,1)S(1)}, bf16[1,256,512]{2,1,0:T(8,128)(2,1)S(1)}, u32[]{:S(2)}, u32[]{:S(2)}) %collective-permute-start.1) | collective-permute-done | bytes 262176 | tf_op jit(solution)/shard_map/ppermute | solution.py:70
  56.8 1.5 %slice_bitcast_fusion.1 = (bf16[512,1024]{1,0:T(8,128)(2,1)}, bf16[512,1024]{1,0:T(8,128)(2,1)}) fusion(bf16[2,1,512,1024]{3,2,1,0:T(8,128)(2,1)S(1)} %copy-done.2), kind=kLoop, calls=%fused_computation.4 | loop fusion | bytes 4194304 | tf_op jit(solution)/shard_map/squeeze | solution.py:97
  58.3 2.1 %pad_maximum_fusion.left = bf16[4,256,512]{2,1,0:T(8,128)(2,1)} fusion(bf16[2,256,512]{2,1,0:T(8,128)(2,1)} %collective-permute-done.2, bf16[1,256,512]{2,1,0:T(8,128)(2,1)S(1)} %collective-permute-done.1, bf16[1,256,512]{2,1,0:T(8,128)(2,1)S(1)} %bitcast.116), kind=kLoop, calls=%fused_computation.1 | loop fusion | flops 1048576 | bytes 2097152 | tf_op jit(solution)/shard_map/concatenate | solution.py:71
  60.5 4.6 %shard_map.87 = bf16[4,2,256,256]{3,2,1,0:T(8,128)(2,1)} custom-call(f32[32]{0:T(128)} %mul.39.picks, bf16[4,256,512]{2,1,0:T(8,128)(2,1)} %pad_maximum_fusion.left, bf16[512,1024]{1,0:T(8,128)(2,1)} %get-tuple-element.5.right), custom_call_target="tpu_custom_call" | custom-call | flops 1073741824 | bytes 3145728 | tf_op jit(solution)/shard_map/pallas_call | solution.py:26
  65.1 1.1 dynamic-slice_bitcast_fusion.3
  66.2 2.0 %collective-permute-start.3 = (bf16[2,256,256]{2,1,0:T(8,128)(2,1)S(1)}, bf16[2,256,256]{2,1,0:T(8,128)(2,1)}, u32[]{:S(2)}, u32[]{:S(2)}) collective-permute-start(bf16[2,256,256]{2,1,0:T(8,128)(2,1)S(1)} %get-tuple-element.9), channel_id=1, source_target_pairs={{0,4},{1,5},{2,6},{3,7},{16,20},{17,21},{18,22},{19,23}} | collective-permute-start | bytes 786440 | tf_op jit(solution)/shard_map/ppermute | solution.py:110
  68.9 2.1 %pad_maximum_fusion.1.left = bf16[4,256,512]{2,1,0:T(8,128)(2,1)} fusion(bf16[2,256,512]{2,1,0:T(8,128)(2,1)} %collective-permute-done.12, bf16[1,256,512]{2,1,0:T(8,128)(2,1)S(1)} %collective-permute-done.11, bf16[1,256,512]{2,1,0:T(8,128)(2,1)S(1)} %bitcast.113), kind=kLoop, calls=%fused_computation.2 | loop fusion | flops 1048576 | bytes 2097152 | tf_op jit(solution)/shard_map/concatenate | solution.py:71
  71.0 4.7 %shard_map.88 = bf16[4,2,256,256]{3,2,1,0:T(8,128)(2,1)} custom-call(f32[32]{0:T(128)} %mul.43.picks, bf16[4,256,512]{2,1,0:T(8,128)(2,1)} %pad_maximum_fusion.1.left, bf16[512,1024]{1,0:T(8,128)(2,1)} %get-tuple-element.6.right), custom_call_target="tpu_custom_call" | custom-call | flops 1073741824 | bytes 3145728 | tf_op jit(solution)/shard_map/pallas_call | solution.py:26
  75.7 1.2 dynamic-slice_bitcast_fusion.1
  76.8 2.0 %collective-permute-start.13 = (bf16[2,256,256]{2,1,0:T(8,128)(2,1)S(1)}, bf16[2,256,256]{2,1,0:T(8,128)(2,1)}, u32[]{:S(2)}, u32[]{:S(2)}) collective-permute-start(bf16[2,256,256]{2,1,0:T(8,128)(2,1)S(1)} %get-tuple-element.13), channel_id=1, source_target_pairs={{0,4},{1,5},{2,6},{3,7},{16,20},{17,21},{18,22},{19,23}} | collective-permute-start | bytes 786440 | tf_op jit(solution)/shard_map/ppermute | solution.py:110
  78.8 1.7 %fusion.8 = bf16[2,256,256]{2,1,0:T(8,128)(2,1)} fusion(bf16[2,256,256]{2,1,0:T(8,128)(2,1)} %collective-permute-done.3, bf16[4,2,256,256]{3,2,1,0:T(8,128)(2,1)S(1)} %copy-done, s32[]{:T(128)S(6)} %select_n.257), kind=kLoop, calls=%fused_computation.24 | loop fusion | flops 524288 | bytes 786436 | tf_op jit(solution)/shard_map/convert_element_type | solution.py:108
  80.6 1.3 %collective-permute-start.4 = (bf16[2,256,256]{2,1,0:T(8,128)(2,1)}, bf16[2,256,256]{2,1,0:T(8,128)(2,1)S(1)}, u32[]{:S(2)}, u32[]{:S(2)}) collective-permute-start(bf16[2,256,256]{2,1,0:T(8,128)(2,1)} %fusion.8), channel_id=1, source_target_pairs={{0,4},{4,8},{1,5},{5,9},{2,6},{6,10},{3,7},{7,11},{16,20},{20,24},... | collective-permute-start | bytes 786440 | tf_op jit(solution)/shard_map/ppermute | solution.py:110
  86.5 1.4 %collective-permute-start.16 = (bf16[2,256,256]{2,1,0:T(8,128)(2,1)S(1)}, bf16[2,256,256]{2,1,0:T(8,128)(2,1)}, u32[]{:S(2)}, u32[]{:S(2)}) collective-permute-start(bf16[2,256,256]{2,1,0:T(8,128)(2,1)S(1)} %get-tuple-element.14), channel_id=1, source_target_pairs={{12,8},{13,9},{14,10},{15,11},{28,24},{29,25},{30,26},{31,27}} | collective-permute-start | bytes 786440 | tf_op jit(solution)/shard_map/ppermute | solution.py:111
  87.9 1.7 %fusion.2 = bf16[2,256,256]{2,1,0:T(8,128)(2,1)} fusion(bf16[2,256,256]{2,1,0:T(8,128)(2,1)} %collective-permute-done.13, bf16[4,2,256,256]{3,2,1,0:T(8,128)(2,1)S(1)} %copy-done.1, s32[]{:T(128)S(6)} %select_n.257), kind=kLoop, calls=%fused_computation.13 | loop fusion | flops 524288 | bytes 786436 | tf_op jit(solution)/shard_map/convert_element_type | solution.py:108
  89.6 2.1 %collective-permute-start.14 = (bf16[2,256,256]{2,1,0:T(8,128)(2,1)}, bf16[2,256,256]{2,1,0:T(8,128)(2,1)}, u32[]{:S(2)}, u32[]{:S(2)}) collective-permute-start(bf16[2,256,256]{2,1,0:T(8,128)(2,1)} %fusion.2), channel_id=1, source_target_pairs={{0,4},{4,8},{1,5},{5,9},{2,6},{6,10},{3,7},{7,11},{16,20},{20,24},... | collective-permute-start | bytes 786440 | tf_op jit(solution)/shard_map/ppermute | solution.py:110
  92.6 1.4 %collective-permute-start.7 = (bf16[2,256,256]{2,1,0:T(8,128)(2,1)}, bf16[2,256,256]{2,1,0:T(8,128)(2,1)}, u32[]{:S(2)}, u32[]{:S(2)}) collective-permute-start(bf16[2,256,256]{2,1,0:T(8,128)(2,1)} %get-tuple-element.8), channel_id=1, source_target_pairs={{12,8},{8,4},{13,9},{9,5},{14,10},{10,6},{15,11},{11,7},{28,24},{2... | collective-permute-start | bytes 786440 | tf_op jit(solution)/shard_map/ppermute | solution.py:111
  96.3 2.4 %collective-permute-start.5 = (bf16[2,256,256]{2,1,0:T(8,128)(2,1)S(1)}, bf16[2,256,256]{2,1,0:T(8,128)(2,1)S(1)}, u32[]{:S(2)}, u32[]{:S(2)}) collective-permute-start(bf16[2,256,256]{2,1,0:T(8,128)(2,1)S(1)} %get-tuple-element.7), channel_id=1, source_target_pairs={{0,4},{4,8},{8,12},{1,5},{5,9},{9,13},{2,6},{6,10},{10,14},{3,7},{... | collective-permute-start | bytes 786440 | tf_op jit(solution)/shard_map/ppermute | solution.py:110
  98.7 1.9 %fusion.3 = (bf16[2,256,256]{2,1,0:T(8,128)(2,1)S(1)}, bf16[2,256,256]{2,1,0:T(8,128)(2,1)}) fusion(bf16[2,256,256]{2,1,0:T(8,128)(2,1)} %collective-permute-done.14, bf16[4,2,256,256]{3,2,1,0:T(8,128)(2,1)S(1)} %copy-done.1, s32[]{:T(128)S(6)} %select_n.254, bf16[2,256,256]{2,1,0:T(8,128)(2,1)} %collective-permute-done.16, s32[]{:T(128)S(6)} %select_n.266), kind=kLoop, calls=%fused_computation.15 | loop fusion | flops 1048576 | bytes 1572872 | tf_op jit(solution)/shard_map/convert_element_type | solution.py:108
  100.6 1.4 %collective-permute-start.17 = (bf16[2,256,256]{2,1,0:T(8,128)(2,1)}, bf16[2,256,256]{2,1,0:T(8,128)(2,1)}, u32[]{:S(2)}, u32[]{:S(2)}) collective-permute-start(bf16[2,256,256]{2,1,0:T(8,128)(2,1)} %get-tuple-element.12), channel_id=1, source_target_pairs={{12,8},{8,4},{13,9},{9,5},{14,10},{10,6},{15,11},{11,7},{28,24},{2... | collective-permute-start | bytes 786440 | tf_op jit(solution)/shard_map/ppermute | solution.py:111
  102.0 1.0 fusion.7
  103.0 1.3 collective-permute-start.8
  107.0 5.1 %collective-permute-start.15 = (bf16[2,256,256]{2,1,0:T(8,128)(2,1)S(1)}, bf16[2,256,256]{2,1,0:T(8,128)(2,1)S(1)}, u32[]{:S(2)}, u32[]{:S(2)}) collective-permute-start(bf16[2,256,256]{2,1,0:T(8,128)(2,1)S(1)} %get-tuple-element.11), channel_id=1, source_target_pairs={{0,4},{4,8},{8,12},{1,5},{5,9},{9,13},{2,6},{6,10},{10,14},{3,7},{... | collective-permute-start | bytes 786440 | tf_op jit(solution)/shard_map/ppermute | solution.py:110
  112.1 1.0 fusion.1
  113.2 1.3 collective-permute-start.18
  115.2 1.5 %collective-permute-done.15 = bf16[2,256,256]{2,1,0:T(8,128)(2,1)S(1)} collective-permute-done((bf16[2,256,256]{2,1,0:T(8,128)(2,1)S(1)}, bf16[2,256,256]{2,1,0:T(8,128)(2,1)S(1)}, u32[]{:S(2)}, u32[]{:S(2)}) %collective-permute-start.15) | collective-permute-done | bytes 262176 | tf_op jit(solution)/shard_map/ppermute | solution.py:110
  116.7 5.8 %collective-permute-done.18 = bf16[2,256,256]{2,1,0:T(8,128)(2,1)S(1)} collective-permute-done((bf16[2,256,256]{2,1,0:T(8,128)(2,1)S(1)}, bf16[2,256,256]{2,1,0:T(8,128)(2,1)S(1)}, u32[]{:S(2)}, u32[]{:S(2)}) %collective-permute-start.18) | collective-permute-done | bytes 262176 | tf_op jit(solution)/shard_map/ppermute | solution.py:111
  124.8 2.9 %collective-permute-done.19 = bf16[256,256]{1,0:T(8,128)(2,1)S(1)} collective-permute-done((bf16[256,256]{1,0:T(8,128)(2,1)S(1)}, bf16[256,256]{1,0:T(8,128)(2,1)S(1)}, u32[]{:S(2)}, u32[]{:S(2)}) %collective-permute-start.19) | collective-permute-done | bytes 131104 | tf_op jit(solution)/shard_map/ppermute | solution.py:119
  (82 shorter events, 17.3 us)
Async XLA Ops:
  0.0 47.6 %copy-start.4 = (s32[4]{0:T(128)S(1)}, s32[4]{0:T(128)}, u32[]{:S(2)}) copy-start(s32[4]{0:T(128)} %constant.327.clone) | copy-start | bytes 52
  0.0 56.8 %copy-start.2 = (bf16[2,1,512,1024]{3,2,1,0:T(8,128)(2,1)S(1)}, bf16[2,1,512,1024]{3,2,1,0:T(8,128)(2,1)}, u32[]{:S(2)}) copy-start(bf16[2,1,512,1024]{3,2,1,0:T(8,128)(2,1)} %param.9) | copy-start | bytes 6291460
  1.2 36.2 %collective-permute-start = (bf16[256,512]{1,0:T(8,128)(2,1)S(1)}, bf16[256,512]{1,0:T(8,128)(2,1)S(1)}, u32[]{:S(2)}, u32[]{:S(2)}) collective-permute-start(bf16[256,512]{1,0:T(8,128)(2,1)S(1)} %get-tuple-element.17), channel_id=1, source_target_pairs={{0,0},{1,4},{2,8},{3,12},{4,1},{5,5},{6,9},{7,13},{8,2},{9,6},{10,... | collective-permute-start | bytes 786440 | tf_op jit(solution)/shard_map/ppermute | solution.py:66
  1.9 35.8 %collective-permute-start.10 = (bf16[256,512]{1,0:T(8,128)(2,1)S(1)}, bf16[256,512]{1,0:T(8,128)(2,1)S(1)}, u32[]{:S(2)}, u32[]{:S(2)}) collective-permute-start(bf16[256,512]{1,0:T(8,128)(2,1)S(1)} %get-tuple-element.18), channel_id=1, source_target_pairs={{0,0},{1,4},{2,8},{3,12},{4,1},{5,5},{6,9},{7,13},{8,2},{9,6},{10,... | collective-permute-start | bytes 786440 | tf_op jit(solution)/shard_map/ppermute | solution.py:66
  37.5 9.2 %collective-permute-start.1 = (bf16[1,256,512]{2,1,0:T(8,128)(2,1)S(1)}, bf16[1,256,512]{2,1,0:T(8,128)(2,1)S(1)}, u32[]{:S(2)}, u32[]{:S(2)}) collective-permute-start(bf16[1,256,512]{2,1,0:T(8,128)(2,1)S(1)} %bitcast.114), channel_id=1, source_target_pairs={{0,2},{1,3},{2,0},{3,1},{4,6},{5,7},{6,4},{7,5},{8,10},{9,11},{10,... | collective-permute-start | bytes 786440 | tf_op jit(solution)/shard_map/ppermute | solution.py:70
  37.7 17.7 %collective-permute-start.11 = (bf16[1,256,512]{2,1,0:T(8,128)(2,1)S(1)}, bf16[1,256,512]{2,1,0:T(8,128)(2,1)S(1)}, u32[]{:S(2)}, u32[]{:S(2)}) collective-permute-start(bf16[1,256,512]{2,1,0:T(8,128)(2,1)S(1)} %bitcast.111), channel_id=1, source_target_pairs={{0,2},{1,3},{2,0},{3,1},{4,6},{5,7},{6,4},{7,5},{8,10},{9,11},{10,... | collective-permute-start | bytes 786440 | tf_op jit(solution)/shard_map/ppermute | solution.py:70
  47.6 10.8 %collective-permute-start.2 = (bf16[2,256,512]{2,1,0:T(8,128)(2,1)}, bf16[2,256,512]{2,1,0:T(8,128)(2,1)}, u32[]{:S(2)}, u32[]{:S(2)}) collective-permute-start(bf16[2,256,512]{2,1,0:T(8,128)(2,1)} %pad_maximum_fusion.2), channel_id=1, source_target_pairs={{0,1},{1,0},{2,3},{3,2},{4,5},{5,4},{6,7},{7,6},{8,9},{9,8},{10,11... | collective-permute-start | bytes 1572872 | tf_op jit(solution)/shard_map/ppermute | solution.py:70
  56.3 12.5 %collective-permute-start.12 = (bf16[2,256,512]{2,1,0:T(8,128)(2,1)}, bf16[2,256,512]{2,1,0:T(8,128)(2,1)}, u32[]{:S(2)}, u32[]{:S(2)}) collective-permute-start(bf16[2,256,512]{2,1,0:T(8,128)(2,1)} %pad_maximum_fusion.3), channel_id=1, source_target_pairs={{0,1},{1,0},{2,3},{3,2},{4,5},{5,4},{6,7},{7,6},{8,9},{9,8},{10,11... | collective-permute-start | bytes 1572872 | tf_op jit(solution)/shard_map/ppermute | solution.py:70
  66.2 12.7 %collective-permute-start.3 = (bf16[2,256,256]{2,1,0:T(8,128)(2,1)S(1)}, bf16[2,256,256]{2,1,0:T(8,128)(2,1)}, u32[]{:S(2)}, u32[]{:S(2)}) collective-permute-start(bf16[2,256,256]{2,1,0:T(8,128)(2,1)S(1)} %get-tuple-element.9), channel_id=1, source_target_pairs={{0,4},{1,5},{2,6},{3,7},{16,20},{17,21},{18,22},{19,23}} | collective-permute-start | bytes 786440 | tf_op jit(solution)/shard_map/ppermute | solution.py:110
  68.2 23.6 %collective-permute-start.6 = (bf16[2,256,256]{2,1,0:T(8,128)(2,1)S(1)}, bf16[2,256,256]{2,1,0:T(8,128)(2,1)S(1)}, u32[]{:S(2)}, u32[]{:S(2)}) collective-permute-start(bf16[2,256,256]{2,1,0:T(8,128)(2,1)S(1)} %get-tuple-element.10), channel_id=1, source_target_pairs={{12,8},{13,9},{14,10},{15,11},{28,24},{29,25},{30,26},{31,27}} | collective-permute-start | bytes 786440 | tf_op jit(solution)/shard_map/ppermute | solution.py:111
  71.0 7.8 %copy-start = (bf16[4,2,256,256]{3,2,1,0:T(8,128)(2,1)S(1)}, bf16[4,2,256,256]{3,2,1,0:T(8,128)(2,1)}, u32[]{:S(2)}) copy-start(bf16[4,2,256,256]{3,2,1,0:T(8,128)(2,1)} %shard_map.87) | copy-start | bytes 3145732
  75.7 12.2 %copy-start.1 = (bf16[4,2,256,256]{3,2,1,0:T(8,128)(2,1)S(1)}, bf16[4,2,256,256]{3,2,1,0:T(8,128)(2,1)}, u32[]{:S(2)}) copy-start(bf16[4,2,256,256]{3,2,1,0:T(8,128)(2,1)} %shard_map.88) | copy-start | bytes 3145732
  76.8 11.0 %collective-permute-start.13 = (bf16[2,256,256]{2,1,0:T(8,128)(2,1)S(1)}, bf16[2,256,256]{2,1,0:T(8,128)(2,1)}, u32[]{:S(2)}, u32[]{:S(2)}) collective-permute-start(bf16[2,256,256]{2,1,0:T(8,128)(2,1)S(1)} %get-tuple-element.13), channel_id=1, source_target_pairs={{0,4},{1,5},{2,6},{3,7},{16,20},{17,21},{18,22},{19,23}} | collective-permute-start | bytes 786440 | tf_op jit(solution)/shard_map/ppermute | solution.py:110
  80.6 11.2 %collective-permute-start.4 = (bf16[2,256,256]{2,1,0:T(8,128)(2,1)}, bf16[2,256,256]{2,1,0:T(8,128)(2,1)S(1)}, u32[]{:S(2)}, u32[]{:S(2)}) collective-permute-start(bf16[2,256,256]{2,1,0:T(8,128)(2,1)} %fusion.8), channel_id=1, source_target_pairs={{0,4},{4,8},{1,5},{5,9},{2,6},{6,10},{3,7},{7,11},{16,20},{20,24},... | collective-permute-start | bytes 786440 | tf_op jit(solution)/shard_map/ppermute | solution.py:110
  86.5 12.2 %collective-permute-start.16 = (bf16[2,256,256]{2,1,0:T(8,128)(2,1)S(1)}, bf16[2,256,256]{2,1,0:T(8,128)(2,1)}, u32[]{:S(2)}, u32[]{:S(2)}) collective-permute-start(bf16[2,256,256]{2,1,0:T(8,128)(2,1)S(1)} %get-tuple-element.14), channel_id=1, source_target_pairs={{12,8},{13,9},{14,10},{15,11},{28,24},{29,25},{30,26},{31,27}} | collective-permute-start | bytes 786440 | tf_op jit(solution)/shard_map/ppermute | solution.py:111
  89.6 9.1 %collective-permute-start.14 = (bf16[2,256,256]{2,1,0:T(8,128)(2,1)}, bf16[2,256,256]{2,1,0:T(8,128)(2,1)}, u32[]{:S(2)}, u32[]{:S(2)}) collective-permute-start(bf16[2,256,256]{2,1,0:T(8,128)(2,1)} %fusion.2), channel_id=1, source_target_pairs={{0,4},{4,8},{1,5},{5,9},{2,6},{6,10},{3,7},{7,11},{16,20},{20,24},... | collective-permute-start | bytes 786440 | tf_op jit(solution)/shard_map/ppermute | solution.py:110
  92.6 9.4 %collective-permute-start.7 = (bf16[2,256,256]{2,1,0:T(8,128)(2,1)}, bf16[2,256,256]{2,1,0:T(8,128)(2,1)}, u32[]{:S(2)}, u32[]{:S(2)}) collective-permute-start(bf16[2,256,256]{2,1,0:T(8,128)(2,1)} %get-tuple-element.8), channel_id=1, source_target_pairs={{12,8},{8,4},{13,9},{9,5},{14,10},{10,6},{15,11},{11,7},{28,24},{2... | collective-permute-start | bytes 786440 | tf_op jit(solution)/shard_map/ppermute | solution.py:111
  96.3 18.1 %collective-permute-start.5 = (bf16[2,256,256]{2,1,0:T(8,128)(2,1)S(1)}, bf16[2,256,256]{2,1,0:T(8,128)(2,1)S(1)}, u32[]{:S(2)}, u32[]{:S(2)}) collective-permute-start(bf16[2,256,256]{2,1,0:T(8,128)(2,1)S(1)} %get-tuple-element.7), channel_id=1, source_target_pairs={{0,4},{4,8},{8,12},{1,5},{5,9},{9,13},{2,6},{6,10},{10,14},{3,7},{... | collective-permute-start | bytes 786440 | tf_op jit(solution)/shard_map/ppermute | solution.py:110
  100.6 11.5 %collective-permute-start.17 = (bf16[2,256,256]{2,1,0:T(8,128)(2,1)}, bf16[2,256,256]{2,1,0:T(8,128)(2,1)}, u32[]{:S(2)}, u32[]{:S(2)}) collective-permute-start(bf16[2,256,256]{2,1,0:T(8,128)(2,1)} %get-tuple-element.12), channel_id=1, source_target_pairs={{12,8},{8,4},{13,9},{9,5},{14,10},{10,6},{15,11},{11,7},{28,24},{2... | collective-permute-start | bytes 786440 | tf_op jit(solution)/shard_map/ppermute | solution.py:111
  103.0 11.5 %collective-permute-start.8 = (bf16[2,256,256]{2,1,0:T(8,128)(2,1)S(1)}, bf16[2,256,256]{2,1,0:T(8,128)(2,1)S(1)}, u32[]{:S(2)}, u32[]{:S(2)}) collective-permute-start(bf16[2,256,256]{2,1,0:T(8,128)(2,1)S(1)} %fusion.7), channel_id=1, source_target_pairs={{12,8},{8,4},{4,0},{13,9},{9,5},{5,1},{14,10},{10,6},{6,2},{15,11}... | collective-permute-start | bytes 786440 | tf_op jit(solution)/shard_map/ppermute | solution.py:111
  107.0 9.7 %collective-permute-start.15 = (bf16[2,256,256]{2,1,0:T(8,128)(2,1)S(1)}, bf16[2,256,256]{2,1,0:T(8,128)(2,1)S(1)}, u32[]{:S(2)}, u32[]{:S(2)}) collective-permute-start(bf16[2,256,256]{2,1,0:T(8,128)(2,1)S(1)} %get-tuple-element.11), channel_id=1, source_target_pairs={{0,4},{4,8},{8,12},{1,5},{5,9},{9,13},{2,6},{6,10},{10,14},{3,7},{... | collective-permute-start | bytes 786440 | tf_op jit(solution)/shard_map/ppermute | solution.py:110
  113.2 9.3 %collective-permute-start.18 = (bf16[2,256,256]{2,1,0:T(8,128)(2,1)S(1)}, bf16[2,256,256]{2,1,0:T(8,128)(2,1)S(1)}, u32[]{:S(2)}, u32[]{:S(2)}) collective-permute-start(bf16[2,256,256]{2,1,0:T(8,128)(2,1)S(1)} %fusion.1), channel_id=1, source_target_pairs={{12,8},{8,4},{4,0},{13,9},{9,5},{5,1},{14,10},{10,6},{6,2},{15,11}... | collective-permute-start | bytes 786440 | tf_op jit(solution)/shard_map/ppermute | solution.py:111
  114.6 13.2 %copy-start.3 = (bf16[2,512,256]{2,1,0:T(8,128)(2,1)S(1)}, bf16[2,512,256]{2,1,0:T(8,128)(2,1)}, u32[]{:S(2)}) copy-start(bf16[2,512,256]{2,1,0:T(8,128)(2,1)} %param.13) | copy-start | bytes 1572868
  114.6 10.1 %collective-permute-start.9 = (bf16[256,256]{1,0:T(8,128)(2,1)S(1)}, bf16[256,256]{1,0:T(8,128)(2,1)S(1)}, u32[]{:S(2)}, u32[]{:S(2)}) collective-permute-start(bf16[256,256]{1,0:T(8,128)(2,1)S(1)} %get-tuple-element.20), channel_id=1, source_target_pairs={{0,16},{16,0},{1,17},{17,1},{2,18},{18,2},{3,19},{19,3},{4,20},{20... | collective-permute-start | bytes 393224 | tf_op jit(solution)/shard_map/ppermute | solution.py:119
  122.6 5.0 %collective-permute-start.19 = (bf16[256,256]{1,0:T(8,128)(2,1)S(1)}, bf16[256,256]{1,0:T(8,128)(2,1)S(1)}, u32[]{:S(2)}, u32[]{:S(2)}) collective-permute-start(bf16[256,256]{1,0:T(8,128)(2,1)S(1)} %get-tuple-element.22), channel_id=1, source_target_pairs={{0,16},{16,0},{1,17},{17,1},{2,18},{18,2},{3,19},{19,3},{4,20},{20... | collective-permute-start | bytes 393224 | tf_op jit(solution)/shard_map/ppermute | solution.py:119
  128.5 0.8 copy-start.5

commit v2 on v0

v2 whole, which is shorter than its diff:
```python
import functools

import jax
import jax.numpy as jnp
from jax import lax
from jax.experimental import pallas as pl
from jax.experimental.pallas import tpu as pltpu
from jax.sharding import PartitionSpec as P


def product_kernel(level, turns, n_row, n_col, *refs):
    folds = n_row // n_col
    masks, colmap = refs[:n_row], refs[n_row]
    lefts, right = refs[n_row + 1 : 2 * n_row + 1], refs[2 * n_row + 1]
    outs, held = refs[2 * n_row + 2 : -1], refs[-1]
    g, z, c = (lax.axis_index(name) for name in ("gz", "row", "col"))
    for slot, left in enumerate(lefts):
        held[slot] = left[...]
    layers, _, width = outs[0].shape
    count = right.shape[3] // width
    for turn, out in zip(turns, outs):
        a = z ^ turn
        slot = (c ^ (a % n_col)) * folds + ((z % folds) ^ (a // n_col))
        tile = jnp.dot(held[slot], right[0, 0], preferred_element_type=jnp.float32)
        for u in range(layers):
            total = None
            for j in range(count):
                pick = jnp.where(colmap[level, 0, j] == (g ^ u), masks[turn][level, 0, 0, j], 0)
                term = pick.astype(jnp.float32) * tile[:, j * width : (j + 1) * width]
                total = term if total is None else total + term
            out[u] = total.astype(out.dtype)


def products(level, turns, masks, colmap, lefts, upanel, layers, n_row, n_col):
    rows, depth = lefts[0].shape
    columns = upanel.shape[3]
    whole = pl.BlockSpec(memory_space=pltpu.VMEM)
    room = 4 * (2 * n_row * rows * depth + depth * columns + 2 * len(turns) * layers * rows * rows) + (4 << 20)
    return pl.pallas_call(
        functools.partial(product_kernel, level, turns, n_row, n_col),
        grid=(1,),
        in_specs=[pl.BlockSpec(memory_space=pltpu.SMEM)] * (n_row + 1)
        + [whole] * n_row
        + [pl.BlockSpec((1, 1, depth, columns), lambda i: (level, 0, 0, 0))],
        out_specs=[whole] * len(turns),
        out_shape=[jax.ShapeDtypeStruct((layers, rows, rows), jnp.bfloat16)] * len(turns),
        scratch_shapes=[pltpu.VMEM((n_row, rows, depth), jnp.bfloat16)],
        compiler_params=pltpu.CompilerParams(vmem_limit_bytes=room),
        cost_estimate=pl.CostEstimate(
            flops=2 * len(turns) * rows * depth * columns,
            bytes_accessed=2 * (n_row * rows * depth + depth * columns + len(turns) * layers * rows * rows),
            transcendentals=0,
        ),
        name=f"product_{level}_{turns[0]}",
    )(*masks, colmap, *lefts, upanel)


def place_kernel(level, layers, counts, *refs):
    maps, front, out = refs[:layers], refs[layers], refs[-1]
    blocks = list(refs[layers + 1 : layers + 1 + sum(counts)])
    width = out.shape[2]
    totals = []
    for n in counts:
        total = None
        for _ in range(n):
            ref = blocks.pop(0)
            term = (ref[0] if len(ref.shape) == 3 else ref[...]).astype(jnp.float32)
            total = term if total is None else total + term
        totals.append(total)
    for f in range(out.shape[1] // width):
        span = slice(f * width, (f + 1) * width)
        moved = None
        for u in range(layers):
            here = (maps[u][level, 0, 0] == f).astype(jnp.float32)
            moved = here * totals[u] if moved is None else moved + here * totals[u]
        out[0, span] = (front[0, span].astype(jnp.float32) - moved).astype(out.dtype)


def place(level, maps, front, groups, before):
    layers = len(groups)
    counts = tuple(len(group) for group in groups)
    _, height, width = front.shape
    specs = [pl.BlockSpec(memory_space=pltpu.SMEM)] * layers
    specs.append(pl.BlockSpec((1, height, width), lambda i: (level, 0, 0)))
    blocks = [block for group in groups for block in group]
    for block in blocks:
        if block.ndim == 3:
            specs.append(pl.BlockSpec((1, *block.shape[1:]), lambda i: (0, 0, 0)))
        else:
            specs.append(pl.BlockSpec(memory_space=pltpu.VMEM))
    args = [*maps, front, *blocks]
    aliases = {}
    if before is not None:
        aliases = {len(args): 0}
        args.append(before)
        specs.append(pl.BlockSpec(memory_space=pl.ANY))
    return pl.pallas_call(
        functools.partial(place_kernel, level, layers, counts),
        grid=(1,),
        in_specs=specs,
        out_specs=pl.BlockSpec((1, height, width), lambda i: (level, 0, 0)),
        out_shape=jax.ShapeDtypeStruct(front.shape, front.dtype),
        input_output_aliases=aliases,
        compiler_params=pltpu.CompilerParams(vmem_limit_bytes=32 * height * width + (2 << 20)),
        cost_estimate=pl.CostEstimate(
            flops=2 * layers * height * width, bytes_accessed=8 * height * width, transcendentals=0
        ),
        name=f"place_{level}",
    )(*args)


def on_device(lpanel, upanel, rowmap, colmap, blockmask, front_blocks):
    layers, n_row, n_col = (lax.axis_size(name) for name in ("gz", "row", "col"))
    levels = lpanel.shape[0]
    depth = upanel.shape[2]
    folds = n_row // n_col
    row = lax.axis_index("row")

    lefts = []
    for level in range(levels):
        hop = (level % 2) * (n_col // 2)
        pieces = {}
        for turn in range(folds):
            part = lpanel[level, 0]
            if folds > 1:
                part = lax.dynamic_slice_in_dim(part, ((row // n_col) ^ turn) * depth, depth, 1)
            if hop:
                part = lax.ppermute(part, "col", [(k, k ^ hop) for k in range(n_col)])
            pairs = []
            for a in range(n_row):
                for k in range(n_col):
                    target = k * folds + ((a // n_col) ^ turn)
                    pairs.append((a * n_col + (k ^ hop), target * n_col + a % n_col))
            pieces[0, turn] = lax.ppermute(part, ("row", "col"), pairs)
        step = n_col // 2
        while step >= 1:
            swap = [(k, k ^ step) for k in range(n_col)]
            for (flip, turn), piece in list(pieces.items()):
                pieces[flip ^ step, turn] = lax.ppermute(piece, "col", swap)
            step //= 2
        lefts.append([pieces[flip, turn] for flip in range(n_col) for turn in range(folds)])

    masks = [blockmask]
    for turn in range(1, n_row):
        masks.append(lax.ppermute(blockmask, "row", [(z, z ^ turn) for z in range(n_row)]))
    maps = [rowmap]
    for u in range(1, layers):
        maps.append(lax.ppermute(rowmap, "gz", [(g, g ^ u) for g in range(layers)]))

    def total(blocks):
        return sum(block.astype(jnp.float32) for block in blocks).astype(jnp.bfloat16)

    result = None
    half = n_row // 2
    away = [turn for turn in reversed(range(n_row)) if turn % 2]
    stay = [turn for turn in reversed(range(n_row)) if not turn % 2]
    for level in range(levels):
        terms = {}
        for turns in (away, stay):
            made = products(level, turns, masks, colmap, lefts[level], upanel, layers, n_row, n_col)
            terms.update({turn: [block] for turn, block in zip(turns, made)})
        bit = 1
        while bit < half:
            swap = [(z, z ^ bit) for z in range(n_row)]
            for turn in reversed(range(0, n_row, bit)):
                if turn & bit:
                    terms[turn ^ bit].append(lax.ppermute(total(terms.pop(turn)), "row", swap))
            bit *= 2
        groups = [terms[0]]
        ends = [(g, z) for g in range(layers) for z in range(n_row)]
        for u in range(layers):
            far = [(g * n_row + z, (g ^ u) * n_row + (z ^ half)) for g, z in ends]
            block = lax.ppermute(total([term[u] for term in terms[half]]), ("gz", "row"), far)
            if u:
                swap = [(g, g ^ u) for g in range(layers)]
                near = lax.ppermute(total([term[u] for term in terms[0]]), "gz", swap)
                groups.append([near, block])
            else:
                groups[0] = [*groups[0], block]
        result = place(level, maps, front_blocks, groups, result)
    return result


def solution(mesh):
    return jax.shard_map(
        on_device,
        mesh=mesh,
        in_specs=(
            P(None, "gz", "row", "col"),
            P(None, "gz", "row", "col"),
            P(None, "gz", "row"),
            P(None, "gz", "col"),
            P(None, "gz", "row", "col"),
            P(None, "row", ("gz", "col")),
        ),
        out_specs=P(None, "row", ("gz", "col")),
        check_vma=False,
    )
```

time: 234 us -> 89.5 us (0.38)
  waiting for transfers between devices: 187 us -> 32.5 us
  starting transfers between devices: 7.01 us -> 40 us
  between operations: 13.3 us -> 0.12 us
  matrix products: 12.1 us -> 0 us
  Pallas kernels: 0 us -> 9.61 us
  blocking collectives: 5.19 us -> 0 us
  local copies, waits for them, and re-layouts: 8.54 us -> 5.82 us
    all_gather x4 -> x0, waiting for transfers between devices: 181 us -> none  [the longest x2 165 us: on_device(): lax.all_gather(upanel[depth, 0], 'row', axis=0, tiled=True)]
    ppermute x0 -> x23, starting transfers between devices: none -> 40 us  [the longest x6 15.5 us: on_device(): pieces[flip ^ step, turn] = lax.ppermute(piece, 'col', swap)]
    ppermute x0 -> x23, waiting for transfers between devices: none -> 32.5 us  [the longest x4 12.4 us: on_device(): terms[turn ^ bit].append(lax.ppermute(total(terms.pop(turn)), 'row', swap))]
    dot_general x6 -> x0, matrix products: 12.1 us -> none  [the longest x2 7.52 us: on_device(): jnp.dot(left_rows, lax.all_gather(upanel[depth, 0], 'row', axis=0, tiled=...]
    pallas_call x0 -> x6, Pallas kernels: none -> 9.61 us  [the longest x4 6.39 us: products(): pl.pallas_call(functools.partial(product_kernel, level, turns, n_row, n_c...]
    all_to_all x2 -> x0, starting transfers between devices: 6.89 us -> none  [on_device(): lax.all_to_all(sums, 'gz', split_axis=0, concat_axis=0, tiled=True)]
    all_gather x1 -> x0, blocking collectives: 5.19 us -> none  [on_device(): every_row = lax.all_gather(rowmap[:, :, 0], 'gz', axis=1, tiled=True)]
    slice x3 -> x0, local copies, waits for them, and re-layouts: 5.19 us -> none  [the longest x1 3.05 us: on_device(): upanel[depth, 0]]
  transfers between devices with their start and end apart: 6 -> 23, of which waited for: 5 -> 10; matrix products, arithmetic and copies ran while one was open for 7% -> 1% of each run, Pallas kernels for 0% -> 9%
where the time goes in v2:
time: 89.5 us; the launch traced here: 89.2 us
  starting transfers between devices  40 us (45%)
  waiting for transfers between devices  32.5 us (36%)
  Pallas kernels  9.61 us (11%)
  local copies, waits for them, and re-layouts  5.82 us (7%)
  other arithmetic  1.1 us (1%)
    ppermute x6, starting transfers between devices, on_device(): pieces[flip ^ step, turn] = lax.ppermute(piece, 'col', swap)  15.5 us
    ppermute x4, waiting for transfers between devices, on_device(): terms[turn ^ bit].append(lax.ppermute(total(terms.pop(turn)), 'row', swap))  12.4 us
    ppermute x4, waiting for transfers between devices, on_device(): lax.ppermute(total([term[u] for term in terms[half]]), ('gz', 'row'), far)  8.12 us
    ppermute x6, waiting for transfers between devices, on_device(): pieces[flip ^ step, turn] = lax.ppermute(piece, 'col', swap)  7.07 us
    ppermute x1, starting transfers between devices, on_device(): part = lax.ppermute(part, 'col', [(k, k ^ hop) for k in range(n_col)])  6.82 us
    pallas_call x4, Pallas kernels, products(): pl.pallas_call(functools.partial(product_kernel, level, turns, n_row, n_c...  6.39 us
    ppermute x3, waiting for transfers between devices, on_device(): lax.ppermute(blockmask, 'row', [(z, z ^ turn) for z in range(n_row)])  4.95 us
    ppermute x4, starting transfers between devices, on_device(): lax.ppermute(total([term[u] for term in terms[half]]), ('gz', 'row'), far)  4.92 us
  transfers between devices with their start and end apart: 23, of which 10 were waited for; matrix products, arithmetic and copies ran while one was open for 1% of the time, Pallas kernels for 9%

profile of v2, /device:TPU:0, one launch (start us, length us, event | category | flops | bytes accessed | tf_op | source)
XLA Modules:
  0.0 89.2 jit_solution(4400146325368163794)
XLA Ops:
  0.0 1.1 %slice_bitcast_fusion = (bf16[256,512]{1,0:T(8,128)(2,1)S(1)}, bf16[256,512]{1,0:T(8,128)(2,1)S(1)}) fusion(bf16[2,1,256,512]{3,2,1,0:T(8,128)(2,1)} %param.6), kind=kLoop, calls=%fused_computation.3 | loop fusion | bytes 1048576 | tf_op jit(solution)/shard_map/squeeze | solution.py:124
  1.8 6.8 %collective-permute-start.4 = (bf16[256,512]{1,0:T(8,128)(2,1)S(1)}, bf16[256,512]{1,0:T(8,128)(2,1)S(1)}, u32[]{:S(2)}, u32[]{:S(2)}) collective-permute-start(bf16[256,512]{1,0:T(8,128)(2,1)S(1)} %get-tuple-element.24), channel_id=1, source_target_pairs={{0,2},{1,3},{2,0},{3,1},{4,6},{5,7},{6,4},{7,5},{8,10},{9,11},{10,... | collective-permute-start | bytes 786440 | tf_op jit(solution)/shard_map/ppermute | solution.py:128
  8.6 13.5 %collective-permute-start.16 = (bf16[256,512]{1,0:T(8,128)(2,1)S(1)}, bf16[256,512]{1,0:T(8,128)(2,1)S(1)}, u32[]{:S(2)}, u32[]{:S(2)}) collective-permute-start(bf16[256,512]{1,0:T(8,128)(2,1)S(1)} %collective-permute-done.14.refs_5_), channel_id=1, source_target_pairs={{0,2},{1,3},{2,0},{3,1},{4,6},{5,7},{6,4},{7,5},{8,10},{9,11},{10,... | collective-permute-start | bytes 786440 | tf_op jit(solution)/shard_map/ppermute | solution.py:139
  22.2 7.1 %collective-permute-done.16.refs_7_ = bf16[256,512]{1,0:T(8,128)(2,1)S(1)} collective-permute-done((bf16[256,512]{1,0:T(8,128)(2,1)S(1)}, bf16[256,512]{1,0:T(8,128)(2,1)S(1)}, u32[]{:S(2)}, u32[]{:S(2)}) %collective-permute-start.16) | collective-permute-done | bytes 262176 | tf_op jit(solution)/shard_map/ppermute | solution.py:139
  29.3 2.9 %collective-permute-start.1 = (s32[2,1,1,4]{3,2,1,0:T(1,128)}, s32[2,1,1,4]{3,2,1,0:T(1,128)S(1)}, u32[]{:S(2)}, u32[]{:S(2)}) collective-permute-start(s32[2,1,1,4]{3,2,1,0:T(1,128)} %refs_0_.9), channel_id=1, source_target_pairs={{0,4},{4,0},{8,12},{12,8},{1,5},{5,1},{9,13},{13,9},{2,6},{6,2},{1... | collective-permute-start | bytes 104 | tf_op jit(solution)/shard_map/ppermute | solution.py:145
  32.2 1.8 %collective-permute-done.1.refs_1_ = s32[2,1,1,4]{3,2,1,0:T(1,128)S(1)} collective-permute-done((s32[2,1,1,4]{3,2,1,0:T(1,128)}, s32[2,1,1,4]{3,2,1,0:T(1,128)S(1)}, u32[]{:S(2)}, u32[]{:S(2)}) %collective-permute-start.1) | collective-permute-done | bytes 64 | tf_op jit(solution)/shard_map/ppermute | solution.py:145
  34.6 1.8 %collective-permute-start.7 = (bf16[256,512]{1,0:T(8,128)(2,1)S(1)}, bf16[256,512]{1,0:T(8,128)(2,1)S(1)}, u32[]{:S(2)}, u32[]{:S(2)}) collective-permute-start(bf16[256,512]{1,0:T(8,128)(2,1)S(1)} %collective-permute-done.5.refs_5_), channel_id=1, source_target_pairs={{0,2},{1,3},{2,0},{3,1},{4,6},{5,7},{6,4},{7,5},{8,10},{9,11},{10,... | collective-permute-start | bytes 786440 | tf_op jit(solution)/shard_map/ppermute | solution.py:139
  36.9 2.7 %collective-permute-done.3.refs_3_ = s32[2,1,1,4]{3,2,1,0:T(1,128)S(1)} collective-permute-done((s32[2,1,1,4]{3,2,1,0:T(1,128)}, s32[2,1,1,4]{3,2,1,0:T(1,128)S(1)}, u32[]{:S(2)}, u32[]{:S(2)}) %collective-permute-start.3) | collective-permute-done | bytes 64 | tf_op jit(solution)/shard_map/ppermute | solution.py:145
  39.6 1.6 %copy-done = bf16[2,1,512,1024]{3,2,1,0:T(8,128)(2,1)S(1)} copy-done((bf16[2,1,512,1024]{3,2,1,0:T(8,128)(2,1)S(1)}, bf16[2,1,512,1024]{3,2,1,0:T(8,128)(2,1)}, u32[]{:S(2)}) %copy-start) | copy-done | bytes 2097176
  42.5 2.1 %product_0_3.1 = (bf16[2,256,256]{2,1,0:T(8,128)(2,1)S(1)}, bf16[2,256,256]{2,1,0:T(8,128)(2,1)}) custom-call(s32[2,1,1,4]{3,2,1,0:T(1,128)S(1)} %copy-done.5, s32[2,1,1,4]{3,2,1,0:T(1,128)S(1)} %collective-permute-done.1.refs_1_, s32[2,1,1,4]{3,2,1,0:T(1,128)S(1)} %collective-permute-done.2.refs_2_, s32[2,1,1,4]{3,2,1,0:T(1,128)S(1)} %collective-permute-done.3.refs_3_, ...), custom_call_target="tpu_custom_call" | custom-call | flops 536870912 | bytes 2621440 | tf_op jit(solution)/shard_map/product_0_3/pallas_call | solution.py:39
  44.6 0.7 copy-done.9
  45.7 1.5 %collective-permute-start = (s32[2,1,1]{2,1,0:T(1,128)S(1)}, s32[2,1,1]{2,1,0:T(1,128)S(1)}, u32[]{:S(2)}, u32[]{:S(2)}) collective-permute-start(s32[2,1,1]{2,1,0:T(1,128)S(1)} %copy.10.refs_0_), channel_id=1, source_target_pairs={{0,16},{16,0},{1,17},{17,1},{2,18},{18,2},{3,19},{19,3},{4,20},{20... | collective-permute-start | bytes 32 | tf_op jit(solution)/shard_map/ppermute | solution.py:148
  47.2 1.8 %collective-permute-start.19 = (bf16[2,256,256]{2,1,0:T(8,128)(2,1)}, bf16[2,256,256]{2,1,0:T(8,128)(2,1)S(1)}, u32[]{:S(2)}, u32[]{:S(2)}) collective-permute-start(bf16[2,256,256]{2,1,0:T(8,128)(2,1)} %copy-done.9), channel_id=1, source_target_pairs={{0,4},{4,0},{8,12},{12,8},{1,5},{5,1},{9,13},{13,9},{2,6},{6,2},{1... | collective-permute-start | bytes 786440 | tf_op jit(solution)/shard_map/ppermute | solution.py:167
  49.2 0.9 %copy-done.4 = bf16[256,512]{1,0:T(8,128)(2,1)S(1)} copy-done((bf16[256,512]{1,0:T(8,128)(2,1)S(1)}, bf16[256,512]{1,0:T(8,128)(2,1)}, u32[]{:S(2)}) %copy-start.4) | copy-done | bytes 262168
  50.2 1.4 %product_0_2.1 = (bf16[2,256,256]{2,1,0:T(8,128)(2,1)S(1)}, bf16[2,256,256]{2,1,0:T(8,128)(2,1)S(1)}) custom-call(s32[2,1,1,4]{3,2,1,0:T(1,128)S(1)} %copy-done.6, s32[2,1,1,4]{3,2,1,0:T(1,128)S(1)} %collective-permute-done.1.refs_1_, s32[2,1,1,4]{3,2,1,0:T(1,128)S(1)} %collective-permute-done.2.refs_2_, s32[2,1,1,4]{3,2,1,0:T(1,128)S(1)} %collective-permute-done.3.refs_3_, ...), custom_call_target="tpu_custom_call" | custom-call | flops 536870912 | bytes 2621440 | tf_op jit(solution)/shard_map/product_0_2/pallas_call | solution.py:39
  51.6 2.4 %collective-permute-done.18.refs_4_ = bf16[2,256,256]{2,1,0:T(8,128)(2,1)} collective-permute-done((bf16[2,256,256]{2,1,0:T(8,128)(2,1)}, bf16[2,256,256]{2,1,0:T(8,128)(2,1)}, u32[]{:S(2)}, u32[]{:S(2)}) %collective-permute-start.18) | collective-permute-done | bytes 262176 | tf_op jit(solution)/shard_map/ppermute | solution.py:167
  54.1 0.9 %fusion.4 = bf16[256,256]{1,0:T(8,128)(2,1)S(1)} fusion(bf16[2,256,256]{2,1,0:T(8,128)(2,1)} %collective-permute-done.18.refs_4_, bf16[2,256,256]{2,1,0:T(8,128)(2,1)S(1)} %get-tuple-element.17.refs_3_), kind=kLoop, calls=%fused_computation.12 | loop fusion | flops 262144 | bytes 393216 | tf_op jit(solution)/shard_map/convert_element_type | solution.py:151
  55.0 2.4 %collective-permute-start.21 = (bf16[256,256]{1,0:T(8,128)(2,1)S(1)}, bf16[256,256]{1,0:T(8,128)(2,1)S(1)}, u32[]{:S(2)}, u32[]{:S(2)}) collective-permute-start(bf16[256,256]{1,0:T(8,128)(2,1)S(1)} %fusion.4), channel_id=1, source_target_pairs={{0,16},{16,0},{1,17},{17,1},{2,18},{18,2},{3,19},{19,3},{4,20},{20... | collective-permute-start | bytes 393224 | tf_op jit(solution)/shard_map/ppermute | solution.py:176
  57.4 1.4 %product_1_3.1 = (bf16[2,256,256]{2,1,0:T(8,128)(2,1)S(1)}, bf16[2,256,256]{2,1,0:T(8,128)(2,1)S(1)}) custom-call(s32[2,1,1,4]{3,2,1,0:T(1,128)S(1)} %copy-done.6, s32[2,1,1,4]{3,2,1,0:T(1,128)S(1)} %collective-permute-done.1.refs_1_, s32[2,1,1,4]{3,2,1,0:T(1,128)S(1)} %collective-permute-done.2.refs_2_, s32[2,1,1,4]{3,2,1,0:T(1,128)S(1)} %collective-permute-done.3.refs_3_, ...), custom_call_target="tpu_custom_call" | custom-call | flops 536870912 | bytes 2621440 | tf_op jit(solution)/shard_map/product_1_3/pallas_call | solution.py:39
  59.0 1.2 %collective-permute-start.20 = (bf16[256,256]{1,0:T(8,128)(2,1)S(1)}, bf16[256,256]{1,0:T(8,128)(2,1)S(1)}, u32[]{:S(2)}, u32[]{:S(2)}) collective-permute-start(bf16[256,256]{1,0:T(8,128)(2,1)S(1)} %get-tuple-element.22), channel_id=1, source_target_pairs={{0,8},{4,12},{8,0},{12,4},{16,24},{20,28},{24,16},{28,20},{1,9},{5... | collective-permute-start | bytes 393224 | tf_op jit(solution)/shard_map/ppermute | solution.py:173
  60.2 0.9 %collective-permute-start.10 = (bf16[2,256,256]{2,1,0:T(8,128)(2,1)S(1)}, bf16[2,256,256]{2,1,0:T(8,128)(2,1)S(1)}, u32[]{:S(2)}, u32[]{:S(2)}) collective-permute-start(bf16[2,256,256]{2,1,0:T(8,128)(2,1)S(1)} %get-tuple-element.16), channel_id=1, source_target_pairs={{0,4},{4,0},{8,12},{12,8},{1,5},{5,1},{9,13},{13,9},{2,6},{6,2},{1... | collective-permute-start | bytes 786440 | tf_op jit(solution)/shard_map/ppermute | solution.py:167
  61.1 1.4 %product_1_2.1 = (bf16[2,256,256]{2,1,0:T(8,128)(2,1)S(1)}, bf16[2,256,256]{2,1,0:T(8,128)(2,1)S(1)}) custom-call(s32[2,1,1,4]{3,2,1,0:T(1,128)S(1)} %copy-done.6, s32[2,1,1,4]{3,2,1,0:T(1,128)S(1)} %collective-permute-done.1.refs_1_, s32[2,1,1,4]{3,2,1,0:T(1,128)S(1)} %collective-permute-done.2.refs_2_, s32[2,1,1,4]{3,2,1,0:T(1,128)S(1)} %collective-permute-done.3.refs_3_, ...), custom_call_target="tpu_custom_call" | custom-call | flops 536870912 | bytes 2621440 | tf_op jit(solution)/shard_map/product_1_2/pallas_call | solution.py:39
  62.6 6.5 %collective-permute-done.9.refs_4_ = bf16[2,256,256]{2,1,0:T(8,128)(2,1)S(1)} collective-permute-done((bf16[2,256,256]{2,1,0:T(8,128)(2,1)S(1)}, bf16[2,256,256]{2,1,0:T(8,128)(2,1)S(1)}, u32[]{:S(2)}, u32[]{:S(2)}) %collective-permute-start.9) | collective-permute-done | bytes 262176 | tf_op jit(solution)/shard_map/ppermute | solution.py:167
  69.1 0.8 collective-permute-start.22
  69.9 3.4 %collective-permute-done.10 = bf16[2,256,256]{2,1,0:T(8,128)(2,1)S(1)} collective-permute-done((bf16[2,256,256]{2,1,0:T(8,128)(2,1)S(1)}, bf16[2,256,256]{2,1,0:T(8,128)(2,1)S(1)}, u32[]{:S(2)}, u32[]{:S(2)}) %collective-permute-start.10) | collective-permute-done | bytes 262176 | tf_op jit(solution)/shard_map/ppermute | solution.py:167
  73.3 1.5 %collective-permute-start.12 = (bf16[256,256]{1,0:T(8,128)(2,1)S(1)}, bf16[256,256]{1,0:T(8,128)(2,1)S(1)}, u32[]{:S(2)}, u32[]{:S(2)}) collective-permute-start(bf16[256,256]{1,0:T(8,128)(2,1)S(1)} %fusion.1), channel_id=1, source_target_pairs={{0,16},{16,0},{1,17},{17,1},{2,18},{18,2},{3,19},{19,3},{4,20},{20... | collective-permute-start | bytes 393224 | tf_op jit(solution)/shard_map/ppermute | solution.py:176
  75.0 2.8 %collective-permute-start.13 = (bf16[256,256]{1,0:T(8,128)(2,1)S(1)}, bf16[256,256]{1,0:T(8,128)(2,1)S(1)}, u32[]{:S(2)}, u32[]{:S(2)}) collective-permute-start(bf16[256,256]{1,0:T(8,128)(2,1)S(1)} %get-tuple-element.25), channel_id=1, source_target_pairs={{0,24},{4,28},{8,16},{12,20},{16,8},{20,12},{24,0},{28,4},{1,25},{... | collective-permute-start | bytes 393224 | tf_op jit(solution)/shard_map/ppermute | solution.py:173
  77.9 5.5 %collective-permute-done.22.refs_7_ = bf16[256,256]{1,0:T(8,128)(2,1)S(1)} collective-permute-done((bf16[256,256]{1,0:T(8,128)(2,1)S(1)}, bf16[256,256]{1,0:T(8,128)(2,1)S(1)}, u32[]{:S(2)}, u32[]{:S(2)}) %collective-permute-start.22) | collective-permute-done | bytes 131104 | tf_op jit(solution)/shard_map/ppermute | solution.py:173
  83.4 1.8 %place_0.1.refs_8_ = bf16[2,512,256]{2,1,0:T(8,128)(2,1)} custom-call(s32[2,1,1]{2,1,0:T(1,128)S(1)} %copy.10.refs_0_, s32[2,1,1]{2,1,0:T(1,128)S(1)} %collective-permute-done.refs_1_, bf16[2,512,256]{2,1,0:T(8,128)(2,1)S(1)} %copy-done.2, bf16[2,256,256]{2,1,0:T(8,128)(2,1)S(1)} %get-tuple-element.17.refs_3_, ...), custom_call_target="tpu_custom_call" | custom-call | flops 524288 | bytes 1048576 | tf_op jit(solution)/shard_map/place_0/pallas_call | solution.py:97
  85.2 0.9 %collective-permute-done.11.refs_5_ = bf16[256,256]{1,0:T(8,128)(2,1)S(1)} collective-permute-done((bf16[256,256]{1,0:T(8,128)(2,1)S(1)}, bf16[256,256]{1,0:T(8,128)(2,1)S(1)}, u32[]{:S(2)}, u32[]{:S(2)}) %collective-permute-start.11) | collective-permute-done | bytes 131104 | tf_op jit(solution)/shard_map/ppermute | solution.py:173
  86.1 1.7 %collective-permute-done.13.refs_7_ = bf16[256,256]{1,0:T(8,128)(2,1)S(1)} collective-permute-done((bf16[256,256]{1,0:T(8,128)(2,1)S(1)}, bf16[256,256]{1,0:T(8,128)(2,1)S(1)}, u32[]{:S(2)}, u32[]{:S(2)}) %collective-permute-start.13) | collective-permute-done | bytes 131104 | tf_op jit(solution)/shard_map/ppermute | solution.py:173
  87.8 1.4 %place_1.1 = bf16[2,512,256]{2,1,0:T(8,128)(2,1)} custom-call(s32[2,1,1]{2,1,0:T(1,128)S(1)} %copy.10.refs_0_, s32[2,1,1]{2,1,0:T(1,128)S(1)} %collective-permute-done.refs_1_, bf16[2,512,256]{2,1,0:T(8,128)(2,1)S(1)} %copy-done.2, bf16[2,256,256]{2,1,0:T(8,128)(2,1)S(1)} %get-tuple-element.13.refs_3_, ...), custom_call_target="tpu_custom_call", output_to_operand_aliasing={{}: (8, {})} | custom-call | flops 524288 | bytes 1048576 | tf_op jit(solution)/shard_map/place_1/pallas_call | solution.py:97
  (48 shorter events, 4.2 us)
Async XLA Ops:
  0.0 49.2 %copy-start.6 = (s32[2,1,1,4]{3,2,1,0:T(1,128)S(1)}, s32[2,1,1,4]{3,2,1,0:T(1,128)}, u32[]{:S(2)}) copy-start(s32[2,1,1,4]{3,2,1,0:T(1,128)} %refs_0_.9) | copy-start | bytes 100
  0.0 49.2 %copy-start.8 = (s32[2,1,4]{2,1,0:T(1,128)S(1)}, s32[2,1,4]{2,1,0:T(1,128)}, u32[]{:S(2)}) copy-start(s32[2,1,4]{2,1,0:T(1,128)} %refs_4_.7) | copy-start | bytes 100
  0.0 45.6 %copy-start.10 = (s32[2,1,1]{0,2,1:T(1,128)S(1)}, s32[2,1,1]{0,2,1:T(1,128)}, u32[]{:S(2)}) copy-start(s32[2,1,1]{0,2,1:T(1,128)} %param.8) | copy-start | bytes 28
  1.1 7.5 %collective-permute-start.14 = (bf16[256,512]{1,0:T(8,128)(2,1)S(1)}, bf16[256,512]{1,0:T(8,128)(2,1)S(1)}, u32[]{:S(2)}, u32[]{:S(2)}) collective-permute-start(bf16[256,512]{1,0:T(8,128)(2,1)S(1)} %get-tuple-element.23), channel_id=1, source_target_pairs={{0,0},{1,4},{2,8},{3,12},{4,1},{5,5},{6,9},{7,13},{8,2},{9,6},{10,... | collective-permute-start | bytes 786440 | tf_op jit(solution)/shard_map/ppermute | solution.py:134
  1.8 20.3 %collective-permute-start.4 = (bf16[256,512]{1,0:T(8,128)(2,1)S(1)}, bf16[256,512]{1,0:T(8,128)(2,1)S(1)}, u32[]{:S(2)}, u32[]{:S(2)}) collective-permute-start(bf16[256,512]{1,0:T(8,128)(2,1)S(1)} %get-tuple-element.24), channel_id=1, source_target_pairs={{0,2},{1,3},{2,0},{3,1},{4,6},{5,7},{6,4},{7,5},{8,10},{9,11},{10,... | collective-permute-start | bytes 786440 | tf_op jit(solution)/shard_map/ppermute | solution.py:128
  8.6 20.6 %collective-permute-start.16 = (bf16[256,512]{1,0:T(8,128)(2,1)S(1)}, bf16[256,512]{1,0:T(8,128)(2,1)S(1)}, u32[]{:S(2)}, u32[]{:S(2)}) collective-permute-start(bf16[256,512]{1,0:T(8,128)(2,1)S(1)} %collective-permute-done.14.refs_5_), channel_id=1, source_target_pairs={{0,2},{1,3},{2,0},{3,1},{4,6},{5,7},{6,4},{7,5},{8,10},{9,11},{10,... | collective-permute-start | bytes 786440 | tf_op jit(solution)/shard_map/ppermute | solution.py:139
  22.1 12.5 %collective-permute-start.5 = (bf16[256,512]{1,0:T(8,128)(2,1)S(1)}, bf16[256,512]{1,0:T(8,128)(2,1)S(1)}, u32[]{:S(2)}, u32[]{:S(2)}) collective-permute-start(bf16[256,512]{1,0:T(8,128)(2,1)S(1)} %collective-permute-done.4), channel_id=1, source_target_pairs={{2,0},{3,4},{0,8},{1,12},{6,1},{7,5},{4,9},{5,13},{10,2},{11,6},{8... | collective-permute-start | bytes 786440 | tf_op jit(solution)/shard_map/ppermute | solution.py:134
  22.2 17.3 %collective-permute-start.15 = (bf16[256,512]{1,0:T(8,128)(2,1)S(1)}, bf16[256,512]{1,0:T(8,128)(2,1)S(1)}, u32[]{:S(2)}, u32[]{:S(2)}) collective-permute-start(bf16[256,512]{1,0:T(8,128)(2,1)S(1)} %collective-permute-done.14.refs_5_), channel_id=1, source_target_pairs={{0,1},{1,0},{2,3},{3,2},{4,5},{5,4},{6,7},{7,6},{8,9},{9,8},{10,11... | collective-permute-start | bytes 786440 | tf_op jit(solution)/shard_map/ppermute | solution.py:139
  29.3 10.3 %collective-permute-start.17 = (bf16[256,512]{1,0:T(8,128)(2,1)S(1)}, bf16[256,512]{1,0:T(8,128)(2,1)S(1)}, u32[]{:S(2)}, u32[]{:S(2)}) collective-permute-start(bf16[256,512]{1,0:T(8,128)(2,1)S(1)} %collective-permute-done.16.refs_7_), channel_id=1, source_target_pairs={{0,1},{1,0},{2,3},{3,2},{4,5},{5,4},{6,7},{7,6},{8,9},{9,8},{10,11... | collective-permute-start | bytes 786440 | tf_op jit(solution)/shard_map/ppermute | solution.py:139
  29.3 4.7 %collective-permute-start.1 = (s32[2,1,1,4]{3,2,1,0:T(1,128)}, s32[2,1,1,4]{3,2,1,0:T(1,128)S(1)}, u32[]{:S(2)}, u32[]{:S(2)}) collective-permute-start(s32[2,1,1,4]{3,2,1,0:T(1,128)} %refs_0_.9), channel_id=1, source_target_pairs={{0,4},{4,0},{8,12},{12,8},{1,5},{5,1},{9,13},{13,9},{2,6},{6,2},{1... | collective-permute-start | bytes 104 | tf_op jit(solution)/shard_map/ppermute | solution.py:145
  32.2 4.7 %collective-permute-start.2 = (s32[2,1,1,4]{3,2,1,0:T(1,128)}, s32[2,1,1,4]{3,2,1,0:T(1,128)S(1)}, u32[]{:S(2)}, u32[]{:S(2)}) collective-permute-start(s32[2,1,1,4]{3,2,1,0:T(1,128)} %refs_0_.9), channel_id=1, source_target_pairs={{0,8},{4,12},{8,0},{12,4},{1,9},{5,13},{9,1},{13,5},{2,10},{6,14},... | collective-permute-start | bytes 104 | tf_op jit(solution)/shard_map/ppermute | solution.py:145
  34.0 5.6 %collective-permute-start.3 = (s32[2,1,1,4]{3,2,1,0:T(1,128)}, s32[2,1,1,4]{3,2,1,0:T(1,128)S(1)}, u32[]{:S(2)}, u32[]{:S(2)}) collective-permute-start(s32[2,1,1,4]{3,2,1,0:T(1,128)} %refs_0_.9), channel_id=1, source_target_pairs={{0,12},{4,8},{8,4},{12,0},{1,13},{5,9},{9,5},{13,1},{2,14},{6,10},... | collective-permute-start | bytes 104 | tf_op jit(solution)/shard_map/ppermute | solution.py:145
  34.6 14.4 %collective-permute-start.7 = (bf16[256,512]{1,0:T(8,128)(2,1)S(1)}, bf16[256,512]{1,0:T(8,128)(2,1)S(1)}, u32[]{:S(2)}, u32[]{:S(2)}) collective-permute-start(bf16[256,512]{1,0:T(8,128)(2,1)S(1)} %collective-permute-done.5.refs_5_), channel_id=1, source_target_pairs={{0,2},{1,3},{2,0},{3,1},{4,6},{5,7},{6,4},{7,5},{8,10},{9,11},{10,... | collective-permute-start | bytes 786440 | tf_op jit(solution)/shard_map/ppermute | solution.py:139
  39.6 1.6 %copy-start = (bf16[2,1,512,1024]{3,2,1,0:T(8,128)(2,1)S(1)}, bf16[2,1,512,1024]{3,2,1,0:T(8,128)(2,1)}, u32[]{:S(2)}) copy-start(bf16[2,1,512,1024]{3,2,1,0:T(8,128)(2,1)} %refs_9_.7) | copy-start | bytes 6291460
  42.5 2.1 %copy-start.3 = (bf16[256,512]{1,0:T(8,128)(2,1)}, bf16[256,512]{1,0:T(8,128)(2,1)S(1)}, u32[]{:S(2)}) copy-start(bf16[256,512]{1,0:T(8,128)(2,1)S(1)} %collective-permute-done.17.refs_8_) | copy-start | bytes 786436
  42.5 6.7 %copy-start.1 = (bf16[2,1,512,1024]{3,2,1,0:T(8,128)(2,1)S(1)}, bf16[2,1,512,1024]{3,2,1,0:T(8,128)(2,1)}, u32[]{:S(2)}) copy-start(bf16[2,1,512,1024]{3,2,1,0:T(8,128)(2,1)} %refs_9_.7) | copy-start | bytes 6291460
  44.6 0.7 copy-start.9
  45.3 8.7 %collective-permute-start.18 = (bf16[2,256,256]{2,1,0:T(8,128)(2,1)}, bf16[2,256,256]{2,1,0:T(8,128)(2,1)}, u32[]{:S(2)}, u32[]{:S(2)}) collective-permute-start(bf16[2,256,256]{2,1,0:T(8,128)(2,1)} %get-tuple-element.18), channel_id=1, source_target_pairs={{0,4},{4,0},{8,12},{12,8},{1,5},{5,1},{9,13},{13,9},{2,6},{6,2},{1... | collective-permute-start | bytes 786440 | tf_op jit(solution)/shard_map/ppermute | solution.py:167
  45.7 29.2 %collective-permute-start = (s32[2,1,1]{2,1,0:T(1,128)S(1)}, s32[2,1,1]{2,1,0:T(1,128)S(1)}, u32[]{:S(2)}, u32[]{:S(2)}) collective-permute-start(s32[2,1,1]{2,1,0:T(1,128)S(1)} %copy.10.refs_0_), channel_id=1, source_target_pairs={{0,16},{16,0},{1,17},{17,1},{2,18},{18,2},{3,19},{19,3},{4,20},{20... | collective-permute-start | bytes 32 | tf_op jit(solution)/shard_map/ppermute | solution.py:148
  47.2 10.2 %collective-permute-start.6 = (bf16[256,512]{1,0:T(8,128)(2,1)S(1)}, bf16[256,512]{1,0:T(8,128)(2,1)S(1)}, u32[]{:S(2)}, u32[]{:S(2)}) collective-permute-start(bf16[256,512]{1,0:T(8,128)(2,1)S(1)} %collective-permute-done.5.refs_5_), channel_id=1, source_target_pairs={{0,1},{1,0},{2,3},{3,2},{4,5},{5,4},{6,7},{7,6},{8,9},{9,8},{10,11... | collective-permute-start | bytes 786440 | tf_op jit(solution)/shard_map/ppermute | solution.py:139
  47.2 11.7 %collective-permute-start.19 = (bf16[2,256,256]{2,1,0:T(8,128)(2,1)}, bf16[2,256,256]{2,1,0:T(8,128)(2,1)S(1)}, u32[]{:S(2)}, u32[]{:S(2)}) collective-permute-start(bf16[2,256,256]{2,1,0:T(8,128)(2,1)} %copy-done.9), channel_id=1, source_target_pairs={{0,4},{4,0},{8,12},{12,8},{1,5},{5,1},{9,13},{13,9},{2,6},{6,2},{1... | collective-permute-start | bytes 786440 | tf_op jit(solution)/shard_map/ppermute | solution.py:167
  49.0 8.4 %collective-permute-start.8 = (bf16[256,512]{1,0:T(8,128)(2,1)S(1)}, bf16[256,512]{1,0:T(8,128)(2,1)S(1)}, u32[]{:S(2)}, u32[]{:S(2)}) collective-permute-start(bf16[256,512]{1,0:T(8,128)(2,1)S(1)} %collective-permute-done.7.refs_7_), channel_id=1, source_target_pairs={{0,1},{1,0},{2,3},{3,2},{4,5},{5,4},{6,7},{7,6},{8,9},{9,8},{10,11... | collective-permute-start | bytes 786440 | tf_op jit(solution)/shard_map/ppermute | solution.py:139
  49.2 1.0 %copy-start.4 = (bf16[256,512]{1,0:T(8,128)(2,1)S(1)}, bf16[256,512]{1,0:T(8,128)(2,1)}, u32[]{:S(2)}) copy-start(bf16[256,512]{1,0:T(8,128)(2,1)} %copy-done.3) | copy-start | bytes 786436
  55.0 20.0 %collective-permute-start.21 = (bf16[256,256]{1,0:T(8,128)(2,1)S(1)}, bf16[256,256]{1,0:T(8,128)(2,1)S(1)}, u32[]{:S(2)}, u32[]{:S(2)}) collective-permute-start(bf16[256,256]{1,0:T(8,128)(2,1)S(1)} %fusion.4), channel_id=1, source_target_pairs={{0,16},{16,0},{1,17},{17,1},{2,18},{18,2},{3,19},{19,3},{4,20},{20... | collective-permute-start | bytes 393224 | tf_op jit(solution)/shard_map/ppermute | solution.py:176
  58.8 10.3 %collective-permute-start.9 = (bf16[2,256,256]{2,1,0:T(8,128)(2,1)S(1)}, bf16[2,256,256]{2,1,0:T(8,128)(2,1)S(1)}, u32[]{:S(2)}, u32[]{:S(2)}) collective-permute-start(bf16[2,256,256]{2,1,0:T(8,128)(2,1)S(1)} %get-tuple-element.14), channel_id=1, source_target_pairs={{0,4},{4,0},{8,12},{12,8},{1,5},{5,1},{9,13},{13,9},{2,6},{6,2},{1... | collective-permute-start | bytes 786440 | tf_op jit(solution)/shard_map/ppermute | solution.py:167
  59.0 18.9 %collective-permute-start.20 = (bf16[256,256]{1,0:T(8,128)(2,1)S(1)}, bf16[256,256]{1,0:T(8,128)(2,1)S(1)}, u32[]{:S(2)}, u32[]{:S(2)}) collective-permute-start(bf16[256,256]{1,0:T(8,128)(2,1)S(1)} %get-tuple-element.22), channel_id=1, source_target_pairs={{0,8},{4,12},{8,0},{12,4},{16,24},{20,28},{24,16},{28,20},{1,9},{5... | collective-permute-start | bytes 393224 | tf_op jit(solution)/shard_map/ppermute | solution.py:173
  60.2 23.2 %copy-start.2 = (bf16[2,512,256]{2,1,0:T(8,128)(2,1)S(1)}, bf16[2,512,256]{2,1,0:T(8,128)(2,1)}, u32[]{:S(2)}) copy-start(bf16[2,512,256]{2,1,0:T(8,128)(2,1)} %refs_2_.3) | copy-start | bytes 1572868
  60.2 13.1 %collective-permute-start.10 = (bf16[2,256,256]{2,1,0:T(8,128)(2,1)S(1)}, bf16[2,256,256]{2,1,0:T(8,128)(2,1)S(1)}, u32[]{:S(2)}, u32[]{:S(2)}) collective-permute-start(bf16[2,256,256]{2,1,0:T(8,128)(2,1)S(1)} %get-tuple-element.16), channel_id=1, source_target_pairs={{0,4},{4,0},{8,12},{12,8},{1,5},{5,1},{9,13},{13,9},{2,6},{6,2},{1... | collective-permute-start | bytes 786440 | tf_op jit(solution)/shard_map/ppermute | solution.py:167
  69.1 14.3 %collective-permute-start.22 = (bf16[256,256]{1,0:T(8,128)(2,1)S(1)}, bf16[256,256]{1,0:T(8,128)(2,1)S(1)}, u32[]{:S(2)}, u32[]{:S(2)}) collective-permute-start(bf16[256,256]{1,0:T(8,128)(2,1)S(1)} %get-tuple-element.21), channel_id=1, source_target_pairs={{0,24},{4,28},{8,16},{12,20},{16,8},{20,12},{24,0},{28,4},{1,25},{... | collective-permute-start | bytes 393224 | tf_op jit(solution)/shard_map/ppermute | solution.py:173
  73.3 11.8 %collective-permute-start.12 = (bf16[256,256]{1,0:T(8,128)(2,1)S(1)}, bf16[256,256]{1,0:T(8,128)(2,1)S(1)}, u32[]{:S(2)}, u32[]{:S(2)}) collective-permute-start(bf16[256,256]{1,0:T(8,128)(2,1)S(1)} %fusion.1), channel_id=1, source_target_pairs={{0,16},{16,0},{1,17},{17,1},{2,18},{18,2},{3,19},{19,3},{4,20},{20... | collective-permute-start | bytes 393224 | tf_op jit(solution)/shard_map/ppermute | solution.py:176
  74.9 11.2 %collective-permute-start.11 = (bf16[256,256]{1,0:T(8,128)(2,1)S(1)}, bf16[256,256]{1,0:T(8,128)(2,1)S(1)}, u32[]{:S(2)}, u32[]{:S(2)}) collective-permute-start(bf16[256,256]{1,0:T(8,128)(2,1)S(1)} %get-tuple-element.26), channel_id=1, source_target_pairs={{0,8},{4,12},{8,0},{12,4},{16,24},{20,28},{24,16},{28,20},{1,9},{5... | collective-permute-start | bytes 393224 | tf_op jit(solution)/shard_map/ppermute | solution.py:173
  75.0 12.8 %collective-permute-start.13 = (bf16[256,256]{1,0:T(8,128)(2,1)S(1)}, bf16[256,256]{1,0:T(8,128)(2,1)S(1)}, u32[]{:S(2)}, u32[]{:S(2)}) collective-permute-start(bf16[256,256]{1,0:T(8,128)(2,1)S(1)} %get-tuple-element.25), channel_id=1, source_target_pairs={{0,24},{4,28},{8,16},{12,20},{16,8},{20,12},{24,0},{28,4},{1,25},{... | collective-permute-start | bytes 393224 | tf_op jit(solution)/shard_map/ppermute | solution.py:173
  (2 other events, 1.4 us)

commit v3 on v2

v3 whole, which is shorter than its diff:
```python
import functools

import jax
import jax.numpy as jnp
from jax import lax
from jax.experimental import pallas as pl
from jax.experimental.pallas import tpu as pltpu
from jax.sharding import PartitionSpec as P


def prepare_kernel(n_row, *refs):
    masks, colmap, panel = refs[:n_row], refs[n_row], refs[n_row + 1]
    picks, held, done = refs[n_row + 2 :]
    copy = pltpu.make_async_copy(panel, held, done)
    copy.start()
    g = lax.axis_index("gz")
    levels, _, count = colmap.shape
    layers = picks.shape[0] // (levels * n_row * count)
    at = 0
    for level in range(levels):
        for turn in range(n_row):
            for u in range(layers):
                for j in range(count):
                    pick = jnp.where(colmap[level, 0, j] == (g ^ u), masks[turn][level, 0, 0, j], 0)
                    picks[at] = pick.astype(jnp.float32)
                    at += 1
    copy.wait()


def prepare(masks, colmap, upanel, layers):
    n_row = len(masks)
    levels, _, count = colmap.shape
    smem = pl.BlockSpec(memory_space=pltpu.SMEM)
    return pl.pallas_call(
        functools.partial(prepare_kernel, n_row),
        in_specs=[smem] * (n_row + 1) + [pl.BlockSpec(memory_space=pl.ANY)],
        out_specs=[smem, pl.BlockSpec(memory_space=pl.ANY)],
        out_shape=[
            jax.ShapeDtypeStruct((levels * n_row * layers * count,), jnp.float32),
            jax.ShapeDtypeStruct(upanel.shape, upanel.dtype),
        ],
        scratch_shapes=[pltpu.SemaphoreType.DMA],
        compiler_params=pltpu.CompilerParams(vmem_limit_bytes=1 << 20),
        cost_estimate=pl.CostEstimate(flops=1 << 20, bytes_accessed=4 * upanel.size, transcendentals=0),
        name="prepare",
    )(*masks, colmap, upanel)


def product_kernel(level, turns, n_row, n_col, layers, picks, *refs):
    folds = n_row // n_col
    lefts, right, outs, held = refs[:n_row], refs[n_row], list(refs[n_row + 1 : -1]), refs[-1]
    z, c = lax.axis_index("row"), lax.axis_index("col")
    for slot, left in enumerate(lefts):
        held[slot] = left[...]
    width = outs[0].shape[-1]
    count = right.shape[3] // width
    for turn, whole in turns:
        parts = [outs[0].at[u] for u in range(layers)] if whole else outs[:layers]
        del outs[: 1 if whole else layers]
        a = z ^ turn
        slot = (c ^ (a % n_col)) * folds + ((z % folds) ^ (a // n_col))
        tile = jnp.dot(held[slot], right[0, 0], preferred_element_type=jnp.float32)
        for u in range(layers):
            total = None
            for j in range(count):
                pick = picks[((level * n_row + turn) * layers + u) * count + j]
                term = pick * tile[:, j * width : (j + 1) * width]
                total = term if total is None else total + term
            parts[u][...] = total.astype(jnp.bfloat16)


def products(level, turns, picks, lefts, upanel, layers, n_col):
    n_row = len(lefts)
    rows, depth = lefts[0].shape
    columns = upanel.shape[3]
    whole = pl.BlockSpec(memory_space=pltpu.VMEM)
    room = 4 * (2 * n_row * rows * depth + depth * columns + 2 * len(turns) * layers * rows * rows) + (4 << 20)
    shapes = []
    for _, joint in turns:
        shapes += [(layers, rows, rows)] if joint else [(rows, rows)] * layers
    call = pl.pallas_call(
        functools.partial(product_kernel, level, turns, n_row, n_col, layers),
        grid=(1,),
        in_specs=[pl.BlockSpec(memory_space=pltpu.SMEM)]
        + [whole] * n_row
        + [pl.BlockSpec((1, 1, depth, columns), lambda i: (level, 0, 0, 0))],
        out_specs=[whole] * len(shapes),
        out_shape=[jax.ShapeDtypeStruct(shape, jnp.bfloat16) for shape in shapes],
        scratch_shapes=[pltpu.VMEM((n_row, rows, depth), jnp.bfloat16)],
        compiler_params=pltpu.CompilerParams(vmem_limit_bytes=room),
        cost_estimate=pl.CostEstimate(
            flops=2 * len(turns) * rows * depth * columns,
            bytes_accessed=2 * (n_row * rows * depth + depth * columns + len(turns) * layers * rows * rows),
            transcendentals=0,
        ),
    )
    made = list(call(picks, *lefts, upanel))
    results = []
    for _, joint in turns:
        results.append(made.pop(0) if joint else [made.pop(0) for _ in range(layers)])
    return results


def place_kernel(level, layers, counts, *refs):
    maps, front, out = refs[:layers], refs[layers], refs[-1]
    blocks = list(refs[layers + 1 : layers + 1 + sum(counts)])
    width = out.shape[2]
    totals = []
    for n in counts:
        total = None
        for _ in range(n):
            ref = blocks.pop(0)
            term = ref[...].astype(jnp.float32)
            total = term if total is None else total + term
        totals.append(total)
    for f in range(out.shape[1] // width):
        span = slice(f * width, (f + 1) * width)
        moved = None
        for u in range(layers):
            here = (maps[u][level, 0, 0] == f).astype(jnp.float32)
            moved = here * totals[u] if moved is None else moved + here * totals[u]
        out[0, span] = (front[0, span].astype(jnp.float32) - moved).astype(out.dtype)


def place(level, maps, front, groups, before):
    layers = len(groups)
    counts = tuple(len(group) for group in groups)
    _, height, width = front.shape
    specs = [pl.BlockSpec(memory_space=pltpu.SMEM)] * layers
    specs.append(pl.BlockSpec((1, height, width), lambda i: (level, 0, 0)))
    blocks = [block for group in groups for block in group]
    specs += [pl.BlockSpec(memory_space=pltpu.VMEM)] * len(blocks)
    args = [*maps, front, *blocks]
    aliases = {}
    if before is not None:
        aliases = {len(args): 0}
        args.append(before)
        specs.append(pl.BlockSpec(memory_space=pl.ANY))
    return pl.pallas_call(
        functools.partial(place_kernel, level, layers, counts),
        grid=(1,),
        in_specs=specs,
        out_specs=pl.BlockSpec((1, height, width), lambda i: (level, 0, 0)),
        out_shape=jax.ShapeDtypeStruct(front.shape, front.dtype),
        input_output_aliases=aliases,
        compiler_params=pltpu.CompilerParams(vmem_limit_bytes=32 * height * width + (2 << 20)),
        cost_estimate=pl.CostEstimate(
            flops=2 * layers * height * width, bytes_accessed=8 * height * width, transcendentals=0
        ),
    )(*args)


def on_device(lpanel, upanel, rowmap, colmap, blockmask, front_blocks):
    layers, n_row, n_col = (lax.axis_size(name) for name in ("gz", "row", "col"))
    levels = lpanel.shape[0]
    depth = upanel.shape[2]
    folds = n_row // n_col
    row = lax.axis_index("row")

    masks = [blockmask]
    for turn in range(1, n_row):
        masks.append(lax.ppermute(blockmask, "row", [(z, z ^ turn) for z in range(n_row)]))
    maps = [rowmap]
    for u in range(1, layers):
        maps.append(lax.ppermute(rowmap, "gz", [(g, g ^ u) for g in range(layers)]))

    lefts = []
    for level in range(levels):
        pieces = {}
        for turn in range(folds):
            part = lpanel[level, 0]
            if folds > 1:
                part = lax.dynamic_slice_in_dim(part, ((row // n_col) ^ turn) * depth, depth, 1)
            hop = (level % 2) * (n_col // 2)
            if hop:
                part = lax.ppermute(part, "col", [(k, k ^ hop) for k in range(n_col)])
            pairs = []
            for a in range(n_row):
                for k in range(n_col):
                    target = k * folds + ((a // n_col) ^ turn)
                    pairs.append((a * n_col + (k ^ hop), target * n_col + a % n_col))
            pieces[0, turn] = lax.ppermute(part, ("row", "col"), pairs)
        step = n_col // 2
        while step >= 1:
            swap = [(k, k ^ step) for k in range(n_col)]
            for (flip, turn), piece in list(pieces.items()):
                pieces[flip ^ step, turn] = lax.ppermute(piece, "col", swap)
            step //= 2
        lefts.append([pieces[flip, turn] for flip in range(n_col) for turn in range(folds)])
    picks, held = prepare(masks, colmap, upanel, layers)

    def total(blocks):
        if len(blocks) == 1:
            return blocks[0]
        return sum(block.astype(jnp.float32) for block in blocks).astype(jnp.bfloat16)

    result = None
    half = n_row // 2
    away = [(turn, turn & (turn - 1) != 0) for turn in reversed(range(n_row)) if turn % 2]
    stay = [(turn, turn & (turn - 1) != 0 or turn == half) for turn in reversed(range(n_row)) if not turn % 2]
    stay[-1] = (0, False)
    ends = [(g, z) for g in range(layers) for z in range(n_row)]
    for level in range(levels):
        terms = {}
        for turns in (away, stay):
            made = products(level, turns, picks, lefts[level], held, layers, n_col)
            terms.update({turn: [block] for (turn, _), block in zip(turns, made)})
        groups = [[block] for block in terms.pop(0)[0]]
        for u in range(1, layers):
            swap = [(g, g ^ u) for g in range(layers)]
            groups[u] = [lax.ppermute(groups[u][0], "gz", swap)]
        bit = 1
        while bit < n_row:
            swap = [(z, z ^ bit) for z in range(n_row)]
            for turn in reversed(range(0, n_row, bit)):
                if turn & bit and turn != bit:
                    terms[turn ^ bit].append(lax.ppermute(total(terms.pop(turn)), "row", swap))
            last = terms.pop(bit)
            for u in range(layers):
                block = total([term[u] for term in last])
                pairs = [(g * n_row + z, (g ^ u) * n_row + (z ^ bit)) for g, z in ends]
                groups[u].append(lax.ppermute(block, ("gz", "row"), pairs))
            bit *= 2
        result = place(level, maps, front_blocks, groups, result)
    return result


def solution(mesh):
    return jax.shard_map(
        on_device,
        mesh=mesh,
        in_specs=(
            P(None, "gz", "row", "col"),
            P(None, "gz", "row", "col"),
            P(None, "gz", "row"),
            P(None, "gz", "col"),
            P(None, "gz", "row", "col"),
            P(None, "row", ("gz", "col")),
        ),
        out_specs=P(None, "row", ("gz", "col")),
        check_vma=False,
    )
```

time: 89.5 us -> 94.9 us (1.060)
  starting transfers between devices: 40 us -> 43.5 us
  local copies, waits for them, and re-layouts: 5.82 us -> 7.37 us
  Pallas kernels: 9.61 us -> 11.1 us
  waiting for transfers between devices: 32.5 us -> 31.4 us
    ppermute x4 -> x2, waiting for transfers between devices: 12.4 us -> 1.58 us  [on_device(): terms[turn ^ bit].append(lax.ppermute(total(terms.pop(turn)), 'row', swap))]
    ppermute x1, waiting for transfers between devices: 0.01 us -> 5.63 us  [on_device(): part = lax.ppermute(part, 'col', [(k, k ^ hop) for k in range(n_col)])]
    ppermute x2, starting transfers between devices: 0.77 us -> 5.42 us  [on_device(): pieces[0, turn] = lax.ppermute(part, ('row', 'col'), pairs)]
    ppermute x1, starting transfers between devices: 6.82 us -> 3.03 us  [on_device(): part = lax.ppermute(part, 'col', [(k, k ^ hop) for k in range(n_col)])]
    ppermute x6 -> x10, waiting for transfers between devices: 8.13 us -> 11.7 us  [the longest x8 11.7 us: on_device(): groups[u].append(lax.ppermute(block, ('gz', 'row'), pairs))]
    ppermute x6 -> x10, starting transfers between devices: 8.81 us -> 12.3 us  [the longest x8 9.29 us: on_device(): groups[u].append(lax.ppermute(block, ('gz', 'row'), pairs))]
    ppermute x3, starting transfers between devices: 3.54 us -> 6.77 us  [on_device(): lax.ppermute(blockmask, 'row', [(z, z ^ turn) for z in range(n_row)])]
    ppermute x6, starting transfers between devices: 15.5 us -> 12.4 us  [on_device(): pieces[flip ^ step, turn] = lax.ppermute(piece, 'col', swap)]
  transfers between devices with their start and end apart: 23 -> 25, of which waited for: 10 -> 11; matrix products, arithmetic and copies ran while one was open for 1% -> 1% of each run, Pallas kernels for 9% -> 10%
where the time goes in v3:
time: 94.9 us; the launch traced here: 94.6 us
  starting transfers between devices  43.5 us (46%)
  waiting for transfers between devices  31.4 us (33%)
  Pallas kernels  11.1 us (12%)
  local copies, waits for them, and re-layouts  7.37 us (8%)
  other arithmetic  1.11 us (1%)
    ppermute x6, starting transfers between devices, on_device(): pieces[flip ^ step, turn] = lax.ppermute(piece, 'col', swap)  12.4 us
    ppermute x8, waiting for transfers between devices, on_device(): groups[u].append(lax.ppermute(block, ('gz', 'row'), pairs))  11.7 us
    ppermute x8, starting transfers between devices, on_device(): groups[u].append(lax.ppermute(block, ('gz', 'row'), pairs))  9.29 us
    ppermute x3, waiting for transfers between devices, on_device(): lax.ppermute(blockmask, 'row', [(z, z ^ turn) for z in range(n_row)])  7.28 us
    ppermute x3, starting transfers between devices, on_device(): lax.ppermute(blockmask, 'row', [(z, z ^ turn) for z in range(n_row)])  6.77 us
    pallas_call x4, Pallas kernels, products(): made = list(call(picks, *lefts, upanel))  6.72 us
    unnamed x21, local copies, waits for them, and re-layouts  6.31 us
    ppermute x1, waiting for transfers between devices, on_device(): part = lax.ppermute(part, 'col', [(k, k ^ hop) for k in range(n_col)])  5.63 us
  transfers between devices with their start and end apart: 25, of which 11 were waited for; matrix products, arithmetic and copies ran while one was open for 1% of the time, Pallas kernels for 10%

profile of v3, /device:TPU:0, one launch (start us, length us, event | category | flops | bytes accessed | tf_op | source)
XLA Modules:
  0.0 94.6 jit_solution(5402320470475897469)
XLA Ops:
  1.1 3.0 %collective-permute-start.4 = (bf16[256,512]{1,0:T(8,128)(2,1)S(1)}, bf16[256,512]{1,0:T(8,128)(2,1)S(1)}, u32[]{:S(2)}, u32[]{:S(2)}) collective-permute-start(bf16[256,512]{1,0:T(8,128)(2,1)S(1)} %get-tuple-element.36), channel_id=1, source_target_pairs={{0,2},{1,3},{2,0},{3,1},{4,6},{5,7},{6,4},{7,5},{8,10},{9,11},{10,... | collective-permute-start | bytes 786440 | tf_op jit(solution)/shard_map/ppermute | solution.py:176
  4.8 5.6 %collective-permute-done.4 = bf16[256,512]{1,0:T(8,128)(2,1)S(1)} collective-permute-done((bf16[256,512]{1,0:T(8,128)(2,1)S(1)}, bf16[256,512]{1,0:T(8,128)(2,1)S(1)}, u32[]{:S(2)}, u32[]{:S(2)}) %collective-permute-start.4) | collective-permute-done | bytes 262176 | tf_op jit(solution)/shard_map/ppermute | solution.py:176
  10.4 4.8 %collective-permute-start.5 = (bf16[256,512]{1,0:T(8,128)(2,1)S(1)}, bf16[256,512]{1,0:T(8,128)(2,1)S(1)}, u32[]{:S(2)}, u32[]{:S(2)}) collective-permute-start(bf16[256,512]{1,0:T(8,128)(2,1)S(1)} %collective-permute-done.4), channel_id=1, source_target_pairs={{2,0},{3,4},{0,8},{1,12},{6,1},{7,5},{4,9},{5,13},{10,2},{11,6},{8... | collective-permute-start | bytes 786440 | tf_op jit(solution)/shard_map/ppermute | solution.py:182
  15.2 7.6 %collective-permute-start.17 = (bf16[256,512]{1,0:T(8,128)(2,1)S(1)}, bf16[256,512]{1,0:T(8,128)(2,1)S(1)}, u32[]{:S(2)}, u32[]{:S(2)}) collective-permute-start(bf16[256,512]{1,0:T(8,128)(2,1)S(1)} %collective-permute-done.15.refs_0_), channel_id=1, source_target_pairs={{0,2},{1,3},{2,0},{3,1},{4,6},{5,7},{6,4},{7,5},{8,10},{9,11},{10,... | collective-permute-start | bytes 786440 | tf_op jit(solution)/shard_map/ppermute | solution.py:187
  22.8 4.3 %collective-permute-start.7 = (bf16[256,512]{1,0:T(8,128)(2,1)S(1)}, bf16[256,512]{1,0:T(8,128)(2,1)S(1)}, u32[]{:S(2)}, u32[]{:S(2)}) collective-permute-start(bf16[256,512]{1,0:T(8,128)(2,1)S(1)} %collective-permute-done.5.refs_0_), channel_id=1, source_target_pairs={{0,2},{1,3},{2,0},{3,1},{4,6},{5,7},{6,4},{7,5},{8,10},{9,11},{10,... | collective-permute-start | bytes 786440 | tf_op jit(solution)/shard_map/ppermute | solution.py:187
  27.1 1.9 %collective-permute-done.17.refs_2_ = bf16[256,512]{1,0:T(8,128)(2,1)S(1)} collective-permute-done((bf16[256,512]{1,0:T(8,128)(2,1)S(1)}, bf16[256,512]{1,0:T(8,128)(2,1)S(1)}, u32[]{:S(2)}, u32[]{:S(2)}) %collective-permute-start.17) | collective-permute-done | bytes 262176 | tf_op jit(solution)/shard_map/ppermute | solution.py:187
  29.5 3.3 %collective-permute-done.7.refs_2_ = bf16[256,512]{1,0:T(8,128)(2,1)S(1)} collective-permute-done((bf16[256,512]{1,0:T(8,128)(2,1)S(1)}, bf16[256,512]{1,0:T(8,128)(2,1)S(1)}, u32[]{:S(2)}, u32[]{:S(2)}) %collective-permute-start.7) | collective-permute-done | bytes 262176 | tf_op jit(solution)/shard_map/ppermute | solution.py:187
  32.8 1.5 %collective-permute-start.1 = (s32[2,1,1,4]{3,2,1,0:T(1,128)}, s32[2,1,1,4]{3,2,1,0:T(1,128)S(1)}, u32[]{:S(2)}, u32[]{:S(2)}) collective-permute-start(s32[2,1,1,4]{3,2,1,0:T(1,128)} %refs_0_.3), channel_id=1, source_target_pairs={{0,4},{4,0},{8,12},{12,8},{1,5},{5,1},{9,13},{13,9},{2,6},{6,2},{1... | collective-permute-start | bytes 104 | tf_op jit(solution)/shard_map/ppermute | solution.py:162
  34.3 2.3 %collective-permute-done.1.refs_1_ = s32[2,1,1,4]{3,2,1,0:T(1,128)S(1)} collective-permute-done((s32[2,1,1,4]{3,2,1,0:T(1,128)}, s32[2,1,1,4]{3,2,1,0:T(1,128)S(1)}, u32[]{:S(2)}, u32[]{:S(2)}) %collective-permute-start.1) | collective-permute-done | bytes 64 | tf_op jit(solution)/shard_map/ppermute | solution.py:162
  36.5 2.6 %collective-permute-start.2 = (s32[2,1,1,4]{3,2,1,0:T(1,128)}, s32[2,1,1,4]{3,2,1,0:T(1,128)S(1)}, u32[]{:S(2)}, u32[]{:S(2)}) collective-permute-start(s32[2,1,1,4]{3,2,1,0:T(1,128)} %refs_0_.3), channel_id=1, source_target_pairs={{0,8},{4,12},{8,0},{12,4},{1,9},{5,13},{9,1},{13,5},{2,10},{6,14},... | collective-permute-start | bytes 104 | tf_op jit(solution)/shard_map/ppermute | solution.py:162
  39.2 2.1 %collective-permute-done.2.refs_2_ = s32[2,1,1,4]{3,2,1,0:T(1,128)S(1)} collective-permute-done((s32[2,1,1,4]{3,2,1,0:T(1,128)}, s32[2,1,1,4]{3,2,1,0:T(1,128)S(1)}, u32[]{:S(2)}, u32[]{:S(2)}) %collective-permute-start.2) | collective-permute-done | bytes 64 | tf_op jit(solution)/shard_map/ppermute | solution.py:162
  41.2 2.6 %collective-permute-start.3 = (s32[2,1,1,4]{3,2,1,0:T(1,128)}, s32[2,1,1,4]{3,2,1,0:T(1,128)S(1)}, u32[]{:S(2)}, u32[]{:S(2)}) collective-permute-start(s32[2,1,1,4]{3,2,1,0:T(1,128)} %refs_0_.3), channel_id=1, source_target_pairs={{0,12},{4,8},{8,4},{12,0},{1,13},{5,9},{9,5},{13,1},{2,14},{6,10},... | collective-permute-start | bytes 104 | tf_op jit(solution)/shard_map/ppermute | solution.py:162
  43.9 3.0 %collective-permute-done.3.refs_3_ = s32[2,1,1,4]{3,2,1,0:T(1,128)S(1)} collective-permute-done((s32[2,1,1,4]{3,2,1,0:T(1,128)}, s32[2,1,1,4]{3,2,1,0:T(1,128)S(1)}, u32[]{:S(2)}, u32[]{:S(2)}) %collective-permute-start.3) | collective-permute-done | bytes 64 | tf_op jit(solution)/shard_map/ppermute | solution.py:162
  46.8 1.6 %copy-done = bf16[2,1,512,1024]{3,2,1,0:T(8,128)(2,1)S(1)} copy-done((bf16[2,1,512,1024]{3,2,1,0:T(8,128)(2,1)S(1)}, bf16[2,1,512,1024]{3,2,1,0:T(8,128)(2,1)}, u32[]{:S(2)}) %copy-start) | copy-done | bytes 2097176
  49.8 1.4 %prepare.1 = (f32[64]{0:T(128)S(1)}, bf16[2,1,512,1024]{3,2,1,0:T(8,128)(2,1)S(1)}) custom-call(s32[2,1,1,4]{3,2,1,0:T(1,128)S(1)} %copy-done.6, s32[2,1,1,4]{3,2,1,0:T(1,128)S(1)} %collective-permute-done.1.refs_1_, s32[2,1,1,4]{3,2,1,0:T(1,128)S(1)} %collective-permute-done.2.refs_2_, s32[2,1,1,4]{3,2,1,0:T(1,128)S(1)} %collective-permute-done.3.refs_3_, ...), custom_call_target="tpu_custom_call" | custom-call | flops 1048576 | bytes 4194304 | tf_op jit(solution)/shard_map/prepare/pallas_call | solution.py:34
  51.3 1.8 %shard_map.67 = (bf16[2,256,256]{2,1,0:T(8,128)(2,1)}, bf16[256,256]{1,0:T(8,128)(2,1)S(1)}, bf16[256,256]{1,0:T(8,128)(2,1)S(1)}) custom-call(f32[64]{0:T(128)S(1)} %get-tuple-element.19.picks, bf16[256,512]{1,0:T(8,128)(2,1)S(1)} %collective-permute-done.15.refs_0_, bf16[256,512]{1,0:T(8,128)(2,1)S(1)} %collective-permute-done.16.refs_1_, ...), custom_call_target="tpu_custom_call" | custom-call | flops 536870912 | bytes 2621440 | tf_op jit(solution)/shard_map/pallas_call | solution.py:97
  54.5 1.5 %collective-permute-start = (s32[2,1,1]{2,1,0:T(1,128)S(1)}, s32[2,1,1]{2,1,0:T(1,128)S(1)}, u32[]{:S(2)}, u32[]{:S(2)}) collective-permute-start(s32[2,1,1]{2,1,0:T(1,128)S(1)} %copy.10.refs_0_), channel_id=1, source_target_pairs={{0,16},{16,0},{1,17},{17,1},{2,18},{18,2},{3,19},{19,3},{4,20},{20... | collective-permute-start | bytes 32 | tf_op jit(solution)/shard_map/ppermute | solution.py:165
  56.0 2.0 %collective-permute-start.19 = (bf16[256,256]{1,0:T(8,128)(2,1)}, bf16[256,256]{1,0:T(8,128)(2,1)S(1)}, u32[]{:S(2)}, u32[]{:S(2)}) collective-permute-start(bf16[256,256]{1,0:T(8,128)(2,1)} %copy-done.8), channel_id=1, source_target_pairs={{0,4},{4,0},{8,12},{12,8},{16,20},{20,16},{24,28},{28,24},{1,5},{5... | collective-permute-start | bytes 393224 | tf_op jit(solution)/shard_map/ppermute | solution.py:222
  60.0 1.4 %shard_map.66 = (bf16[2,256,256]{2,1,0:T(8,128)(2,1)S(1)}, bf16[256,256]{1,0:T(8,128)(2,1)S(1)}, bf16[256,256]{1,0:T(8,128)(2,1)S(1)}) custom-call(f32[64]{0:T(128)S(1)} %get-tuple-element.19.picks, bf16[256,512]{1,0:T(8,128)(2,1)S(1)} %collective-permute-done.15.refs_0_, bf16[256,512]{1,0:T(8,128)(2,1)S(1)} %copy-done.3, ...), custom_call_target="tpu_custom_call" | custom-call | flops 536870912 | bytes 2621440 | tf_op jit(solution)/shard_map/pallas_call | solution.py:97
  61.4 1.8 %shard_map.65 = (bf16[2,256,256]{2,1,0:T(8,128)(2,1)S(1)}, bf16[256,256]{1,0:T(8,128)(2,1)S(1)}, bf16[256,256]{1,0:T(8,128)(2,1)S(1)}) custom-call(f32[64]{0:T(128)S(1)} %get-tuple-element.19.picks, bf16[256,512]{1,0:T(8,128)(2,1)S(1)} %collective-permute-done.5.refs_0_, bf16[256,512]{1,0:T(8,128)(2,1)S(1)} %collective-permute-done.6.refs_1_, ...), custom_call_target="tpu_custom_call" | custom-call | flops 536870912 | bytes 2621440 | tf_op jit(solution)/shard_map/pallas_call | solution.py:97
  63.2 2.0 %collective-permute-start.10 = (bf16[2,256,256]{2,1,0:T(8,128)(2,1)S(1)}, bf16[2,256,256]{2,1,0:T(8,128)(2,1)S(1)}, u32[]{:S(2)}, u32[]{:S(2)}) collective-permute-start(bf16[2,256,256]{2,1,0:T(8,128)(2,1)S(1)} %get-tuple-element.24), channel_id=1, source_target_pairs={{0,4},{4,0},{8,12},{12,8},{1,5},{5,1},{9,13},{13,9},{2,6},{6,2},{1... | collective-permute-start | bytes 786440 | tf_op jit(solution)/shard_map/ppermute | solution.py:217
  65.2 1.8 %shard_map.64 = (bf16[2,256,256]{2,1,0:T(8,128)(2,1)S(1)}, bf16[256,256]{1,0:T(8,128)(2,1)S(1)}, bf16[256,256]{1,0:T(8,128)(2,1)S(1)}) custom-call(f32[64]{0:T(128)S(1)} %get-tuple-element.19.picks, bf16[256,512]{1,0:T(8,128)(2,1)S(1)} %collective-permute-done.5.refs_0_, bf16[256,512]{1,0:T(8,128)(2,1)S(1)} %collective-permute-done.6.refs_1_, ...), custom_call_target="tpu_custom_call" | custom-call | flops 536870912 | bytes 2621440 | tf_op jit(solution)/shard_map/pallas_call | solution.py:97
  67.0 1.6 %collective-permute-start.22 = (bf16[256,256]{1,0:T(8,128)(2,1)S(1)}, bf16[256,256]{1,0:T(8,128)(2,1)S(1)}, u32[]{:S(2)}, u32[]{:S(2)}) collective-permute-start(bf16[256,256]{1,0:T(8,128)(2,1)S(1)} %get-tuple-element.31), channel_id=1, source_target_pairs={{0,16},{16,0},{1,17},{17,1},{2,18},{18,2},{3,19},{19,3},{4,20},{20... | collective-permute-start | bytes 393224 | tf_op jit(solution)/shard_map/ppermute | solution.py:211
  71.0 1.6 %collective-permute-done.10 = bf16[2,256,256]{2,1,0:T(8,128)(2,1)S(1)} collective-permute-done((bf16[2,256,256]{2,1,0:T(8,128)(2,1)S(1)}, bf16[2,256,256]{2,1,0:T(8,128)(2,1)S(1)}, u32[]{:S(2)}, u32[]{:S(2)}) %collective-permute-start.10) | collective-permute-done | bytes 262176 | tf_op jit(solution)/shard_map/ppermute | solution.py:217
  72.5 2.1 %collective-permute-start.24 = (bf16[256,256]{1,0:T(8,128)(2,1)S(1)}, bf16[256,256]{1,0:T(8,128)(2,1)S(1)}, u32[]{:S(2)}, u32[]{:S(2)}) collective-permute-start(bf16[256,256]{1,0:T(8,128)(2,1)S(1)} %get-tuple-element.33), channel_id=1, source_target_pairs={{0,24},{4,28},{8,16},{12,20},{16,8},{20,12},{24,0},{28,4},{1,25},{... | collective-permute-start | bytes 393224 | tf_op jit(solution)/shard_map/ppermute | solution.py:222
  74.7 1.8 %collective-permute-start.13 = (bf16[256,256]{1,0:T(8,128)(2,1)S(1)}, bf16[256,256]{1,0:T(8,128)(2,1)S(1)}, u32[]{:S(2)}, u32[]{:S(2)}) collective-permute-start(bf16[256,256]{1,0:T(8,128)(2,1)S(1)} %get-tuple-element.26), channel_id=1, source_target_pairs={{0,20},{4,16},{8,28},{12,24},{16,4},{20,0},{24,12},{28,8},{1,21},{... | collective-permute-start | bytes 393224 | tf_op jit(solution)/shard_map/ppermute | solution.py:222
  77.5 1.4 %collective-permute-start.12 = (bf16[256,256]{1,0:T(8,128)(2,1)S(1)}, bf16[256,256]{1,0:T(8,128)(2,1)S(1)}, u32[]{:S(2)}, u32[]{:S(2)}) collective-permute-start(bf16[256,256]{1,0:T(8,128)(2,1)S(1)} %get-tuple-element.25), channel_id=1, source_target_pairs={{0,16},{16,0},{1,17},{17,1},{2,18},{18,2},{3,19},{19,3},{4,20},{20... | collective-permute-start | bytes 393224 | tf_op jit(solution)/shard_map/ppermute | solution.py:211
  81.1 5.2 %collective-permute-done.24.refs_8_ = bf16[256,256]{1,0:T(8,128)(2,1)S(1)} collective-permute-done((bf16[256,256]{1,0:T(8,128)(2,1)S(1)}, bf16[256,256]{1,0:T(8,128)(2,1)S(1)}, u32[]{:S(2)}, u32[]{:S(2)}) %collective-permute-start.24) | collective-permute-done | bytes 131104 | tf_op jit(solution)/shard_map/ppermute | solution.py:222
  86.3 1.5 %shard_map.68.refs_9_ = bf16[2,512,256]{2,1,0:T(8,128)(2,1)} custom-call(s32[2,1,1]{2,1,0:T(1,128)S(1)} %copy.10.refs_0_, s32[2,1,1]{2,1,0:T(1,128)S(1)} %collective-permute-done.refs_1_, bf16[2,512,256]{2,1,0:T(8,128)(2,1)S(1)} %copy-done.1, bf16[256,256]{1,0:T(8,128)(2,1)S(1)} %get-tuple-element.27.refs_3_, ...), custom_call_target="tpu_custom_call" | custom-call | flops 524288 | bytes 1048576 | tf_op jit(solution)/shard_map/pallas_call | solution.py:139
  87.8 3.8 %collective-permute-done.11.refs_5_ = bf16[256,256]{1,0:T(8,128)(2,1)S(1)} collective-permute-done((bf16[256,256]{1,0:T(8,128)(2,1)S(1)}, bf16[256,256]{1,0:T(8,128)(2,1)S(1)}, u32[]{:S(2)}, u32[]{:S(2)}) %collective-permute-start.11) | collective-permute-done | bytes 131104 | tf_op jit(solution)/shard_map/ppermute | solution.py:222
  91.6 1.6 %collective-permute-done.14.refs_8_ = bf16[256,256]{1,0:T(8,128)(2,1)S(1)} collective-permute-done((bf16[256,256]{1,0:T(8,128)(2,1)S(1)}, bf16[256,256]{1,0:T(8,128)(2,1)S(1)}, u32[]{:S(2)}, u32[]{:S(2)}) %collective-permute-start.14) | collective-permute-done | bytes 131104 | tf_op jit(solution)/shard_map/ppermute | solution.py:222
  93.1 1.5 %shard_map.69 = bf16[2,512,256]{2,1,0:T(8,128)(2,1)} custom-call(s32[2,1,1]{2,1,0:T(1,128)S(1)} %copy.10.refs_0_, s32[2,1,1]{2,1,0:T(1,128)S(1)} %collective-permute-done.refs_1_, bf16[2,512,256]{2,1,0:T(8,128)(2,1)S(1)} %copy-done.1, bf16[256,256]{1,0:T(8,128)(2,1)S(1)} %get-tuple-element.21.refs_3_, ...), custom_call_target="tpu_custom_call", output_to_operand_aliasing={{}: (9, {})} | custom-call | flops 524288 | bytes 1048576 | tf_op jit(solution)/shard_map/pallas_call | solution.py:139
  (49 shorter events, 12.7 us)
Async XLA Ops:
  1.1 9.3 %collective-permute-start.4 = (bf16[256,512]{1,0:T(8,128)(2,1)S(1)}, bf16[256,512]{1,0:T(8,128)(2,1)S(1)}, u32[]{:S(2)}, u32[]{:S(2)}) collective-permute-start(bf16[256,512]{1,0:T(8,128)(2,1)S(1)} %get-tuple-element.36), channel_id=1, source_target_pairs={{0,2},{1,3},{2,0},{3,1},{4,6},{5,7},{6,4},{7,5},{8,10},{9,11},{10,... | collective-permute-start | bytes 786440 | tf_op jit(solution)/shard_map/ppermute | solution.py:176
  4.1 11.1 %collective-permute-start.15 = (bf16[256,512]{1,0:T(8,128)(2,1)S(1)}, bf16[256,512]{1,0:T(8,128)(2,1)S(1)}, u32[]{:S(2)}, u32[]{:S(2)}) collective-permute-start(bf16[256,512]{1,0:T(8,128)(2,1)S(1)} %get-tuple-element.35), channel_id=1, source_target_pairs={{0,0},{1,4},{2,8},{3,12},{4,1},{5,5},{6,9},{7,13},{8,2},{9,6},{10,... | collective-permute-start | bytes 786440 | tf_op jit(solution)/shard_map/ppermute | solution.py:182
  10.4 12.4 %collective-permute-start.5 = (bf16[256,512]{1,0:T(8,128)(2,1)S(1)}, bf16[256,512]{1,0:T(8,128)(2,1)S(1)}, u32[]{:S(2)}, u32[]{:S(2)}) collective-permute-start(bf16[256,512]{1,0:T(8,128)(2,1)S(1)} %collective-permute-done.4), channel_id=1, source_target_pairs={{2,0},{3,4},{0,8},{1,12},{6,1},{7,5},{4,9},{5,13},{10,2},{11,6},{8... | collective-permute-start | bytes 786440 | tf_op jit(solution)/shard_map/ppermute | solution.py:182
  15.2 13.8 %collective-permute-start.17 = (bf16[256,512]{1,0:T(8,128)(2,1)S(1)}, bf16[256,512]{1,0:T(8,128)(2,1)S(1)}, u32[]{:S(2)}, u32[]{:S(2)}) collective-permute-start(bf16[256,512]{1,0:T(8,128)(2,1)S(1)} %collective-permute-done.15.refs_0_), channel_id=1, source_target_pairs={{0,2},{1,3},{2,0},{3,1},{4,6},{5,7},{6,4},{7,5},{8,10},{9,11},{10,... | collective-permute-start | bytes 786440 | tf_op jit(solution)/shard_map/ppermute | solution.py:187
  22.8 10.0 %collective-permute-start.7 = (bf16[256,512]{1,0:T(8,128)(2,1)S(1)}, bf16[256,512]{1,0:T(8,128)(2,1)S(1)}, u32[]{:S(2)}, u32[]{:S(2)}) collective-permute-start(bf16[256,512]{1,0:T(8,128)(2,1)S(1)} %collective-permute-done.5.refs_0_), channel_id=1, source_target_pairs={{0,2},{1,3},{2,0},{3,1},{4,6},{5,7},{6,4},{7,5},{8,10},{9,11},{10,... | collective-permute-start | bytes 786440 | tf_op jit(solution)/shard_map/ppermute | solution.py:187
  27.1 24.2 %collective-permute-start.16 = (bf16[256,512]{1,0:T(8,128)(2,1)S(1)}, bf16[256,512]{1,0:T(8,128)(2,1)S(1)}, u32[]{:S(2)}, u32[]{:S(2)}) collective-permute-start(bf16[256,512]{1,0:T(8,128)(2,1)S(1)} %collective-permute-done.15.refs_0_), channel_id=1, source_target_pairs={{0,1},{1,0},{2,3},{3,2},{4,5},{5,4},{6,7},{7,6},{8,9},{9,8},{10,11... | collective-permute-start | bytes 786440 | tf_op jit(solution)/shard_map/ppermute | solution.py:187
  28.9 22.3 %collective-permute-start.18 = (bf16[256,512]{1,0:T(8,128)(2,1)S(1)}, bf16[256,512]{1,0:T(8,128)(2,1)S(1)}, u32[]{:S(2)}, u32[]{:S(2)}) collective-permute-start(bf16[256,512]{1,0:T(8,128)(2,1)S(1)} %collective-permute-done.17.refs_2_), channel_id=1, source_target_pairs={{0,1},{1,0},{2,3},{3,2},{4,5},{5,4},{6,7},{7,6},{8,9},{9,8},{10,11... | collective-permute-start | bytes 786440 | tf_op jit(solution)/shard_map/ppermute | solution.py:187
  28.9 32.4 %collective-permute-start.6 = (bf16[256,512]{1,0:T(8,128)(2,1)S(1)}, bf16[256,512]{1,0:T(8,128)(2,1)S(1)}, u32[]{:S(2)}, u32[]{:S(2)}) collective-permute-start(bf16[256,512]{1,0:T(8,128)(2,1)S(1)} %collective-permute-done.5.refs_0_), channel_id=1, source_target_pairs={{0,1},{1,0},{2,3},{3,2},{4,5},{5,4},{6,7},{7,6},{8,9},{9,8},{10,11... | collective-permute-start | bytes 786440 | tf_op jit(solution)/shard_map/ppermute | solution.py:187
  32.8 28.7 %collective-permute-start.8 = (bf16[256,512]{1,0:T(8,128)(2,1)S(1)}, bf16[256,512]{1,0:T(8,128)(2,1)}, u32[]{:S(2)}, u32[]{:S(2)}) collective-permute-start(bf16[256,512]{1,0:T(8,128)(2,1)S(1)} %collective-permute-done.7.refs_2_), channel_id=1, source_target_pairs={{0,1},{1,0},{2,3},{3,2},{4,5},{5,4},{6,7},{7,6},{8,9},{9,8},{10,11... | collective-permute-start | bytes 786440 | tf_op jit(solution)/shard_map/ppermute | solution.py:187
  32.8 3.8 %collective-permute-start.1 = (s32[2,1,1,4]{3,2,1,0:T(1,128)}, s32[2,1,1,4]{3,2,1,0:T(1,128)S(1)}, u32[]{:S(2)}, u32[]{:S(2)}) collective-permute-start(s32[2,1,1,4]{3,2,1,0:T(1,128)} %refs_0_.3), channel_id=1, source_target_pairs={{0,4},{4,0},{8,12},{12,8},{1,5},{5,1},{9,13},{13,9},{2,6},{6,2},{1... | collective-permute-start | bytes 104 | tf_op jit(solution)/shard_map/ppermute | solution.py:162
  36.5 4.7 %collective-permute-start.2 = (s32[2,1,1,4]{3,2,1,0:T(1,128)}, s32[2,1,1,4]{3,2,1,0:T(1,128)S(1)}, u32[]{:S(2)}, u32[]{:S(2)}) collective-permute-start(s32[2,1,1,4]{3,2,1,0:T(1,128)} %refs_0_.3), channel_id=1, source_target_pairs={{0,8},{4,12},{8,0},{12,4},{1,9},{5,13},{9,1},{13,5},{2,10},{6,14},... | collective-permute-start | bytes 104 | tf_op jit(solution)/shard_map/ppermute | solution.py:162
  41.2 5.6 %collective-permute-start.3 = (s32[2,1,1,4]{3,2,1,0:T(1,128)}, s32[2,1,1,4]{3,2,1,0:T(1,128)S(1)}, u32[]{:S(2)}, u32[]{:S(2)}) collective-permute-start(s32[2,1,1,4]{3,2,1,0:T(1,128)} %refs_0_.3), channel_id=1, source_target_pairs={{0,12},{4,8},{8,4},{12,0},{1,13},{5,9},{9,5},{13,1},{2,14},{6,10},... | collective-permute-start | bytes 104 | tf_op jit(solution)/shard_map/ppermute | solution.py:162
  46.8 1.6 %copy-start = (bf16[2,1,512,1024]{3,2,1,0:T(8,128)(2,1)S(1)}, bf16[2,1,512,1024]{3,2,1,0:T(8,128)(2,1)}, u32[]{:S(2)}) copy-start(bf16[2,1,512,1024]{3,2,1,0:T(8,128)(2,1)} %refs_5_.1) | copy-start | bytes 6291460
  51.2 3.2 %copy-start.9 = (s32[2,1,1]{0,2,1:T(1,128)S(1)}, s32[2,1,1]{0,2,1:T(1,128)}, u32[]{:S(2)}) copy-start(s32[2,1,1]{0,2,1:T(1,128)} %param.8) | copy-start | bytes 28
  51.2 1.8 %copy-start.4 = (bf16[256,512]{1,0:T(8,128)(2,1)}, bf16[256,512]{1,0:T(8,128)(2,1)S(1)}, u32[]{:S(2)}) copy-start(bf16[256,512]{1,0:T(8,128)(2,1)S(1)} %collective-permute-done.18.refs_3_) | copy-start | bytes 786436
  53.1 0.7 copy-start.2
  54.4 12.6 %collective-permute-start.20 = (bf16[2,256,256]{2,1,0:T(8,128)(2,1)}, bf16[2,256,256]{2,1,0:T(8,128)(2,1)}, u32[]{:S(2)}, u32[]{:S(2)}) collective-permute-start(bf16[2,256,256]{2,1,0:T(8,128)(2,1)} %get-tuple-element.30), channel_id=1, source_target_pairs={{0,4},{4,0},{8,12},{12,8},{1,5},{5,1},{9,13},{13,9},{2,6},{6,2},{1... | collective-permute-start | bytes 786440 | tf_op jit(solution)/shard_map/ppermute | solution.py:217
  54.5 15.1 %collective-permute-start = (s32[2,1,1]{2,1,0:T(1,128)S(1)}, s32[2,1,1]{2,1,0:T(1,128)S(1)}, u32[]{:S(2)}, u32[]{:S(2)}) collective-permute-start(s32[2,1,1]{2,1,0:T(1,128)S(1)} %copy.10.refs_0_), channel_id=1, source_target_pairs={{0,16},{16,0},{1,17},{17,1},{2,18},{18,2},{3,19},{19,3},{4,20},{20... | collective-permute-start | bytes 32 | tf_op jit(solution)/shard_map/ppermute | solution.py:165
  56.0 18.6 %collective-permute-start.19 = (bf16[256,256]{1,0:T(8,128)(2,1)}, bf16[256,256]{1,0:T(8,128)(2,1)S(1)}, u32[]{:S(2)}, u32[]{:S(2)}) collective-permute-start(bf16[256,256]{1,0:T(8,128)(2,1)} %copy-done.8), channel_id=1, source_target_pairs={{0,4},{4,0},{8,12},{12,8},{16,20},{20,16},{24,28},{28,24},{1,5},{5... | collective-permute-start | bytes 393224 | tf_op jit(solution)/shard_map/ppermute | solution.py:222
  58.1 0.9 %copy-start.3 = (bf16[256,512]{1,0:T(8,128)(2,1)S(1)}, bf16[256,512]{1,0:T(8,128)(2,1)}, u32[]{:S(2)}) copy-start(bf16[256,512]{1,0:T(8,128)(2,1)} %copy-done.2) | copy-start | bytes 786436
  59.0 0.9 %copy-start.5 = (bf16[256,512]{1,0:T(8,128)(2,1)S(1)}, bf16[256,512]{1,0:T(8,128)(2,1)}, u32[]{:S(2)}) copy-start(bf16[256,512]{1,0:T(8,128)(2,1)} %copy-done.4) | copy-start | bytes 786436
  61.3 15.1 %collective-permute-start.23 = (bf16[256,256]{1,0:T(8,128)(2,1)S(1)}, bf16[256,256]{1,0:T(8,128)(2,1)S(1)}, u32[]{:S(2)}, u32[]{:S(2)}) collective-permute-start(bf16[256,256]{1,0:T(8,128)(2,1)S(1)} %get-tuple-element.32), channel_id=1, source_target_pairs={{0,20},{4,16},{8,28},{12,24},{16,4},{20,0},{24,12},{28,8},{1,21},{... | collective-permute-start | bytes 393224 | tf_op jit(solution)/shard_map/ppermute | solution.py:222
  63.2 23.1 %copy-start.1 = (bf16[2,512,256]{2,1,0:T(8,128)(2,1)S(1)}, bf16[2,512,256]{2,1,0:T(8,128)(2,1)}, u32[]{:S(2)}) copy-start(bf16[2,512,256]{2,1,0:T(8,128)(2,1)} %refs_2_.3) | copy-start | bytes 1572868
  63.2 9.3 %collective-permute-start.10 = (bf16[2,256,256]{2,1,0:T(8,128)(2,1)S(1)}, bf16[2,256,256]{2,1,0:T(8,128)(2,1)S(1)}, u32[]{:S(2)}, u32[]{:S(2)}) collective-permute-start(bf16[2,256,256]{2,1,0:T(8,128)(2,1)S(1)} %get-tuple-element.24), channel_id=1, source_target_pairs={{0,4},{4,0},{8,12},{12,8},{1,5},{5,1},{9,13},{13,9},{2,6},{6,2},{1... | collective-permute-start | bytes 786440 | tf_op jit(solution)/shard_map/ppermute | solution.py:217
  67.0 10.4 %collective-permute-start.22 = (bf16[256,256]{1,0:T(8,128)(2,1)S(1)}, bf16[256,256]{1,0:T(8,128)(2,1)S(1)}, u32[]{:S(2)}, u32[]{:S(2)}) collective-permute-start(bf16[256,256]{1,0:T(8,128)(2,1)S(1)} %get-tuple-element.31), channel_id=1, source_target_pairs={{0,16},{16,0},{1,17},{17,1},{2,18},{18,2},{3,19},{19,3},{4,20},{20... | collective-permute-start | bytes 393224 | tf_op jit(solution)/shard_map/ppermute | solution.py:211
  69.7 10.4 %collective-permute-start.21 = (bf16[256,256]{1,0:T(8,128)(2,1)S(1)}, bf16[256,256]{1,0:T(8,128)(2,1)S(1)}, u32[]{:S(2)}, u32[]{:S(2)}) collective-permute-start(bf16[256,256]{1,0:T(8,128)(2,1)S(1)} %get-tuple-element.34), channel_id=1, source_target_pairs={{0,8},{4,12},{8,0},{12,4},{16,24},{20,28},{24,16},{28,20},{1,9},{5... | collective-permute-start | bytes 393224 | tf_op jit(solution)/shard_map/ppermute | solution.py:222
  72.5 13.8 %collective-permute-start.24 = (bf16[256,256]{1,0:T(8,128)(2,1)S(1)}, bf16[256,256]{1,0:T(8,128)(2,1)S(1)}, u32[]{:S(2)}, u32[]{:S(2)}) collective-permute-start(bf16[256,256]{1,0:T(8,128)(2,1)S(1)} %get-tuple-element.33), channel_id=1, source_target_pairs={{0,24},{4,28},{8,16},{12,20},{16,8},{20,12},{24,0},{28,4},{1,25},{... | collective-permute-start | bytes 393224 | tf_op jit(solution)/shard_map/ppermute | solution.py:222
  74.7 13.1 %collective-permute-start.13 = (bf16[256,256]{1,0:T(8,128)(2,1)S(1)}, bf16[256,256]{1,0:T(8,128)(2,1)S(1)}, u32[]{:S(2)}, u32[]{:S(2)}) collective-permute-start(bf16[256,256]{1,0:T(8,128)(2,1)S(1)} %get-tuple-element.26), channel_id=1, source_target_pairs={{0,20},{4,16},{8,28},{12,24},{16,4},{20,0},{24,12},{28,8},{1,21},{... | collective-permute-start | bytes 393224 | tf_op jit(solution)/shard_map/ppermute | solution.py:222
  76.5 11.3 %collective-permute-start.9 = (bf16[256,256]{1,0:T(8,128)(2,1)S(1)}, bf16[256,256]{1,0:T(8,128)(2,1)S(1)}, u32[]{:S(2)}, u32[]{:S(2)}) collective-permute-start(bf16[256,256]{1,0:T(8,128)(2,1)S(1)} %get-tuple-element.22), channel_id=1, source_target_pairs={{0,4},{4,0},{8,12},{12,8},{16,20},{20,16},{24,28},{28,24},{1,5},{5... | collective-permute-start | bytes 393224 | tf_op jit(solution)/shard_map/ppermute | solution.py:222
  77.5 10.3 %collective-permute-start.12 = (bf16[256,256]{1,0:T(8,128)(2,1)S(1)}, bf16[256,256]{1,0:T(8,128)(2,1)S(1)}, u32[]{:S(2)}, u32[]{:S(2)}) collective-permute-start(bf16[256,256]{1,0:T(8,128)(2,1)S(1)} %get-tuple-element.25), channel_id=1, source_target_pairs={{0,16},{16,0},{1,17},{17,1},{2,18},{18,2},{3,19},{19,3},{4,20},{20... | collective-permute-start | bytes 393224 | tf_op jit(solution)/shard_map/ppermute | solution.py:211
  80.0 11.6 %collective-permute-start.11 = (bf16[256,256]{1,0:T(8,128)(2,1)S(1)}, bf16[256,256]{1,0:T(8,128)(2,1)S(1)}, u32[]{:S(2)}, u32[]{:S(2)}) collective-permute-start(bf16[256,256]{1,0:T(8,128)(2,1)S(1)} %get-tuple-element.38), channel_id=1, source_target_pairs={{0,8},{4,12},{8,0},{12,4},{16,24},{20,28},{24,16},{28,20},{1,9},{5... | collective-permute-start | bytes 393224 | tf_op jit(solution)/shard_map/ppermute | solution.py:222
  86.3 6.8 %collective-permute-start.14 = (bf16[256,256]{1,0:T(8,128)(2,1)S(1)}, bf16[256,256]{1,0:T(8,128)(2,1)S(1)}, u32[]{:S(2)}, u32[]{:S(2)}) collective-permute-start(bf16[256,256]{1,0:T(8,128)(2,1)S(1)} %get-tuple-element.37), channel_id=1, source_target_pairs={{0,24},{4,28},{8,16},{12,20},{16,8},{20,12},{24,0},{28,4},{1,25},{... | collective-permute-start | bytes 393224 | tf_op jit(solution)/shard_map/ppermute | solution.py:222
  (3 other events, 2.0 us)

commit v4 on v3

--- a/solution.py
+++ b/solution.py
@@ -195,10 +195,8 @@
         return sum(block.astype(jnp.float32) for block in blocks).astype(jnp.bfloat16)
 
     result = None
-    half = n_row // 2
-    away = [(turn, turn & (turn - 1) != 0) for turn in reversed(range(n_row)) if turn % 2]
-    stay = [(turn, turn & (turn - 1) != 0 or turn == half) for turn in reversed(range(n_row)) if not turn % 2]
-    stay[-1] = (0, False)
+    away = [(turn, False) for turn in reversed(range(n_row)) if turn % 2]
+    stay = [(turn, False) for turn in reversed(range(n_row)) if not turn % 2]
     ends = [(g, z) for g in range(layers) for z in range(n_row)]
     for level in range(levels):
         terms = {}
@@ -214,7 +212,12 @@
             swap = [(z, z ^ bit) for z in range(n_row)]
             for turn in reversed(range(0, n_row, bit)):
                 if turn & bit and turn != bit:
-                    terms[turn ^ bit].append(lax.ppermute(total(terms.pop(turn)), "row", swap))
+                    parts = terms.pop(turn)
+                    got = {}
+                    for u in reversed(range(layers)):
+                        block = total([part[u] for part in parts])
+                        got[u] = lax.ppermute(block, "row", swap)
+                    terms[turn ^ bit].append([got[u] for u in range(layers)])
             last = terms.pop(bit)
             for u in range(layers):
                 block = total([term[u] for term in last])

time: 94.9 us -> 98.8 us (1.041)
  waiting for transfers between devices: 31.4 us -> 40.5 us
  starting transfers between devices: 43.5 us -> 39.8 us
  Pallas kernels: 11.1 us -> 10 us
    ppermute x3, starting transfers between devices: 6.77 us -> 0.61 us  [on_device(): lax.ppermute(blockmask, 'row', [(z, z ^ turn) for z in range(n_row)])]
    ppermute x2 -> x4, waiting for transfers between devices: 1.58 us -> 7.73 us  [on_device(): got[u] = lax.ppermute(block, 'row', swap)]
    ppermute x1, waiting for transfers between devices: 5.63 us -> 0.01 us  [on_device(): part = lax.ppermute(part, 'col', [(k, k ^ hop) for k in range(n_col)])]
    ppermute x6, starting transfers between devices: 12.4 us -> 18 us  [on_device(): pieces[flip ^ step, turn] = lax.ppermute(piece, 'col', swap)]
    ppermute x2, starting transfers between devices: 5.42 us -> 0.77 us  [on_device(): pieces[0, turn] = lax.ppermute(part, ('row', 'col'), pairs)]
    ppermute x1, starting transfers between devices: 3.03 us -> 6.82 us  [on_device(): part = lax.ppermute(part, 'col', [(k, k ^ hop) for k in range(n_col)])]
    ppermute x2, waiting for transfers between devices: 0.01 us -> 2.81 us  [on_device(): pieces[0, turn] = lax.ppermute(part, ('row', 'col'), pairs)]
    ppermute x8, waiting for transfers between devices: 11.7 us -> 14.1 us  [on_device(): groups[u].append(lax.ppermute(block, ('gz', 'row'), pairs))]
  transfers between devices with their start and end apart: 25 -> 27, of which waited for: 11 -> 11; matrix products, arithmetic and copies ran while one was open for 1% -> 1% of each run, Pallas kernels for 10% -> 9%
where the time goes in v4:
time: 98.8 us; the launch traced here: 98.6 us
  waiting for transfers between devices  40.5 us (41%)
  starting transfers between devices  39.8 us (40%)
  Pallas kernels  10 us (10%)
  local copies, waits for them, and re-layouts  7.07 us (7%)
  other arithmetic  1.05 us (1%)
    ppermute x6, starting transfers between devices, on_device(): pieces[flip ^ step, turn] = lax.ppermute(piece, 'col', swap)  18 us
    ppermute x8, waiting for transfers between devices, on_device(): groups[u].append(lax.ppermute(block, ('gz', 'row'), pairs))  14.1 us
    ppermute x3, waiting for transfers between devices, on_device(): lax.ppermute(blockmask, 'row', [(z, z ^ turn) for z in range(n_row)])  8.75 us
    ppermute x4, waiting for transfers between devices, on_device(): got[u] = lax.ppermute(block, 'row', swap)  7.73 us
    ppermute x8, starting transfers between devices, on_device(): groups[u].append(lax.ppermute(block, ('gz', 'row'), pairs))  7.21 us
    ppermute x6, waiting for transfers between devices, on_device(): pieces[flip ^ step, turn] = lax.ppermute(piece, 'col', swap)  7.07 us
    ppermute x1, starting transfers between devices, on_device(): part = lax.ppermute(part, 'col', [(k, k ^ hop) for k in range(n_col)])  6.82 us
    unnamed x21, local copies, waits for them, and re-layouts  6.01 us
  transfers between devices with their start and end apart: 27, of which 11 were waited for; matrix products, arithmetic and copies ran while one was open for 1% of the time, Pallas kernels for 9%

profile of v4, /device:TPU:0, one launch (start us, length us, event | category | flops | bytes accessed | tf_op | source)
XLA Modules:
  0.0 98.6 jit_solution(1746682302607794642)
XLA Ops:
  0.0 1.1 %slice_bitcast_fusion = (bf16[256,512]{1,0:T(8,128)(2,1)S(1)}, bf16[256,512]{1,0:T(8,128)(2,1)S(1)}) fusion(bf16[2,1,256,512]{3,2,1,0:T(8,128)(2,1)} %param.6), kind=kLoop, calls=%fused_computation.2 | loop fusion | bytes 1048576 | tf_op jit(solution)/shard_map/squeeze | solution.py:171
  1.1 0.7 collective-permute-start.16
  1.8 6.8 %collective-permute-start.4 = (bf16[256,512]{1,0:T(8,128)(2,1)S(1)}, bf16[256,512]{1,0:T(8,128)(2,1)S(1)}, u32[]{:S(2)}, u32[]{:S(2)}) collective-permute-start(bf16[256,512]{1,0:T(8,128)(2,1)S(1)} %get-tuple-element.42), channel_id=1, source_target_pairs={{0,2},{1,3},{2,0},{3,1},{4,6},{5,7},{6,4},{7,5},{8,10},{9,11},{10,... | collective-permute-start | bytes 786440 | tf_op jit(solution)/shard_map/ppermute | solution.py:176
  8.6 13.5 %collective-permute-start.18 = (bf16[256,512]{1,0:T(8,128)(2,1)S(1)}, bf16[256,512]{1,0:T(8,128)(2,1)S(1)}, u32[]{:S(2)}, u32[]{:S(2)}) collective-permute-start(bf16[256,512]{1,0:T(8,128)(2,1)S(1)} %collective-permute-done.16.refs_0_), channel_id=1, source_target_pairs={{0,2},{1,3},{2,0},{3,1},{4,6},{5,7},{6,4},{7,5},{8,10},{9,11},{10,... | collective-permute-start | bytes 786440 | tf_op jit(solution)/shard_map/ppermute | solution.py:187
  22.2 7.1 %collective-permute-done.18.refs_2_ = bf16[256,512]{1,0:T(8,128)(2,1)S(1)} collective-permute-done((bf16[256,512]{1,0:T(8,128)(2,1)S(1)}, bf16[256,512]{1,0:T(8,128)(2,1)S(1)}, u32[]{:S(2)}, u32[]{:S(2)}) %collective-permute-start.18) | collective-permute-done | bytes 262176 | tf_op jit(solution)/shard_map/ppermute | solution.py:187
  29.2 2.8 %collective-permute-done.5.refs_0_ = bf16[256,512]{1,0:T(8,128)(2,1)S(1)} collective-permute-done((bf16[256,512]{1,0:T(8,128)(2,1)S(1)}, bf16[256,512]{1,0:T(8,128)(2,1)S(1)}, u32[]{:S(2)}, u32[]{:S(2)}) %collective-permute-start.5) | collective-permute-done | bytes 262176 | tf_op jit(solution)/shard_map/ppermute | solution.py:182
  32.0 4.2 %collective-permute-start.7 = (bf16[256,512]{1,0:T(8,128)(2,1)S(1)}, bf16[256,512]{1,0:T(8,128)(2,1)S(1)}, u32[]{:S(2)}, u32[]{:S(2)}) collective-permute-start(bf16[256,512]{1,0:T(8,128)(2,1)S(1)} %collective-permute-done.5.refs_0_), channel_id=1, source_target_pairs={{0,2},{1,3},{2,0},{3,1},{4,6},{5,7},{6,4},{7,5},{8,10},{9,11},{10,... | collective-permute-start | bytes 786440 | tf_op jit(solution)/shard_map/ppermute | solution.py:187
  36.3 3.8 %collective-permute-done.1.refs_1_ = s32[2,1,1,4]{3,2,1,0:T(1,128)S(1)} collective-permute-done((s32[2,1,1,4]{3,2,1,0:T(1,128)}, s32[2,1,1,4]{3,2,1,0:T(1,128)S(1)}, u32[]{:S(2)}, u32[]{:S(2)}) %collective-permute-start.1) | collective-permute-done | bytes 64 | tf_op jit(solution)/shard_map/ppermute | solution.py:162
  41.0 4.7 %collective-permute-done.3.refs_3_ = s32[2,1,1,4]{3,2,1,0:T(1,128)S(1)} collective-permute-done((s32[2,1,1,4]{3,2,1,0:T(1,128)}, s32[2,1,1,4]{3,2,1,0:T(1,128)S(1)}, u32[]{:S(2)}, u32[]{:S(2)}) %collective-permute-start.3) | collective-permute-done | bytes 64 | tf_op jit(solution)/shard_map/ppermute | solution.py:162
  45.6 1.6 %copy-done = bf16[2,1,512,1024]{3,2,1,0:T(8,128)(2,1)S(1)} copy-done((bf16[2,1,512,1024]{3,2,1,0:T(8,128)(2,1)S(1)}, bf16[2,1,512,1024]{3,2,1,0:T(8,128)(2,1)}, u32[]{:S(2)}) %copy-start) | copy-done | bytes 2097176
  48.6 1.4 %prepare.1 = (f32[64]{0:T(128)S(1)}, bf16[2,1,512,1024]{3,2,1,0:T(8,128)(2,1)S(1)}) custom-call(s32[2,1,1,4]{3,2,1,0:T(1,128)S(1)} %copy-done.4, s32[2,1,1,4]{3,2,1,0:T(1,128)S(1)} %collective-permute-done.1.refs_1_, s32[2,1,1,4]{3,2,1,0:T(1,128)S(1)} %collective-permute-done.2.refs_2_, s32[2,1,1,4]{3,2,1,0:T(1,128)S(1)} %collective-permute-done.3.refs_3_, ...), custom_call_target="tpu_custom_call" | custom-call | flops 1048576 | bytes 4194304 | tf_op jit(solution)/shard_map/prepare/pallas_call | solution.py:34
  50.1 1.7 %shard_map.67 = (bf16[256,256]{1,0:T(8,128)(2,1)S(1)}, bf16[256,256]{1,0:T(8,128)(2,1)}, bf16[256,256]{1,0:T(8,128)(2,1)S(1)}, bf16[256,256]{1,0:T(8,128)(2,1)S(1)}) custom-call(f32[64]{0:T(128)S(1)} %get-tuple-element.23.picks, bf16[256,512]{1,0:T(8,128)(2,1)S(1)} %collective-permute-done.16.refs_0_, bf16[256,512]{1,0:T(8,128)(2,1)S(1)} %collective-permute-done.17.refs_1_, ...), custom_call_target="tpu_custom_call" | custom-call | flops 536870912 | bytes 2621440 | tf_op jit(solution)/shard_map/pallas_call | solution.py:97
  51.8 0.7 copy-done.2
  53.9 1.5 %collective-permute-start = (s32[2,1,1]{2,1,0:T(1,128)S(1)}, s32[2,1,1]{2,1,0:T(1,128)S(1)}, u32[]{:S(2)}, u32[]{:S(2)}) collective-permute-start(s32[2,1,1]{2,1,0:T(1,128)S(1)} %copy.10.refs_0_), channel_id=1, source_target_pairs={{0,16},{16,0},{1,17},{17,1},{2,18},{18,2},{3,19},{19,3},{4,20},{20... | collective-permute-start | bytes 32 | tf_op jit(solution)/shard_map/ppermute | solution.py:165
  55.4 2.0 %collective-permute-start.21 = (bf16[256,256]{1,0:T(8,128)(2,1)}, bf16[256,256]{1,0:T(8,128)(2,1)S(1)}, u32[]{:S(2)}, u32[]{:S(2)}) collective-permute-start(bf16[256,256]{1,0:T(8,128)(2,1)} %copy-done.8), channel_id=1, source_target_pairs={{0,4},{4,0},{8,12},{12,8},{1,5},{5,1},{9,13},{13,9},{2,6},{6,2},{1... | collective-permute-start | bytes 393224 | tf_op jit(solution)/shard_map/ppermute | solution.py:219
  57.7 0.9 copy-done.3
  58.6 1.3 %shard_map.66 = (bf16[256,256]{1,0:T(8,128)(2,1)S(1)}, bf16[256,256]{1,0:T(8,128)(2,1)S(1)}, bf16[256,256]{1,0:T(8,128)(2,1)S(1)}, bf16[256,256]{1,0:T(8,128)(2,1)S(1)}) custom-call(f32[64]{0:T(128)S(1)} %get-tuple-element.23.picks, bf16[256,512]{1,0:T(8,128)(2,1)S(1)} %collective-permute-done.16.refs_0_, ...), custom_call_target="tpu_custom_call" | custom-call | flops 536870912 | bytes 2621440 | tf_op jit(solution)/shard_map/pallas_call | solution.py:97
  60.3 0.9 add_convert_fusion
  61.3 2.8 %collective-permute-start.24 = (bf16[256,256]{1,0:T(8,128)(2,1)S(1)}, bf16[256,256]{1,0:T(8,128)(2,1)S(1)}, u32[]{:S(2)}, u32[]{:S(2)}) collective-permute-start(bf16[256,256]{1,0:T(8,128)(2,1)S(1)} %get-tuple-element.38), channel_id=1, source_target_pairs={{0,20},{4,16},{8,28},{12,24},{16,4},{20,0},{24,12},{28,8},{1,21},{... | collective-permute-start | bytes 393224 | tf_op jit(solution)/shard_map/ppermute | solution.py:225
  64.6 1.3 %shard_map.65 = (bf16[256,256]{1,0:T(8,128)(2,1)S(1)}, bf16[256,256]{1,0:T(8,128)(2,1)S(1)}, bf16[256,256]{1,0:T(8,128)(2,1)S(1)}, bf16[256,256]{1,0:T(8,128)(2,1)S(1)}) custom-call(f32[64]{0:T(128)S(1)} %get-tuple-element.23.picks, bf16[256,512]{1,0:T(8,128)(2,1)S(1)} %collective-permute-done.5.refs_0_, ...), custom_call_target="tpu_custom_call" | custom-call | flops 536870912 | bytes 2621440 | tf_op jit(solution)/shard_map/pallas_call | solution.py:97
  66.3 1.3 %shard_map.64 = (bf16[256,256]{1,0:T(8,128)(2,1)S(1)}, bf16[256,256]{1,0:T(8,128)(2,1)S(1)}, bf16[256,256]{1,0:T(8,128)(2,1)S(1)}, bf16[256,256]{1,0:T(8,128)(2,1)S(1)}) custom-call(f32[64]{0:T(128)S(1)} %get-tuple-element.23.picks, bf16[256,512]{1,0:T(8,128)(2,1)S(1)} %collective-permute-done.5.refs_0_, ...), custom_call_target="tpu_custom_call" | custom-call | flops 536870912 | bytes 2621440 | tf_op jit(solution)/shard_map/pallas_call | solution.py:97
  67.6 3.8 %collective-permute-done.14 = bf16[256,256]{1,0:T(8,128)(2,1)S(1)} collective-permute-done((bf16[256,256]{1,0:T(8,128)(2,1)S(1)}, bf16[256,256]{1,0:T(8,128)(2,1)S(1)}, u32[]{:S(2)}, u32[]{:S(2)}) %collective-permute-start.14) | collective-permute-done | bytes 131104 | tf_op jit(solution)/shard_map/ppermute | solution.py:219
  72.1 1.1 %collective-permute-start.26 = (bf16[256,256]{1,0:T(8,128)(2,1)S(1)}, bf16[256,256]{1,0:T(8,128)(2,1)S(1)}, u32[]{:S(2)}, u32[]{:S(2)}) collective-permute-start(bf16[256,256]{1,0:T(8,128)(2,1)S(1)} %add_convert_fusion), channel_id=1, source_target_pairs={{0,24},{4,28},{8,16},{12,20},{16,8},{20,12},{24,0},{28,4},{1,25},{... | collective-permute-start | bytes 393224 | tf_op jit(solution)/shard_map/ppermute | solution.py:225
  73.2 4.0 %collective-permute-done.10 = bf16[256,256]{1,0:T(8,128)(2,1)S(1)} collective-permute-done((bf16[256,256]{1,0:T(8,128)(2,1)S(1)}, bf16[256,256]{1,0:T(8,128)(2,1)S(1)}, u32[]{:S(2)}, u32[]{:S(2)}) %collective-permute-start.10) | collective-permute-done | bytes 131104 | tf_op jit(solution)/shard_map/ppermute | solution.py:219
  77.2 2.8 %collective-permute-start.13 = (bf16[256,256]{1,0:T(8,128)(2,1)S(1)}, bf16[256,256]{1,0:T(8,128)(2,1)S(1)}, u32[]{:S(2)}, u32[]{:S(2)}) collective-permute-start(bf16[256,256]{1,0:T(8,128)(2,1)S(1)} %get-tuple-element.30), channel_id=1, source_target_pairs={{0,20},{4,16},{8,28},{12,24},{16,4},{20,0},{24,12},{28,8},{1,21},{... | collective-permute-start | bytes 393224 | tf_op jit(solution)/shard_map/ppermute | solution.py:225
  80.1 1.4 %collective-permute-start.12 = (bf16[256,256]{1,0:T(8,128)(2,1)S(1)}, bf16[256,256]{1,0:T(8,128)(2,1)S(1)}, u32[]{:S(2)}, u32[]{:S(2)}) collective-permute-start(bf16[256,256]{1,0:T(8,128)(2,1)S(1)} %get-tuple-element.29), channel_id=1, source_target_pairs={{0,16},{16,0},{1,17},{17,1},{2,18},{18,2},{3,19},{19,3},{4,20},{20... | collective-permute-start | bytes 393224 | tf_op jit(solution)/shard_map/ppermute | solution.py:209
  81.5 2.7 %collective-permute-done.26.refs_8_ = bf16[256,256]{1,0:T(8,128)(2,1)S(1)} collective-permute-done((bf16[256,256]{1,0:T(8,128)(2,1)S(1)}, bf16[256,256]{1,0:T(8,128)(2,1)S(1)}, u32[]{:S(2)}, u32[]{:S(2)}) %collective-permute-start.26) | collective-permute-done | bytes 131104 | tf_op jit(solution)/shard_map/ppermute | solution.py:225
  84.3 4.0 %collective-permute-done.22.refs_5_ = bf16[256,256]{1,0:T(8,128)(2,1)S(1)} collective-permute-done((bf16[256,256]{1,0:T(8,128)(2,1)S(1)}, bf16[256,256]{1,0:T(8,128)(2,1)S(1)}, u32[]{:S(2)}, u32[]{:S(2)}) %collective-permute-start.22) | collective-permute-done | bytes 131104 | tf_op jit(solution)/shard_map/ppermute | solution.py:225
  88.3 1.4 %shard_map.68.refs_9_ = bf16[2,512,256]{2,1,0:T(8,128)(2,1)} custom-call(s32[2,1,1]{2,1,0:T(1,128)S(1)} %copy.10.refs_0_, s32[2,1,1]{2,1,0:T(1,128)S(1)} %collective-permute-done.refs_1_, bf16[2,512,256]{2,1,0:T(8,128)(2,1)S(1)} %copy-done.1, bf16[256,256]{1,0:T(8,128)(2,1)S(1)} %get-tuple-element.33.refs_3_, ...), custom_call_target="tpu_custom_call" | custom-call | flops 524288 | bytes 1048576 | tf_op jit(solution)/shard_map/pallas_call | solution.py:139
  89.8 6.2 %collective-permute-done.15.refs_8_ = bf16[256,256]{1,0:T(8,128)(2,1)S(1)} collective-permute-done((bf16[256,256]{1,0:T(8,128)(2,1)S(1)}, bf16[256,256]{1,0:T(8,128)(2,1)S(1)}, u32[]{:S(2)}, u32[]{:S(2)}) %collective-permute-start.15) | collective-permute-done | bytes 131104 | tf_op jit(solution)/shard_map/ppermute | solution.py:225
  96.0 1.1 %collective-permute-done.11.refs_5_ = bf16[256,256]{1,0:T(8,128)(2,1)S(1)} collective-permute-done((bf16[256,256]{1,0:T(8,128)(2,1)S(1)}, bf16[256,256]{1,0:T(8,128)(2,1)S(1)}, u32[]{:S(2)}, u32[]{:S(2)}) %collective-permute-start.11) | collective-permute-done | bytes 131104 | tf_op jit(solution)/shard_map/ppermute | solution.py:225
  97.1 1.4 %shard_map.69 = bf16[2,512,256]{2,1,0:T(8,128)(2,1)} custom-call(s32[2,1,1]{2,1,0:T(1,128)S(1)} %copy.10.refs_0_, s32[2,1,1]{2,1,0:T(1,128)S(1)} %collective-permute-done.refs_1_, bf16[2,512,256]{2,1,0:T(8,128)(2,1)S(1)} %copy-done.1, bf16[256,256]{1,0:T(8,128)(2,1)S(1)} %get-tuple-element.25.refs_3_, ...), custom_call_target="tpu_custom_call", output_to_operand_aliasing={{}: (9, {})} | custom-call | flops 524288 | bytes 1048576 | tf_op jit(solution)/shard_map/pallas_call | solution.py:139
  (55 shorter events, 6.1 us)
Async XLA Ops:
  1.1 7.5 %collective-permute-start.16 = (bf16[256,512]{1,0:T(8,128)(2,1)S(1)}, bf16[256,512]{1,0:T(8,128)(2,1)S(1)}, u32[]{:S(2)}, u32[]{:S(2)}) collective-permute-start(bf16[256,512]{1,0:T(8,128)(2,1)S(1)} %get-tuple-element.41), channel_id=1, source_target_pairs={{0,0},{1,4},{2,8},{3,12},{4,1},{5,5},{6,9},{7,13},{8,2},{9,6},{10,... | collective-permute-start | bytes 786440 | tf_op jit(solution)/shard_map/ppermute | solution.py:182
  1.8 20.3 %collective-permute-start.4 = (bf16[256,512]{1,0:T(8,128)(2,1)S(1)}, bf16[256,512]{1,0:T(8,128)(2,1)S(1)}, u32[]{:S(2)}, u32[]{:S(2)}) collective-permute-start(bf16[256,512]{1,0:T(8,128)(2,1)S(1)} %get-tuple-element.42), channel_id=1, source_target_pairs={{0,2},{1,3},{2,0},{3,1},{4,6},{5,7},{6,4},{7,5},{8,10},{9,11},{10,... | collective-permute-start | bytes 786440 | tf_op jit(solution)/shard_map/ppermute | solution.py:176
  8.6 20.6 %collective-permute-start.18 = (bf16[256,512]{1,0:T(8,128)(2,1)S(1)}, bf16[256,512]{1,0:T(8,128)(2,1)S(1)}, u32[]{:S(2)}, u32[]{:S(2)}) collective-permute-start(bf16[256,512]{1,0:T(8,128)(2,1)S(1)} %collective-permute-done.16.refs_0_), channel_id=1, source_target_pairs={{0,2},{1,3},{2,0},{3,1},{4,6},{5,7},{6,4},{7,5},{8,10},{9,11},{10,... | collective-permute-start | bytes 786440 | tf_op jit(solution)/shard_map/ppermute | solution.py:187
  22.1 10.0 %collective-permute-start.5 = (bf16[256,512]{1,0:T(8,128)(2,1)S(1)}, bf16[256,512]{1,0:T(8,128)(2,1)S(1)}, u32[]{:S(2)}, u32[]{:S(2)}) collective-permute-start(bf16[256,512]{1,0:T(8,128)(2,1)S(1)} %collective-permute-done.4), channel_id=1, source_target_pairs={{2,0},{3,4},{0,8},{1,12},{6,1},{7,5},{4,9},{5,13},{10,2},{11,6},{8... | collective-permute-start | bytes 786440 | tf_op jit(solution)/shard_map/ppermute | solution.py:182
  22.2 27.9 %collective-permute-start.17 = (bf16[256,512]{1,0:T(8,128)(2,1)S(1)}, bf16[256,512]{1,0:T(8,128)(2,1)S(1)}, u32[]{:S(2)}, u32[]{:S(2)}) collective-permute-start(bf16[256,512]{1,0:T(8,128)(2,1)S(1)} %collective-permute-done.16.refs_0_), channel_id=1, source_target_pairs={{0,1},{1,0},{2,3},{3,2},{4,5},{5,4},{6,7},{7,6},{8,9},{9,8},{10,11... | collective-permute-start | bytes 786440 | tf_op jit(solution)/shard_map/ppermute | solution.py:187
  29.2 20.8 %collective-permute-start.19 = (bf16[256,512]{1,0:T(8,128)(2,1)S(1)}, bf16[256,512]{1,0:T(8,128)(2,1)S(1)}, u32[]{:S(2)}, u32[]{:S(2)}) collective-permute-start(bf16[256,512]{1,0:T(8,128)(2,1)S(1)} %collective-permute-done.18.refs_2_), channel_id=1, source_target_pairs={{0,1},{1,0},{2,3},{3,2},{4,5},{5,4},{6,7},{7,6},{8,9},{9,8},{10,11... | collective-permute-start | bytes 786440 | tf_op jit(solution)/shard_map/ppermute | solution.py:187
  32.0 25.4 %collective-permute-start.7 = (bf16[256,512]{1,0:T(8,128)(2,1)S(1)}, bf16[256,512]{1,0:T(8,128)(2,1)S(1)}, u32[]{:S(2)}, u32[]{:S(2)}) collective-permute-start(bf16[256,512]{1,0:T(8,128)(2,1)S(1)} %collective-permute-done.5.refs_0_), channel_id=1, source_target_pairs={{0,2},{1,3},{2,0},{3,1},{4,6},{5,7},{6,4},{7,5},{8,10},{9,11},{10,... | collective-permute-start | bytes 786440 | tf_op jit(solution)/shard_map/ppermute | solution.py:187
  36.3 3.8 %collective-permute-start.1 = (s32[2,1,1,4]{3,2,1,0:T(1,128)}, s32[2,1,1,4]{3,2,1,0:T(1,128)S(1)}, u32[]{:S(2)}, u32[]{:S(2)}) collective-permute-start(s32[2,1,1,4]{3,2,1,0:T(1,128)} %refs_0_.3), channel_id=1, source_target_pairs={{0,4},{4,0},{8,12},{12,8},{1,5},{5,1},{9,13},{13,9},{2,6},{6,2},{1... | collective-permute-start | bytes 104 | tf_op jit(solution)/shard_map/ppermute | solution.py:162
  36.3 4.7 %collective-permute-start.2 = (s32[2,1,1,4]{3,2,1,0:T(1,128)}, s32[2,1,1,4]{3,2,1,0:T(1,128)S(1)}, u32[]{:S(2)}, u32[]{:S(2)}) collective-permute-start(s32[2,1,1,4]{3,2,1,0:T(1,128)} %refs_0_.3), channel_id=1, source_target_pairs={{0,8},{4,12},{8,0},{12,4},{1,9},{5,13},{9,1},{13,5},{2,10},{6,14},... | collective-permute-start | bytes 104 | tf_op jit(solution)/shard_map/ppermute | solution.py:162
  40.1 5.6 %collective-permute-start.3 = (s32[2,1,1,4]{3,2,1,0:T(1,128)}, s32[2,1,1,4]{3,2,1,0:T(1,128)S(1)}, u32[]{:S(2)}, u32[]{:S(2)}) collective-permute-start(s32[2,1,1,4]{3,2,1,0:T(1,128)} %refs_0_.3), channel_id=1, source_target_pairs={{0,12},{4,8},{8,4},{12,0},{1,13},{5,9},{9,5},{13,1},{2,14},{6,10},... | collective-permute-start | bytes 104 | tf_op jit(solution)/shard_map/ppermute | solution.py:162
  45.6 1.6 %copy-start = (bf16[2,1,512,1024]{3,2,1,0:T(8,128)(2,1)S(1)}, bf16[2,1,512,1024]{3,2,1,0:T(8,128)(2,1)}, u32[]{:S(2)}) copy-start(bf16[2,1,512,1024]{3,2,1,0:T(8,128)(2,1)} %refs_5_.1) | copy-start | bytes 6291460
  50.0 3.8 %copy-start.9 = (s32[2,1,1]{0,2,1:T(1,128)S(1)}, s32[2,1,1]{0,2,1:T(1,128)}, u32[]{:S(2)}) copy-start(s32[2,1,1]{0,2,1:T(1,128)} %param.8) | copy-start | bytes 28
  53.8 6.2 %collective-permute-start.25 = (bf16[256,256]{1,0:T(8,128)(2,1)}, bf16[256,256]{1,0:T(8,128)(2,1)}, u32[]{:S(2)}, u32[]{:S(2)}) collective-permute-start(bf16[256,256]{1,0:T(8,128)(2,1)} %get-tuple-element.40), channel_id=1, source_target_pairs={{0,4},{4,0},{8,12},{12,8},{1,5},{5,1},{9,13},{13,9},{2,6},{6,2},{1... | collective-permute-start | bytes 393224 | tf_op jit(solution)/shard_map/ppermute | solution.py:219
  53.9 18.2 %collective-permute-start = (s32[2,1,1]{2,1,0:T(1,128)S(1)}, s32[2,1,1]{2,1,0:T(1,128)S(1)}, u32[]{:S(2)}, u32[]{:S(2)}) collective-permute-start(s32[2,1,1]{2,1,0:T(1,128)S(1)} %copy.10.refs_0_), channel_id=1, source_target_pairs={{0,16},{16,0},{1,17},{17,1},{2,18},{18,2},{3,19},{19,3},{4,20},{20... | collective-permute-start | bytes 32 | tf_op jit(solution)/shard_map/ppermute | solution.py:165
  55.4 5.9 %collective-permute-start.6 = (bf16[256,512]{1,0:T(8,128)(2,1)S(1)}, bf16[256,512]{1,0:T(8,128)(2,1)S(1)}, u32[]{:S(2)}, u32[]{:S(2)}) collective-permute-start(bf16[256,512]{1,0:T(8,128)(2,1)S(1)} %collective-permute-done.5.refs_0_), channel_id=1, source_target_pairs={{0,1},{1,0},{2,3},{3,2},{4,5},{5,4},{6,7},{7,6},{8,9},{9,8},{10,11... | collective-permute-start | bytes 786440 | tf_op jit(solution)/shard_map/ppermute | solution.py:187
  55.4 10.5 %collective-permute-start.21 = (bf16[256,256]{1,0:T(8,128)(2,1)}, bf16[256,256]{1,0:T(8,128)(2,1)S(1)}, u32[]{:S(2)}, u32[]{:S(2)}) collective-permute-start(bf16[256,256]{1,0:T(8,128)(2,1)} %copy-done.8), channel_id=1, source_target_pairs={{0,4},{4,0},{8,12},{12,8},{1,5},{5,1},{9,13},{13,9},{2,6},{6,2},{1... | collective-permute-start | bytes 393224 | tf_op jit(solution)/shard_map/ppermute | solution.py:219
  57.5 6.6 %collective-permute-start.8 = (bf16[256,512]{1,0:T(8,128)(2,1)S(1)}, bf16[256,512]{1,0:T(8,128)(2,1)S(1)}, u32[]{:S(2)}, u32[]{:S(2)}) collective-permute-start(bf16[256,512]{1,0:T(8,128)(2,1)S(1)} %collective-permute-done.7.refs_2_), channel_id=1, source_target_pairs={{0,1},{1,0},{2,3},{3,2},{4,5},{5,4},{6,7},{7,6},{8,9},{9,8},{10,11... | collective-permute-start | bytes 786440 | tf_op jit(solution)/shard_map/ppermute | solution.py:187
  57.7 0.9 copy-start.3
  58.6 1.4 %copy-start.7 = (bf16[256,256]{1,0:T(8,128)(2,1)S(1)}, bf16[256,256]{1,0:T(8,128)(2,1)}, u32[]{:S(2)}) copy-start(bf16[256,256]{1,0:T(8,128)(2,1)} %copy-done.6) | copy-start | bytes 393220
  60.0 17.2 %collective-permute-start.20 = (bf16[256,256]{1,0:T(8,128)(2,1)S(1)}, bf16[256,256]{1,0:T(8,128)(2,1)S(1)}, u32[]{:S(2)}, u32[]{:S(2)}) collective-permute-start(bf16[256,256]{1,0:T(8,128)(2,1)S(1)} %copy-done.7), channel_id=1, source_target_pairs={{0,4},{4,0},{8,12},{12,8},{16,20},{20,16},{24,28},{28,24},{1,5},{5... | collective-permute-start | bytes 393224 | tf_op jit(solution)/shard_map/ppermute | solution.py:225
  61.3 18.8 %collective-permute-start.24 = (bf16[256,256]{1,0:T(8,128)(2,1)S(1)}, bf16[256,256]{1,0:T(8,128)(2,1)S(1)}, u32[]{:S(2)}, u32[]{:S(2)}) collective-permute-start(bf16[256,256]{1,0:T(8,128)(2,1)S(1)} %get-tuple-element.38), channel_id=1, source_target_pairs={{0,20},{4,16},{8,28},{12,24},{16,4},{20,0},{24,12},{28,8},{1,21},{... | collective-permute-start | bytes 393224 | tf_op jit(solution)/shard_map/ppermute | solution.py:225
  64.1 16.0 %collective-permute-start.23 = (bf16[256,256]{1,0:T(8,128)(2,1)S(1)}, bf16[256,256]{1,0:T(8,128)(2,1)S(1)}, u32[]{:S(2)}, u32[]{:S(2)}) collective-permute-start(bf16[256,256]{1,0:T(8,128)(2,1)S(1)} %get-tuple-element.37), channel_id=1, source_target_pairs={{0,16},{16,0},{1,17},{17,1},{2,18},{18,2},{3,19},{19,3},{4,20},{20... | collective-permute-start | bytes 393224 | tf_op jit(solution)/shard_map/ppermute | solution.py:209
  65.9 5.5 %collective-permute-start.14 = (bf16[256,256]{1,0:T(8,128)(2,1)S(1)}, bf16[256,256]{1,0:T(8,128)(2,1)S(1)}, u32[]{:S(2)}, u32[]{:S(2)}) collective-permute-start(bf16[256,256]{1,0:T(8,128)(2,1)S(1)} %get-tuple-element.32), channel_id=1, source_target_pairs={{0,4},{4,0},{8,12},{12,8},{1,5},{5,1},{9,13},{13,9},{2,6},{6,2},{1... | collective-permute-start | bytes 393224 | tf_op jit(solution)/shard_map/ppermute | solution.py:219
  66.3 22.1 %copy-start.1 = (bf16[2,512,256]{2,1,0:T(8,128)(2,1)S(1)}, bf16[2,512,256]{2,1,0:T(8,128)(2,1)}, u32[]{:S(2)}) copy-start(bf16[2,512,256]{2,1,0:T(8,128)(2,1)} %refs_2_.3) | copy-start | bytes 1572868
  71.4 5.8 %collective-permute-start.10 = (bf16[256,256]{1,0:T(8,128)(2,1)S(1)}, bf16[256,256]{1,0:T(8,128)(2,1)S(1)}, u32[]{:S(2)}, u32[]{:S(2)}) collective-permute-start(bf16[256,256]{1,0:T(8,128)(2,1)S(1)} %get-tuple-element.28), channel_id=1, source_target_pairs={{0,4},{4,0},{8,12},{12,8},{1,5},{5,1},{9,13},{13,9},{2,6},{6,2},{1... | collective-permute-start | bytes 393224 | tf_op jit(solution)/shard_map/ppermute | solution.py:219
  72.1 12.1 %collective-permute-start.26 = (bf16[256,256]{1,0:T(8,128)(2,1)S(1)}, bf16[256,256]{1,0:T(8,128)(2,1)S(1)}, u32[]{:S(2)}, u32[]{:S(2)}) collective-permute-start(bf16[256,256]{1,0:T(8,128)(2,1)S(1)} %add_convert_fusion), channel_id=1, source_target_pairs={{0,24},{4,28},{8,16},{12,20},{16,8},{20,12},{24,0},{28,4},{1,25},{... | collective-permute-start | bytes 393224 | tf_op jit(solution)/shard_map/ppermute | solution.py:225
  77.2 11.2 %collective-permute-start.22 = (bf16[256,256]{1,0:T(8,128)(2,1)S(1)}, bf16[256,256]{1,0:T(8,128)(2,1)S(1)}, u32[]{:S(2)}, u32[]{:S(2)}) collective-permute-start(bf16[256,256]{1,0:T(8,128)(2,1)S(1)} %add_convert_fusion.1), channel_id=1, source_target_pairs={{0,8},{4,12},{8,0},{12,4},{16,24},{20,28},{24,16},{28,20},{1,9},{5... | collective-permute-start | bytes 393224 | tf_op jit(solution)/shard_map/ppermute | solution.py:225
  77.2 12.6 %collective-permute-start.13 = (bf16[256,256]{1,0:T(8,128)(2,1)S(1)}, bf16[256,256]{1,0:T(8,128)(2,1)S(1)}, u32[]{:S(2)}, u32[]{:S(2)}) collective-permute-start(bf16[256,256]{1,0:T(8,128)(2,1)S(1)} %get-tuple-element.30), channel_id=1, source_target_pairs={{0,20},{4,16},{8,28},{12,24},{16,4},{20,0},{24,12},{28,8},{1,21},{... | collective-permute-start | bytes 393224 | tf_op jit(solution)/shard_map/ppermute | solution.py:225
  80.1 9.7 %collective-permute-start.9 = (bf16[256,256]{1,0:T(8,128)(2,1)S(1)}, bf16[256,256]{1,0:T(8,128)(2,1)S(1)}, u32[]{:S(2)}, u32[]{:S(2)}) collective-permute-start(bf16[256,256]{1,0:T(8,128)(2,1)S(1)} %get-tuple-element.26), channel_id=1, source_target_pairs={{0,4},{4,0},{8,12},{12,8},{16,20},{20,16},{24,28},{28,24},{1,5},{5... | collective-permute-start | bytes 393224 | tf_op jit(solution)/shard_map/ppermute | solution.py:225
  80.1 9.7 %collective-permute-start.12 = (bf16[256,256]{1,0:T(8,128)(2,1)S(1)}, bf16[256,256]{1,0:T(8,128)(2,1)S(1)}, u32[]{:S(2)}, u32[]{:S(2)}) collective-permute-start(bf16[256,256]{1,0:T(8,128)(2,1)S(1)} %get-tuple-element.29), channel_id=1, source_target_pairs={{0,16},{16,0},{1,17},{17,1},{2,18},{18,2},{3,19},{19,3},{4,20},{20... | collective-permute-start | bytes 393224 | tf_op jit(solution)/shard_map/ppermute | solution.py:209
  84.2 11.8 %collective-permute-start.15 = (bf16[256,256]{1,0:T(8,128)(2,1)S(1)}, bf16[256,256]{1,0:T(8,128)(2,1)S(1)}, u32[]{:S(2)}, u32[]{:S(2)}) collective-permute-start(bf16[256,256]{1,0:T(8,128)(2,1)S(1)} %add_convert_fusion.2), channel_id=1, source_target_pairs={{0,24},{4,28},{8,16},{12,20},{16,8},{20,12},{24,0},{28,4},{1,25},{... | collective-permute-start | bytes 393224 | tf_op jit(solution)/shard_map/ppermute | solution.py:225
  88.3 8.8 %collective-permute-start.11 = (bf16[256,256]{1,0:T(8,128)(2,1)S(1)}, bf16[256,256]{1,0:T(8,128)(2,1)S(1)}, u32[]{:S(2)}, u32[]{:S(2)}) collective-permute-start(bf16[256,256]{1,0:T(8,128)(2,1)S(1)} %add_convert_fusion.3), channel_id=1, source_target_pairs={{0,8},{4,12},{8,0},{12,4},{16,24},{20,28},{24,16},{28,20},{1,9},{5... | collective-permute-start | bytes 393224 | tf_op jit(solution)/shard_map/ppermute | solution.py:225
  (5 other events, 3.4 us)

commit v5 on v4

--- a/solution.py
+++ b/solution.py
@@ -6,6 +6,10 @@
 from jax.experimental import pallas as pl
 from jax.experimental.pallas import tpu as pltpu
 from jax.sharding import PartitionSpec as P
+
+
+def landing(n_col):
+    return min(1, n_col - 1)
 
 
 def prepare_kernel(n_row, *refs):
@@ -58,7 +62,7 @@
         parts = [outs[0].at[u] for u in range(layers)] if whole else outs[:layers]
         del outs[: 1 if whole else layers]
         a = z ^ turn
-        slot = (c ^ (a % n_col)) * folds + ((z % folds) ^ (a // n_col))
+        slot = (c ^ (a % n_col) ^ landing(n_col)) * folds + ((z % folds) ^ (a // n_col))
         tile = jnp.dot(held[slot], right[0, 0], preferred_element_type=jnp.float32)
         for u in range(layers):
             total = None
@@ -178,7 +182,7 @@
             for a in range(n_row):
                 for k in range(n_col):
                     target = k * folds + ((a // n_col) ^ turn)
-                    pairs.append((a * n_col + (k ^ hop), target * n_col + a % n_col))
+                    pairs.append((a * n_col + (k ^ hop), target * n_col + (a % n_col ^ landing(n_col))))
             pieces[0, turn] = lax.ppermute(part, ("row", "col"), pairs)
         step = n_col // 2
         while step >= 1:

time: 98.8 us -> 94.2 us (0.953)
  waiting for transfers between devices: 40.5 us -> 28.9 us
  starting transfers between devices: 39.8 us -> 46.8 us
    ppermute x3, starting transfers between devices: 0.61 us -> 8.38 us  [on_device(): lax.ppermute(blockmask, 'row', [(z, z ^ turn) for z in range(n_row)])]
    ppermute x3, waiting for transfers between devices: 8.75 us -> 2.37 us  [on_device(): lax.ppermute(blockmask, 'row', [(z, z ^ turn) for z in range(n_row)])]
    ppermute x6, waiting for transfers between devices: 7.07 us -> 2.87 us  [on_device(): pieces[flip ^ step, turn] = lax.ppermute(piece, 'col', swap)]
    ppermute x8, starting transfers between devices: 7.21 us -> 11.2 us  [on_device(): groups[u].append(lax.ppermute(block, ('gz', 'row'), pairs))]
    ppermute x8, waiting for transfers between devices: 14.1 us -> 11.6 us  [on_device(): groups[u].append(lax.ppermute(block, ('gz', 'row'), pairs))]
    ppermute x1, starting transfers between devices: 6.82 us -> 4.47 us  [on_device(): part = lax.ppermute(part, 'col', [(k, k ^ hop) for k in range(n_col)])]
    ppermute x1, waiting for transfers between devices: 0.01 us -> 2.19 us  [on_device(): part = lax.ppermute(part, 'col', [(k, k ^ hop) for k in range(n_col)])]
    ppermute x6, starting transfers between devices: 18 us -> 16 us  [on_device(): pieces[flip ^ step, turn] = lax.ppermute(piece, 'col', swap)]
  transfers between devices with their start and end apart: 27 -> 27, of which waited for: 11 -> 12; matrix products, arithmetic and copies ran while one was open for 1% -> 1% of each run, Pallas kernels for 9% -> 9%
where the time goes in v5:
time: 94.2 us; the launch traced here: 94 us
  starting transfers between devices  46.8 us (50%)
  waiting for transfers between devices  28.9 us (31%)
  Pallas kernels  10 us (11%)
  local copies, waits for them, and re-layouts  7.07 us (8%)
  other arithmetic  1.05 us (1%)
    ppermute x6, starting transfers between devices, on_device(): pieces[flip ^ step, turn] = lax.ppermute(piece, 'col', swap)  16 us
    ppermute x8, waiting for transfers between devices, on_device(): groups[u].append(lax.ppermute(block, ('gz', 'row'), pairs))  11.6 us
    ppermute x8, starting transfers between devices, on_device(): groups[u].append(lax.ppermute(block, ('gz', 'row'), pairs))  11.2 us
    ppermute x3, starting transfers between devices, on_device(): lax.ppermute(blockmask, 'row', [(z, z ^ turn) for z in range(n_row)])  8.38 us
    ppermute x4, waiting for transfers between devices, on_device(): got[u] = lax.ppermute(block, 'row', swap)  6.72 us
    unnamed x21, local copies, waits for them, and re-layouts  6.01 us
    pallas_call x4, Pallas kernels, products(): made = list(call(picks, *lefts, upanel))  5.71 us
    ppermute x1, starting transfers between devices, on_device(): part = lax.ppermute(part, 'col', [(k, k ^ hop) for k in range(n_col)])  4.47 us
  transfers between devices with their start and end apart: 27, of which 12 were waited for; matrix products, arithmetic and copies ran while one was open for 1% of the time, Pallas kernels for 9%

profile of v5, /device:TPU:0, one launch (start us, length us, event | category | flops | bytes accessed | tf_op | source)
XLA Modules:
  0.0 94.0 jit_solution(12359049217592945577)
XLA Ops:
  0.0 1.1 %slice_bitcast_fusion = (bf16[256,512]{1,0:T(8,128)(2,1)S(1)}, bf16[256,512]{1,0:T(8,128)(2,1)S(1)}) fusion(bf16[2,1,256,512]{3,2,1,0:T(8,128)(2,1)} %param.6), kind=kLoop, calls=%fused_computation.2 | loop fusion | bytes 1048576 | tf_op jit(solution)/shard_map/squeeze | solution.py:175
  1.6 4.5 %collective-permute-start.4 = (bf16[256,512]{1,0:T(8,128)(2,1)S(1)}, bf16[256,512]{1,0:T(8,128)(2,1)S(1)}, u32[]{:S(2)}, u32[]{:S(2)}) collective-permute-start(bf16[256,512]{1,0:T(8,128)(2,1)S(1)} %get-tuple-element.42), channel_id=1, source_target_pairs={{0,2},{1,3},{2,0},{3,1},{4,6},{5,7},{6,4},{7,5},{8,10},{9,11},{10,... | collective-permute-start | bytes 786440 | tf_op jit(solution)/shard_map/ppermute | solution.py:180
  6.1 3.1 %collective-permute-done.16.refs_0_ = bf16[256,512]{1,0:T(8,128)(2,1)S(1)} collective-permute-done((bf16[256,512]{1,0:T(8,128)(2,1)S(1)}, bf16[256,512]{1,0:T(8,128)(2,1)S(1)}, u32[]{:S(2)}, u32[]{:S(2)}) %collective-permute-start.16) | collective-permute-done | bytes 262176 | tf_op jit(solution)/shard_map/ppermute | solution.py:186
  9.2 6.5 %collective-permute-start.18 = (bf16[256,512]{1,0:T(8,128)(2,1)S(1)}, bf16[256,512]{1,0:T(8,128)(2,1)S(1)}, u32[]{:S(2)}, u32[]{:S(2)}) collective-permute-start(bf16[256,512]{1,0:T(8,128)(2,1)S(1)} %collective-permute-done.16.refs_0_), channel_id=1, source_target_pairs={{0,2},{1,3},{2,0},{3,1},{4,6},{5,7},{6,4},{7,5},{8,10},{9,11},{10,... | collective-permute-start | bytes 786440 | tf_op jit(solution)/shard_map/ppermute | solution.py:191
  15.6 2.2 %collective-permute-done.4 = bf16[256,512]{1,0:T(8,128)(2,1)S(1)} collective-permute-done((bf16[256,512]{1,0:T(8,128)(2,1)S(1)}, bf16[256,512]{1,0:T(8,128)(2,1)S(1)}, u32[]{:S(2)}, u32[]{:S(2)}) %collective-permute-start.4) | collective-permute-done | bytes 262176 | tf_op jit(solution)/shard_map/ppermute | solution.py:180
  17.8 1.4 %collective-permute-start.17 = (bf16[256,512]{1,0:T(8,128)(2,1)S(1)}, bf16[256,512]{1,0:T(8,128)(2,1)S(1)}, u32[]{:S(2)}, u32[]{:S(2)}) collective-permute-start(bf16[256,512]{1,0:T(8,128)(2,1)S(1)} %collective-permute-done.16.refs_0_), channel_id=1, source_target_pairs={{0,1},{1,0},{2,3},{3,2},{4,5},{5,4},{6,7},{7,6},{8,9},{9,8},{10,11... | collective-permute-start | bytes 786440 | tf_op jit(solution)/shard_map/ppermute | solution.py:191
  19.2 2.9 %collective-permute-done.18.refs_2_ = bf16[256,512]{1,0:T(8,128)(2,1)S(1)} collective-permute-done((bf16[256,512]{1,0:T(8,128)(2,1)S(1)}, bf16[256,512]{1,0:T(8,128)(2,1)S(1)}, u32[]{:S(2)}, u32[]{:S(2)}) %collective-permute-start.18) | collective-permute-done | bytes 262176 | tf_op jit(solution)/shard_map/ppermute | solution.py:191
  22.1 4.5 %collective-permute-start.19 = (bf16[256,512]{1,0:T(8,128)(2,1)S(1)}, bf16[256,512]{1,0:T(8,128)(2,1)S(1)}, u32[]{:S(2)}, u32[]{:S(2)}) collective-permute-start(bf16[256,512]{1,0:T(8,128)(2,1)S(1)} %collective-permute-done.18.refs_2_), channel_id=1, source_target_pairs={{0,1},{1,0},{2,3},{3,2},{4,5},{5,4},{6,7},{7,6},{8,9},{9,8},{10,11... | collective-permute-start | bytes 786440 | tf_op jit(solution)/shard_map/ppermute | solution.py:191
  26.6 3.2 %collective-permute-start.7 = (bf16[256,512]{1,0:T(8,128)(2,1)S(1)}, bf16[256,512]{1,0:T(8,128)(2,1)S(1)}, u32[]{:S(2)}, u32[]{:S(2)}) collective-permute-start(bf16[256,512]{1,0:T(8,128)(2,1)S(1)} %collective-permute-done.5.refs_0_), channel_id=1, source_target_pairs={{0,2},{1,3},{2,0},{3,1},{4,6},{5,7},{6,4},{7,5},{8,10},{9,11},{10,... | collective-permute-start | bytes 786440 | tf_op jit(solution)/shard_map/ppermute | solution.py:191
  29.8 1.9 %collective-permute-start.1 = (s32[2,1,1,4]{3,2,1,0:T(1,128)}, s32[2,1,1,4]{3,2,1,0:T(1,128)S(1)}, u32[]{:S(2)}, u32[]{:S(2)}) collective-permute-start(s32[2,1,1,4]{3,2,1,0:T(1,128)} %refs_0_.3), channel_id=1, source_target_pairs={{0,4},{4,0},{8,12},{12,8},{1,5},{5,1},{9,13},{13,9},{2,6},{6,2},{1... | collective-permute-start | bytes 104 | tf_op jit(solution)/shard_map/ppermute | solution.py:166
  31.7 3.2 %collective-permute-start.2 = (s32[2,1,1,4]{3,2,1,0:T(1,128)}, s32[2,1,1,4]{3,2,1,0:T(1,128)S(1)}, u32[]{:S(2)}, u32[]{:S(2)}) collective-permute-start(s32[2,1,1,4]{3,2,1,0:T(1,128)} %refs_0_.3), channel_id=1, source_target_pairs={{0,8},{4,12},{8,0},{12,4},{1,9},{5,13},{9,1},{13,5},{2,10},{6,14},... | collective-permute-start | bytes 104 | tf_op jit(solution)/shard_map/ppermute | solution.py:166
  35.0 3.2 %collective-permute-start.3 = (s32[2,1,1,4]{3,2,1,0:T(1,128)}, s32[2,1,1,4]{3,2,1,0:T(1,128)S(1)}, u32[]{:S(2)}, u32[]{:S(2)}) collective-permute-start(s32[2,1,1,4]{3,2,1,0:T(1,128)} %refs_0_.3), channel_id=1, source_target_pairs={{0,12},{4,8},{8,4},{12,0},{1,13},{5,9},{9,5},{13,1},{2,14},{6,10},... | collective-permute-start | bytes 104 | tf_op jit(solution)/shard_map/ppermute | solution.py:166
  38.2 2.4 %collective-permute-done.3.refs_3_ = s32[2,1,1,4]{3,2,1,0:T(1,128)S(1)} collective-permute-done((s32[2,1,1,4]{3,2,1,0:T(1,128)}, s32[2,1,1,4]{3,2,1,0:T(1,128)S(1)}, u32[]{:S(2)}, u32[]{:S(2)}) %collective-permute-start.3) | collective-permute-done | bytes 64 | tf_op jit(solution)/shard_map/ppermute | solution.py:166
  40.6 1.6 %copy-done = bf16[2,1,512,1024]{3,2,1,0:T(8,128)(2,1)S(1)} copy-done((bf16[2,1,512,1024]{3,2,1,0:T(8,128)(2,1)S(1)}, bf16[2,1,512,1024]{3,2,1,0:T(8,128)(2,1)}, u32[]{:S(2)}) %copy-start) | copy-done | bytes 2097176
  43.5 1.4 %prepare.1 = (f32[64]{0:T(128)S(1)}, bf16[2,1,512,1024]{3,2,1,0:T(8,128)(2,1)S(1)}) custom-call(s32[2,1,1,4]{3,2,1,0:T(1,128)S(1)} %copy-done.4, s32[2,1,1,4]{3,2,1,0:T(1,128)S(1)} %collective-permute-done.1.refs_1_, s32[2,1,1,4]{3,2,1,0:T(1,128)S(1)} %collective-permute-done.2.refs_2_, s32[2,1,1,4]{3,2,1,0:T(1,128)S(1)} %collective-permute-done.3.refs_3_, ...), custom_call_target="tpu_custom_call" | custom-call | flops 1048576 | bytes 4194304 | tf_op jit(solution)/shard_map/prepare/pallas_call | solution.py:38
  45.0 1.7 %shard_map.67 = (bf16[256,256]{1,0:T(8,128)(2,1)S(1)}, bf16[256,256]{1,0:T(8,128)(2,1)}, bf16[256,256]{1,0:T(8,128)(2,1)S(1)}, bf16[256,256]{1,0:T(8,128)(2,1)S(1)}) custom-call(f32[64]{0:T(128)S(1)} %get-tuple-element.23.picks, bf16[256,512]{1,0:T(8,128)(2,1)S(1)} %collective-permute-done.16.refs_0_, bf16[256,512]{1,0:T(8,128)(2,1)S(1)} %collective-permute-done.17.refs_1_, ...), custom_call_target="tpu_custom_call" | custom-call | flops 536870912 | bytes 2621440 | tf_op jit(solution)/shard_map/pallas_call | solution.py:101
  48.8 1.5 %collective-permute-start = (s32[2,1,1]{2,1,0:T(1,128)S(1)}, s32[2,1,1]{2,1,0:T(1,128)S(1)}, u32[]{:S(2)}, u32[]{:S(2)}) collective-permute-start(s32[2,1,1]{2,1,0:T(1,128)S(1)} %copy.10.refs_0_), channel_id=1, source_target_pairs={{0,16},{16,0},{1,17},{17,1},{2,18},{18,2},{3,19},{19,3},{4,20},{20... | collective-permute-start | bytes 32 | tf_op jit(solution)/shard_map/ppermute | solution.py:169
  50.6 1.8 %collective-permute-start.21 = (bf16[256,256]{1,0:T(8,128)(2,1)}, bf16[256,256]{1,0:T(8,128)(2,1)S(1)}, u32[]{:S(2)}, u32[]{:S(2)}) collective-permute-start(bf16[256,256]{1,0:T(8,128)(2,1)} %copy-done.8), channel_id=1, source_target_pairs={{0,4},{4,0},{8,12},{12,8},{1,5},{5,1},{9,13},{13,9},{2,6},{6,2},{1... | collective-permute-start | bytes 393224 | tf_op jit(solution)/shard_map/ppermute | solution.py:223
  53.6 1.3 %shard_map.66 = (bf16[256,256]{1,0:T(8,128)(2,1)S(1)}, bf16[256,256]{1,0:T(8,128)(2,1)S(1)}, bf16[256,256]{1,0:T(8,128)(2,1)S(1)}, bf16[256,256]{1,0:T(8,128)(2,1)S(1)}) custom-call(f32[64]{0:T(128)S(1)} %get-tuple-element.23.picks, bf16[256,512]{1,0:T(8,128)(2,1)S(1)} %collective-permute-done.16.refs_0_, ...), custom_call_target="tpu_custom_call" | custom-call | flops 536870912 | bytes 2621440 | tf_op jit(solution)/shard_map/pallas_call | solution.py:101
  56.4 3.0 %collective-permute-start.24 = (bf16[256,256]{1,0:T(8,128)(2,1)S(1)}, bf16[256,256]{1,0:T(8,128)(2,1)S(1)}, u32[]{:S(2)}, u32[]{:S(2)}) collective-permute-start(bf16[256,256]{1,0:T(8,128)(2,1)S(1)} %get-tuple-element.38), channel_id=1, source_target_pairs={{0,20},{4,16},{8,28},{12,24},{16,4},{20,0},{24,12},{28,8},{1,21},{... | collective-permute-start | bytes 393224 | tf_op jit(solution)/shard_map/ppermute | solution.py:229
  59.9 1.3 %shard_map.65 = (bf16[256,256]{1,0:T(8,128)(2,1)S(1)}, bf16[256,256]{1,0:T(8,128)(2,1)S(1)}, bf16[256,256]{1,0:T(8,128)(2,1)S(1)}, bf16[256,256]{1,0:T(8,128)(2,1)S(1)}) custom-call(f32[64]{0:T(128)S(1)} %get-tuple-element.23.picks, bf16[256,512]{1,0:T(8,128)(2,1)S(1)} %collective-permute-done.5.refs_0_, ...), custom_call_target="tpu_custom_call" | custom-call | flops 536870912 | bytes 2621440 | tf_op jit(solution)/shard_map/pallas_call | solution.py:101
  61.5 1.3 %shard_map.64 = (bf16[256,256]{1,0:T(8,128)(2,1)S(1)}, bf16[256,256]{1,0:T(8,128)(2,1)S(1)}, bf16[256,256]{1,0:T(8,128)(2,1)S(1)}, bf16[256,256]{1,0:T(8,128)(2,1)S(1)}) custom-call(f32[64]{0:T(128)S(1)} %get-tuple-element.23.picks, bf16[256,512]{1,0:T(8,128)(2,1)S(1)} %collective-permute-done.5.refs_0_, ...), custom_call_target="tpu_custom_call" | custom-call | flops 536870912 | bytes 2621440 | tf_op jit(solution)/shard_map/pallas_call | solution.py:101
  62.9 3.5 %collective-permute-done.14 = bf16[256,256]{1,0:T(8,128)(2,1)S(1)} collective-permute-done((bf16[256,256]{1,0:T(8,128)(2,1)S(1)}, bf16[256,256]{1,0:T(8,128)(2,1)S(1)}, u32[]{:S(2)}, u32[]{:S(2)}) %collective-permute-start.14) | collective-permute-done | bytes 131104 | tf_op jit(solution)/shard_map/ppermute | solution.py:223
  67.2 3.5 %collective-permute-start.26 = (bf16[256,256]{1,0:T(8,128)(2,1)S(1)}, bf16[256,256]{1,0:T(8,128)(2,1)S(1)}, u32[]{:S(2)}, u32[]{:S(2)}) collective-permute-start(bf16[256,256]{1,0:T(8,128)(2,1)S(1)} %add_convert_fusion), channel_id=1, source_target_pairs={{0,24},{4,28},{8,16},{12,20},{16,8},{20,12},{24,0},{28,4},{1,25},{... | collective-permute-start | bytes 393224 | tf_op jit(solution)/shard_map/ppermute | solution.py:229
  70.7 2.7 %collective-permute-done.10 = bf16[256,256]{1,0:T(8,128)(2,1)S(1)} collective-permute-done((bf16[256,256]{1,0:T(8,128)(2,1)S(1)}, bf16[256,256]{1,0:T(8,128)(2,1)S(1)}, u32[]{:S(2)}, u32[]{:S(2)}) %collective-permute-start.10) | collective-permute-done | bytes 131104 | tf_op jit(solution)/shard_map/ppermute | solution.py:223
  73.5 1.6 %collective-permute-start.22 = (bf16[256,256]{1,0:T(8,128)(2,1)S(1)}, bf16[256,256]{1,0:T(8,128)(2,1)S(1)}, u32[]{:S(2)}, u32[]{:S(2)}) collective-permute-start(bf16[256,256]{1,0:T(8,128)(2,1)S(1)} %add_convert_fusion.1), channel_id=1, source_target_pairs={{0,8},{4,12},{8,0},{12,4},{16,24},{20,28},{24,16},{28,20},{1,9},{5... | collective-permute-start | bytes 393224 | tf_op jit(solution)/shard_map/ppermute | solution.py:229
  75.1 1.4 %collective-permute-start.13 = (bf16[256,256]{1,0:T(8,128)(2,1)S(1)}, bf16[256,256]{1,0:T(8,128)(2,1)S(1)}, u32[]{:S(2)}, u32[]{:S(2)}) collective-permute-start(bf16[256,256]{1,0:T(8,128)(2,1)S(1)} %get-tuple-element.30), channel_id=1, source_target_pairs={{0,20},{4,16},{8,28},{12,24},{16,4},{20,0},{24,12},{28,8},{1,21},{... | collective-permute-start | bytes 393224 | tf_op jit(solution)/shard_map/ppermute | solution.py:229
  77.5 1.2 %collective-permute-start.12 = (bf16[256,256]{1,0:T(8,128)(2,1)S(1)}, bf16[256,256]{1,0:T(8,128)(2,1)S(1)}, u32[]{:S(2)}, u32[]{:S(2)}) collective-permute-start(bf16[256,256]{1,0:T(8,128)(2,1)S(1)} %get-tuple-element.29), channel_id=1, source_target_pairs={{0,16},{16,0},{1,17},{17,1},{2,18},{18,2},{3,19},{19,3},{4,20},{20... | collective-permute-start | bytes 393224 | tf_op jit(solution)/shard_map/ppermute | solution.py:213
  80.2 3.0 %collective-permute-done.22.refs_5_ = bf16[256,256]{1,0:T(8,128)(2,1)S(1)} collective-permute-done((bf16[256,256]{1,0:T(8,128)(2,1)S(1)}, bf16[256,256]{1,0:T(8,128)(2,1)S(1)}, u32[]{:S(2)}, u32[]{:S(2)}) %collective-permute-start.22) | collective-permute-done | bytes 131104 | tf_op jit(solution)/shard_map/ppermute | solution.py:229
  83.2 1.4 %shard_map.68.refs_9_ = bf16[2,512,256]{2,1,0:T(8,128)(2,1)} custom-call(s32[2,1,1]{2,1,0:T(1,128)S(1)} %copy.10.refs_0_, s32[2,1,1]{2,1,0:T(1,128)S(1)} %collective-permute-done.refs_1_, bf16[2,512,256]{2,1,0:T(8,128)(2,1)S(1)} %copy-done.1, bf16[256,256]{1,0:T(8,128)(2,1)S(1)} %get-tuple-element.33.refs_3_, ...), custom_call_target="tpu_custom_call" | custom-call | flops 524288 | bytes 1048576 | tf_op jit(solution)/shard_map/pallas_call | solution.py:143
  85.3 6.3 %collective-permute-done.15.refs_8_ = bf16[256,256]{1,0:T(8,128)(2,1)S(1)} collective-permute-done((bf16[256,256]{1,0:T(8,128)(2,1)S(1)}, bf16[256,256]{1,0:T(8,128)(2,1)S(1)}, u32[]{:S(2)}, u32[]{:S(2)}) %collective-permute-start.15) | collective-permute-done | bytes 131104 | tf_op jit(solution)/shard_map/ppermute | solution.py:229
  92.5 1.4 %shard_map.69 = bf16[2,512,256]{2,1,0:T(8,128)(2,1)} custom-call(s32[2,1,1]{2,1,0:T(1,128)S(1)} %copy.10.refs_0_, s32[2,1,1]{2,1,0:T(1,128)S(1)} %collective-permute-done.refs_1_, bf16[2,512,256]{2,1,0:T(8,128)(2,1)S(1)} %copy-done.1, bf16[256,256]{1,0:T(8,128)(2,1)S(1)} %get-tuple-element.25.refs_3_, ...), custom_call_target="tpu_custom_call", output_to_operand_aliasing={{}: (9, {})} | custom-call | flops 524288 | bytes 1048576 | tf_op jit(solution)/shard_map/pallas_call | solution.py:143
  (55 shorter events, 12.6 us)
Async XLA Ops:
  1.1 8.1 %collective-permute-start.16 = (bf16[256,512]{1,0:T(8,128)(2,1)S(1)}, bf16[256,512]{1,0:T(8,128)(2,1)S(1)}, u32[]{:S(2)}, u32[]{:S(2)}) collective-permute-start(bf16[256,512]{1,0:T(8,128)(2,1)S(1)} %get-tuple-element.41), channel_id=1, source_target_pairs={{0,1},{1,5},{2,9},{3,13},{4,0},{5,4},{6,8},{7,12},{8,3},{9,7},{10,... | collective-permute-start | bytes 786440 | tf_op jit(solution)/shard_map/ppermute | solution.py:186
  1.6 16.2 %collective-permute-start.4 = (bf16[256,512]{1,0:T(8,128)(2,1)S(1)}, bf16[256,512]{1,0:T(8,128)(2,1)S(1)}, u32[]{:S(2)}, u32[]{:S(2)}) collective-permute-start(bf16[256,512]{1,0:T(8,128)(2,1)S(1)} %get-tuple-element.42), channel_id=1, source_target_pairs={{0,2},{1,3},{2,0},{3,1},{4,6},{5,7},{6,4},{7,5},{8,10},{9,11},{10,... | collective-permute-start | bytes 786440 | tf_op jit(solution)/shard_map/ppermute | solution.py:180
  9.2 12.9 %collective-permute-start.18 = (bf16[256,512]{1,0:T(8,128)(2,1)S(1)}, bf16[256,512]{1,0:T(8,128)(2,1)S(1)}, u32[]{:S(2)}, u32[]{:S(2)}) collective-permute-start(bf16[256,512]{1,0:T(8,128)(2,1)S(1)} %collective-permute-done.16.refs_0_), channel_id=1, source_target_pairs={{0,2},{1,3},{2,0},{3,1},{4,6},{5,7},{6,4},{7,5},{8,10},{9,11},{10,... | collective-permute-start | bytes 786440 | tf_op jit(solution)/shard_map/ppermute | solution.py:191
  17.8 8.8 %collective-permute-start.5 = (bf16[256,512]{1,0:T(8,128)(2,1)S(1)}, bf16[256,512]{1,0:T(8,128)(2,1)S(1)}, u32[]{:S(2)}, u32[]{:S(2)}) collective-permute-start(bf16[256,512]{1,0:T(8,128)(2,1)S(1)} %collective-permute-done.4), channel_id=1, source_target_pairs={{2,1},{3,5},{0,9},{1,13},{6,0},{7,4},{4,8},{5,12},{10,3},{11,7},{8... | collective-permute-start | bytes 786440 | tf_op jit(solution)/shard_map/ppermute | solution.py:186
  17.8 27.2 %collective-permute-start.17 = (bf16[256,512]{1,0:T(8,128)(2,1)S(1)}, bf16[256,512]{1,0:T(8,128)(2,1)S(1)}, u32[]{:S(2)}, u32[]{:S(2)}) collective-permute-start(bf16[256,512]{1,0:T(8,128)(2,1)S(1)} %collective-permute-done.16.refs_0_), channel_id=1, source_target_pairs={{0,1},{1,0},{2,3},{3,2},{4,5},{5,4},{6,7},{7,6},{8,9},{9,8},{10,11... | collective-permute-start | bytes 786440 | tf_op jit(solution)/shard_map/ppermute | solution.py:191
  22.1 22.9 %collective-permute-start.19 = (bf16[256,512]{1,0:T(8,128)(2,1)S(1)}, bf16[256,512]{1,0:T(8,128)(2,1)S(1)}, u32[]{:S(2)}, u32[]{:S(2)}) collective-permute-start(bf16[256,512]{1,0:T(8,128)(2,1)S(1)} %collective-permute-done.18.refs_2_), channel_id=1, source_target_pairs={{0,1},{1,0},{2,3},{3,2},{4,5},{5,4},{6,7},{7,6},{8,9},{9,8},{10,11... | collective-permute-start | bytes 786440 | tf_op jit(solution)/shard_map/ppermute | solution.py:191
  26.6 25.8 %collective-permute-start.7 = (bf16[256,512]{1,0:T(8,128)(2,1)S(1)}, bf16[256,512]{1,0:T(8,128)(2,1)S(1)}, u32[]{:S(2)}, u32[]{:S(2)}) collective-permute-start(bf16[256,512]{1,0:T(8,128)(2,1)S(1)} %collective-permute-done.5.refs_0_), channel_id=1, source_target_pairs={{0,2},{1,3},{2,0},{3,1},{4,6},{5,7},{6,4},{7,5},{8,10},{9,11},{10,... | collective-permute-start | bytes 786440 | tf_op jit(solution)/shard_map/ppermute | solution.py:191
  29.8 5.2 %collective-permute-start.1 = (s32[2,1,1,4]{3,2,1,0:T(1,128)}, s32[2,1,1,4]{3,2,1,0:T(1,128)S(1)}, u32[]{:S(2)}, u32[]{:S(2)}) collective-permute-start(s32[2,1,1,4]{3,2,1,0:T(1,128)} %refs_0_.3), channel_id=1, source_target_pairs={{0,4},{4,0},{8,12},{12,8},{1,5},{5,1},{9,13},{13,9},{2,6},{6,2},{1... | collective-permute-start | bytes 104 | tf_op jit(solution)/shard_map/ppermute | solution.py:166
  31.7 6.5 %collective-permute-start.2 = (s32[2,1,1,4]{3,2,1,0:T(1,128)}, s32[2,1,1,4]{3,2,1,0:T(1,128)S(1)}, u32[]{:S(2)}, u32[]{:S(2)}) collective-permute-start(s32[2,1,1,4]{3,2,1,0:T(1,128)} %refs_0_.3), channel_id=1, source_target_pairs={{0,8},{4,12},{8,0},{12,4},{1,9},{5,13},{9,1},{13,5},{2,10},{6,14},... | collective-permute-start | bytes 104 | tf_op jit(solution)/shard_map/ppermute | solution.py:166
  35.0 5.6 %collective-permute-start.3 = (s32[2,1,1,4]{3,2,1,0:T(1,128)}, s32[2,1,1,4]{3,2,1,0:T(1,128)S(1)}, u32[]{:S(2)}, u32[]{:S(2)}) collective-permute-start(s32[2,1,1,4]{3,2,1,0:T(1,128)} %refs_0_.3), channel_id=1, source_target_pairs={{0,12},{4,8},{8,4},{12,0},{1,13},{5,9},{9,5},{13,1},{2,14},{6,10},... | collective-permute-start | bytes 104 | tf_op jit(solution)/shard_map/ppermute | solution.py:166
  40.6 1.6 %copy-start = (bf16[2,1,512,1024]{3,2,1,0:T(8,128)(2,1)S(1)}, bf16[2,1,512,1024]{3,2,1,0:T(8,128)(2,1)}, u32[]{:S(2)}) copy-start(bf16[2,1,512,1024]{3,2,1,0:T(8,128)(2,1)} %refs_5_.1) | copy-start | bytes 6291460
  45.0 3.8 %copy-start.9 = (s32[2,1,1]{0,2,1:T(1,128)S(1)}, s32[2,1,1]{0,2,1:T(1,128)}, u32[]{:S(2)}) copy-start(s32[2,1,1]{0,2,1:T(1,128)} %param.8) | copy-start | bytes 28
  48.7 6.7 %collective-permute-start.25 = (bf16[256,256]{1,0:T(8,128)(2,1)}, bf16[256,256]{1,0:T(8,128)(2,1)}, u32[]{:S(2)}, u32[]{:S(2)}) collective-permute-start(bf16[256,256]{1,0:T(8,128)(2,1)} %get-tuple-element.40), channel_id=1, source_target_pairs={{0,4},{4,0},{8,12},{12,8},{1,5},{5,1},{9,13},{13,9},{2,6},{6,2},{1... | collective-permute-start | bytes 393224 | tf_op jit(solution)/shard_map/ppermute | solution.py:223
  48.8 18.4 %collective-permute-start = (s32[2,1,1]{2,1,0:T(1,128)S(1)}, s32[2,1,1]{2,1,0:T(1,128)S(1)}, u32[]{:S(2)}, u32[]{:S(2)}) collective-permute-start(s32[2,1,1]{2,1,0:T(1,128)S(1)} %copy.10.refs_0_), channel_id=1, source_target_pairs={{0,16},{16,0},{1,17},{17,1},{2,18},{18,2},{3,19},{19,3},{4,20},{20... | collective-permute-start | bytes 32 | tf_op jit(solution)/shard_map/ppermute | solution.py:169
  50.3 6.0 %collective-permute-start.6 = (bf16[256,512]{1,0:T(8,128)(2,1)S(1)}, bf16[256,512]{1,0:T(8,128)(2,1)S(1)}, u32[]{:S(2)}, u32[]{:S(2)}) collective-permute-start(bf16[256,512]{1,0:T(8,128)(2,1)S(1)} %collective-permute-done.5.refs_0_), channel_id=1, source_target_pairs={{0,1},{1,0},{2,3},{3,2},{4,5},{5,4},{6,7},{7,6},{8,9},{9,8},{10,11... | collective-permute-start | bytes 786440 | tf_op jit(solution)/shard_map/ppermute | solution.py:191
  50.6 10.7 %collective-permute-start.21 = (bf16[256,256]{1,0:T(8,128)(2,1)}, bf16[256,256]{1,0:T(8,128)(2,1)S(1)}, u32[]{:S(2)}, u32[]{:S(2)}) collective-permute-start(bf16[256,256]{1,0:T(8,128)(2,1)} %copy-done.8), channel_id=1, source_target_pairs={{0,4},{4,0},{8,12},{12,8},{1,5},{5,1},{9,13},{13,9},{2,6},{6,2},{1... | collective-permute-start | bytes 393224 | tf_op jit(solution)/shard_map/ppermute | solution.py:223
  52.4 7.1 %collective-permute-start.8 = (bf16[256,512]{1,0:T(8,128)(2,1)S(1)}, bf16[256,512]{1,0:T(8,128)(2,1)S(1)}, u32[]{:S(2)}, u32[]{:S(2)}) collective-permute-start(bf16[256,512]{1,0:T(8,128)(2,1)S(1)} %collective-permute-done.7.refs_2_), channel_id=1, source_target_pairs={{0,1},{1,0},{2,3},{3,2},{4,5},{5,4},{6,7},{7,6},{8,9},{9,8},{10,11... | collective-permute-start | bytes 786440 | tf_op jit(solution)/shard_map/ppermute | solution.py:191
  52.6 0.9 %copy-start.3 = (bf16[256,512]{1,0:T(8,128)(2,1)S(1)}, bf16[256,512]{1,0:T(8,128)(2,1)}, u32[]{:S(2)}) copy-start(bf16[256,512]{1,0:T(8,128)(2,1)} %copy-done.2) | copy-start | bytes 786436
  53.5 1.9 %copy-start.7 = (bf16[256,256]{1,0:T(8,128)(2,1)S(1)}, bf16[256,256]{1,0:T(8,128)(2,1)}, u32[]{:S(2)}) copy-start(bf16[256,256]{1,0:T(8,128)(2,1)} %copy-done.6) | copy-start | bytes 393220
  55.4 19.7 %collective-permute-start.20 = (bf16[256,256]{1,0:T(8,128)(2,1)S(1)}, bf16[256,256]{1,0:T(8,128)(2,1)S(1)}, u32[]{:S(2)}, u32[]{:S(2)}) collective-permute-start(bf16[256,256]{1,0:T(8,128)(2,1)S(1)} %copy-done.7), channel_id=1, source_target_pairs={{0,4},{4,0},{8,12},{12,8},{16,20},{20,16},{24,28},{28,24},{1,5},{5... | collective-permute-start | bytes 393224 | tf_op jit(solution)/shard_map/ppermute | solution.py:229
  56.4 20.2 %collective-permute-start.24 = (bf16[256,256]{1,0:T(8,128)(2,1)S(1)}, bf16[256,256]{1,0:T(8,128)(2,1)S(1)}, u32[]{:S(2)}, u32[]{:S(2)}) collective-permute-start(bf16[256,256]{1,0:T(8,128)(2,1)S(1)} %get-tuple-element.38), channel_id=1, source_target_pairs={{0,20},{4,16},{8,28},{12,24},{16,4},{20,0},{24,12},{28,8},{1,21},{... | collective-permute-start | bytes 393224 | tf_op jit(solution)/shard_map/ppermute | solution.py:229
  59.4 18.0 %collective-permute-start.23 = (bf16[256,256]{1,0:T(8,128)(2,1)S(1)}, bf16[256,256]{1,0:T(8,128)(2,1)S(1)}, u32[]{:S(2)}, u32[]{:S(2)}) collective-permute-start(bf16[256,256]{1,0:T(8,128)(2,1)S(1)} %get-tuple-element.37), channel_id=1, source_target_pairs={{0,16},{16,0},{1,17},{17,1},{2,18},{18,2},{3,19},{19,3},{4,20},{20... | collective-permute-start | bytes 393224 | tf_op jit(solution)/shard_map/ppermute | solution.py:213
  61.3 5.0 %collective-permute-start.14 = (bf16[256,256]{1,0:T(8,128)(2,1)S(1)}, bf16[256,256]{1,0:T(8,128)(2,1)S(1)}, u32[]{:S(2)}, u32[]{:S(2)}) collective-permute-start(bf16[256,256]{1,0:T(8,128)(2,1)S(1)} %get-tuple-element.32), channel_id=1, source_target_pairs={{0,4},{4,0},{8,12},{12,8},{1,5},{5,1},{9,13},{13,9},{2,6},{6,2},{1... | collective-permute-start | bytes 393224 | tf_op jit(solution)/shard_map/ppermute | solution.py:223
  61.5 21.7 %copy-start.1 = (bf16[2,512,256]{2,1,0:T(8,128)(2,1)S(1)}, bf16[2,512,256]{2,1,0:T(8,128)(2,1)}, u32[]{:S(2)}) copy-start(bf16[2,512,256]{2,1,0:T(8,128)(2,1)} %refs_2_.3) | copy-start | bytes 1572868
  66.3 7.1 %collective-permute-start.10 = (bf16[256,256]{1,0:T(8,128)(2,1)S(1)}, bf16[256,256]{1,0:T(8,128)(2,1)S(1)}, u32[]{:S(2)}, u32[]{:S(2)}) collective-permute-start(bf16[256,256]{1,0:T(8,128)(2,1)S(1)} %get-tuple-element.28), channel_id=1, source_target_pairs={{0,4},{4,0},{8,12},{12,8},{1,5},{5,1},{9,13},{13,9},{2,6},{6,2},{1... | collective-permute-start | bytes 393224 | tf_op jit(solution)/shard_map/ppermute | solution.py:223
  67.2 12.3 %collective-permute-start.26 = (bf16[256,256]{1,0:T(8,128)(2,1)S(1)}, bf16[256,256]{1,0:T(8,128)(2,1)S(1)}, u32[]{:S(2)}, u32[]{:S(2)}) collective-permute-start(bf16[256,256]{1,0:T(8,128)(2,1)S(1)} %add_convert_fusion), channel_id=1, source_target_pairs={{0,24},{4,28},{8,16},{12,20},{16,8},{20,12},{24,0},{28,4},{1,25},{... | collective-permute-start | bytes 393224 | tf_op jit(solution)/shard_map/ppermute | solution.py:229
  73.5 9.7 %collective-permute-start.22 = (bf16[256,256]{1,0:T(8,128)(2,1)S(1)}, bf16[256,256]{1,0:T(8,128)(2,1)S(1)}, u32[]{:S(2)}, u32[]{:S(2)}) collective-permute-start(bf16[256,256]{1,0:T(8,128)(2,1)S(1)} %add_convert_fusion.1), channel_id=1, source_target_pairs={{0,8},{4,12},{8,0},{12,4},{16,24},{20,28},{24,16},{28,20},{1,9},{5... | collective-permute-start | bytes 393224 | tf_op jit(solution)/shard_map/ppermute | solution.py:229
  75.1 9.5 %collective-permute-start.13 = (bf16[256,256]{1,0:T(8,128)(2,1)S(1)}, bf16[256,256]{1,0:T(8,128)(2,1)S(1)}, u32[]{:S(2)}, u32[]{:S(2)}) collective-permute-start(bf16[256,256]{1,0:T(8,128)(2,1)S(1)} %get-tuple-element.30), channel_id=1, source_target_pairs={{0,20},{4,16},{8,28},{12,24},{16,4},{20,0},{24,12},{28,8},{1,21},{... | collective-permute-start | bytes 393224 | tf_op jit(solution)/shard_map/ppermute | solution.py:229
  76.6 8.7 %collective-permute-start.9 = (bf16[256,256]{1,0:T(8,128)(2,1)S(1)}, bf16[256,256]{1,0:T(8,128)(2,1)S(1)}, u32[]{:S(2)}, u32[]{:S(2)}) collective-permute-start(bf16[256,256]{1,0:T(8,128)(2,1)S(1)} %get-tuple-element.26), channel_id=1, source_target_pairs={{0,4},{4,0},{8,12},{12,8},{16,20},{20,16},{24,28},{28,24},{1,5},{5... | collective-permute-start | bytes 393224 | tf_op jit(solution)/shard_map/ppermute | solution.py:229
  77.5 7.8 %collective-permute-start.12 = (bf16[256,256]{1,0:T(8,128)(2,1)S(1)}, bf16[256,256]{1,0:T(8,128)(2,1)S(1)}, u32[]{:S(2)}, u32[]{:S(2)}) collective-permute-start(bf16[256,256]{1,0:T(8,128)(2,1)S(1)} %get-tuple-element.29), channel_id=1, source_target_pairs={{0,16},{16,0},{1,17},{17,1},{2,18},{18,2},{3,19},{19,3},{4,20},{20... | collective-permute-start | bytes 393224 | tf_op jit(solution)/shard_map/ppermute | solution.py:213
  79.5 12.0 %collective-permute-start.15 = (bf16[256,256]{1,0:T(8,128)(2,1)S(1)}, bf16[256,256]{1,0:T(8,128)(2,1)S(1)}, u32[]{:S(2)}, u32[]{:S(2)}) collective-permute-start(bf16[256,256]{1,0:T(8,128)(2,1)S(1)} %add_convert_fusion.2), channel_id=1, source_target_pairs={{0,24},{4,28},{8,16},{12,20},{16,8},{20,12},{24,0},{28,4},{1,25},{... | collective-permute-start | bytes 393224 | tf_op jit(solution)/shard_map/ppermute | solution.py:229
  83.2 9.3 %collective-permute-start.11 = (bf16[256,256]{1,0:T(8,128)(2,1)S(1)}, bf16[256,256]{1,0:T(8,128)(2,1)S(1)}, u32[]{:S(2)}, u32[]{:S(2)}) collective-permute-start(bf16[256,256]{1,0:T(8,128)(2,1)S(1)} %add_convert_fusion.3), channel_id=1, source_target_pairs={{0,8},{4,12},{8,0},{12,4},{16,24},{20,28},{24,16},{28,20},{1,9},{5... | collective-permute-start | bytes 393224 | tf_op jit(solution)/shard_map/ppermute | solution.py:229
  (5 other events, 3.4 us)
